TPU v7x, 256 devices: a whole 4x4x8 slice. The times are simulated.
256 devices in a mesh: row: 8 (over z_hi, y), col: 32 (over z_lo, x, core).
Axes of the slice: x: 4, y: 4, z: 8 (z_hi: 2, z_lo: 4; z = z_hi * 4 + z_lo), core: 2. Of those that a mesh axis runs over, the one named last changes fastest.
Arguments:
- tokens: bfloat16 [4096, 1024], P(('row', 'col')), may hold values from -6 to 6
- grad_out: bfloat16 [4096, 1024], P(('row', 'col')), may hold values from -1.1953125 to 1.1953125
- gains: float32 [2, 1024], replicated, may hold values from 0.1 to 1.9
- flat_in: bfloat16 [32768, 1024], P(('row', 'col')), may hold values from -0.1875 to 0.1875
- flat_out: bfloat16 [32768, 1024], P(('row', 'col')), may hold values from -0.03125 to 0.03125
- flat_moment: float32 [2, 32768, 1024], P(None, ('row', 'col')), may hold values from -3 to 3
- flat_second: float32 [2, 32768, 1024], P(None, ('row', 'col')), may hold values from 0.05 to 2
- tile_in: bfloat16 [32, 24, 64, 1024], P('col', 'row'), may hold values from -0.1875 to 0.1875
- tile_out: bfloat16 [32, 24, 64, 1024], P('col', 'row'), may hold values from -0.03125 to 0.03125
- tile_moment: float32 [2, 32, 24, 64, 1024], P(None, 'col', 'row'), may hold values from -3 to 3
- tile_second: float32 [2, 32, 24, 64, 1024], P(None, 'col', 'row'), may hold values from 0.05 to 2
- owners: int32 [2, 32, 16], P(None, 'col'), may hold values from 0 to 7, as said below
Outputs:
- hidden_out: bfloat16 [4096, 1024], P(('row', 'col'))
- grad_tokens: bfloat16 [4096, 1024], P(('row', 'col'))
- new_flat_in: bfloat16 [32768, 1024], P(('row', 'col'))
- new_flat_out: bfloat16 [32768, 1024], P(('row', 'col'))
- new_flat_moment: float32 [2, 32768, 1024], P(None, ('row', 'col'))
- new_flat_second: float32 [2, 32768, 1024], P(None, ('row', 'col'))
- new_tile_in: bfloat16 [32, 24, 64, 1024], P('col', 'row')
- new_tile_out: bfloat16 [32, 24, 64, 1024], P('col', 'row')
- new_tile_moment: float32 [2, 32, 24, 64, 1024], P(None, 'col', 'row')
- new_tile_second: float32 [2, 32, 24, 64, 1024], P(None, 'col', 'row')
Inputs may be any that keep to these rules, and one draw needn't show every extreme that they name: `owners`: for each matrix and column block, entry k names the row that owns tile k; each row owns at most 3 tiles of a block and matrix, and in each block and matrix some row owns exactly 3.
All inputs are finite; a program needn't handle non-finite values.
Results may differ from a plain program's by a relative error of at most 0.029.
Values may be sent and summed in bfloat16 or wider, within the bound.
A program may use at most 128 MiB of HBM per device.

v0:
```python
import jax
import jax.numpy as jnp
from jax import lax
from jax.sharding import PartitionSpec as P

norm_eps = 1e-06
beta_one = 0.9
beta_two = 0.95
learn_rate = 0.002
decay_rate = 0.1
adam_eps = 1e-08
gelu_coef = 0.7978845608


def laid_out(parts, dim):
    parts = jnp.moveaxis(parts, 0, dim)
    dims = parts.shape
    return parts.reshape(*dims[:dim], dims[dim] * dims[dim + 1], *dims[dim + 2 :])


def copy_for_each(value, axis):
    peers = lax.axis_size(axis)
    return lax.all_to_all(
        jnp.broadcast_to(value[None], (peers, *value.shape)), axis, 0, 0, tiled=True
    )


def collect(value, axis, dim):
    return laid_out(copy_for_each(value, axis), dim)


def cut_along(value, dim, peers):
    before, after = (value.shape[:dim], value.shape[dim + 1 :])
    return jnp.moveaxis(value.reshape(*before, peers, -1, *after), dim, 0)


def sent_and_summed(value, axis, dim):
    parts = cut_along(value, dim, lax.axis_size(axis))
    arrived = lax.all_to_all(parts, axis, split_axis=0, concat_axis=0, tiled=True)
    return arrived.astype(jnp.float32).sum(axis=0)


def sent_together(arrays, axis, split_dim, concat_dim, along):
    ends, at = ([], 0)
    for a in arrays[:-1]:
        at += a.shape[along]
        ends.append(at)
    both = jnp.concatenate(arrays, axis=along)
    return tuple(
        jnp.split(
            lax.all_to_all(both, axis, split_axis=split_dim, concat_axis=concat_dim, tiled=True),
            ends,
            axis=along,
        )
    )


def sent_together_2(arrays, axis, dim, along):
    both = jnp.concatenate(arrays, axis=along)
    filled, at, gathered = (lax.all_gather(both, axis, axis=dim, tiled=True), 0, [])
    for a in arrays:
        gathered.append(lax.slice_in_dim(filled, at, at + a.shape[along], axis=along))
        at += a.shape[along]
    return tuple(gathered)


def sent_together_3(arrays, axis, dim, along):
    ends, at = ([], 0)
    for a in arrays[:-1]:
        at += a.shape[along]
        ends.append(at)
    both = jnp.concatenate(arrays, axis=along)
    return tuple(
        jnp.split(lax.psum_scatter(both, axis, scatter_dimension=dim, tiled=True), ends, axis=along)
    )


def gelu_value(hidden):
    tanh_term = jnp.tanh(gelu_coef * (hidden + 0.044715 * hidden * hidden * hidden))
    return 0.5 * hidden * (1.0 + tanh_term)


def gelu_slope(hidden):
    tanh_term = jnp.tanh(gelu_coef * (hidden + 0.044715 * hidden * hidden * hidden))
    return 0.5 * (1.0 + tanh_term) + 0.5 * hidden * (1.0 - tanh_term * tanh_term) * gelu_coef * (
        1.0 + 0.134145 * hidden * hidden
    )


def adam_update(weight, gradient, moment, second):
    new_moment = beta_one * moment + (1.0 - beta_one) * gradient
    new_second = beta_two * second + (1.0 - beta_two) * gradient * gradient
    weight_float = weight.astype(jnp.float32)
    stepped = weight_float - learn_rate * (
        new_moment / (jnp.sqrt(new_second) + adam_eps) + decay_rate * weight_float
    )
    return (stepped.astype(jnp.bfloat16), new_moment, new_second)


def slot_tables(owner_rows, slot_cap, row_total):
    tile_count = owner_rows.shape[-1]
    positions = jnp.arange(tile_count, dtype=jnp.int32)
    same_owner = owner_rows[..., :, None] == owner_rows[..., None, :]
    earlier = positions[None, :] < positions[:, None]
    tile_rank = jnp.sum(jnp.where(same_owner & earlier, 1, 0), axis=-1).astype(jnp.int32)
    slot_dest = owner_rows * slot_cap + tile_rank
    slot_ids = jnp.arange(row_total * slot_cap, dtype=jnp.int32)
    matches = slot_dest[..., None, :] == slot_ids[:, None]
    slot_tile = jnp.sum(jnp.where(matches, positions, 0), axis=-1)
    slot_live = jnp.any(matches, axis=-1)
    return (slot_dest, slot_tile, slot_live)


def forward(layer_in, gain_vec, w_in, w_out):
    tok_float = layer_in.astype(jnp.float32)
    inv_rms = lax.rsqrt(jnp.mean(tok_float * tok_float, axis=1, keepdims=True) + norm_eps)
    normed = (tok_float * inv_rms * gain_vec).astype(jnp.bfloat16)
    normed_all = collect(normed, "col", 0)
    hidden = jnp.dot(normed_all, w_in, preferred_element_type=jnp.float32)
    activated = gelu_value(hidden).astype(jnp.bfloat16)
    mixed_sum = sent_and_summed(
        lax.dot_general(
            activated, w_out, (((1,), (1,)), ((), ())), preferred_element_type=jnp.float32
        ).astype(jnp.bfloat16),
        "col",
        0,
    )
    return (
        (tok_float + mixed_sum).astype(jnp.bfloat16),
        (tok_float, inv_rms, normed_all, hidden, activated),
    )


def backward(cotangent, gain_vec, w_in, w_out, saved_state):
    tok_float, inv_rms, normed_all, hidden, activated = saved_state
    grad_all = collect(cotangent, "col", 0)
    d_act = jnp.dot(grad_all, w_out, preferred_element_type=jnp.float32)
    d_hidden = (d_act * gelu_slope(hidden)).astype(jnp.bfloat16)
    d_normed = sent_and_summed(
        lax.dot_general(
            d_hidden, w_in, (((1,), (1,)), ((), ())), preferred_element_type=jnp.float32
        ).astype(jnp.bfloat16),
        "col",
        0,
    )
    gated = d_normed * gain_vec
    tok_grad = (
        cotangent.astype(jnp.float32)
        + inv_rms * gated
        - tok_float
        * inv_rms
        * inv_rms
        * inv_rms
        * jnp.mean(tok_float * gated, axis=1, keepdims=True)
    )
    return (tok_grad.astype(jnp.bfloat16), grad_all, d_hidden)


def group_grads(normed_all, d_hidden, grad_all, activated):
    grad_in = lax.dot_general(
        normed_all, d_hidden, (((0,), (0,)), ((), ())), preferred_element_type=jnp.float32
    )
    grad_wout = lax.dot_general(
        grad_all, activated, (((0,), (0,)), ((), ())), preferred_element_type=jnp.float32
    )
    return (grad_in, grad_wout)


def shards(
    tokens,
    grad_out,
    gains,
    flat_in,
    flat_out,
    flat_moment,
    flat_second,
    tile_in,
    tile_out,
    tile_moment,
    tile_second,
    owners,
):
    row_total = lax.axis_size("row")
    col_total = lax.axis_size("col")
    row_index = lax.axis_index("row")
    model_width = tokens.shape[1]
    block_width = flat_in.shape[1]
    part_rows = flat_in.shape[0] // col_total
    slot_cap = tile_in.shape[1]
    tile_rows = tile_in.shape[2]
    tile_count = model_width // tile_rows
    owner_rows = owners[:, 0, :]
    slot_dest, slot_tile, slot_live = slot_tables(owner_rows, slot_cap, row_total)
    shaped = (
        flat_in.reshape(part_rows, col_total, block_width),
        flat_out.reshape(part_rows, col_total, block_width),
    )
    arrived = sent_together((shaped[0], shaped[1]), "col", 1, 0, 2)
    banded = (
        arrived[0].reshape(col_total * part_rows, block_width),
        arrived[1].reshape(col_total * part_rows, block_width),
    )
    whole_weights = sent_together_2((banded[0], banded[1]), "row", 0, 1)
    first_in, first_out = (whole_weights[0], whole_weights[1])
    middle, saved_one = forward(tokens, gains[0], first_in, first_out)
    whole_slots = sent_together_2((tile_in[0], tile_out[0]), "row", 0, 1)
    second_in = jnp.take(whole_slots[0], slot_dest[0], axis=0).reshape(model_width, block_width)
    second_out = jnp.take(whole_slots[1], slot_dest[1], axis=0).reshape(model_width, block_width)
    hidden_out, saved_two = forward(middle, gains[1], second_in, second_out)
    grad_mid, grad_all_two, d_hidden_two = backward(
        grad_out, gains[1], second_in, second_out, saved_two
    )
    grad_in_two, grad_wout_two = group_grads(saved_two[2], d_hidden_two, grad_all_two, saved_two[4])
    tiles_in = grad_in_two.reshape(tile_count, tile_rows, block_width)
    tiles_out = grad_wout_two.reshape(tile_count, tile_rows, block_width)
    live_in = slot_live[0][:, None, None]
    live_out = slot_live[1][:, None, None]
    outgoing = (
        jnp.where(live_in, jnp.take(tiles_in, slot_tile[0], axis=0), 0.0),
        jnp.where(live_out, jnp.take(tiles_out, slot_tile[1], axis=0), 0.0),
    )
    tile_grad_in, tile_grad_out = tuple(
        (
            part.astype(jnp.float32)
            for part in sent_together_3(
                (outgoing[0].astype(jnp.bfloat16), outgoing[1].astype(jnp.bfloat16)), "row", 0, 1
            )
        )
    )
    grad_tokens, grad_all_one, d_hidden_one = backward(
        grad_mid, gains[0], first_in, first_out, saved_one
    )
    grad_in_one, grad_wout_one = group_grads(saved_one[2], d_hidden_one, grad_all_one, saved_one[4])
    banded_sums = tuple(
        (
            part.astype(jnp.float32)
            for part in sent_together_3(
                (grad_in_one.astype(jnp.bfloat16), grad_wout_one.astype(jnp.bfloat16)), "row", 0, 1
            )
        )
    )
    shaped_sums = (
        banded_sums[0].reshape(col_total, part_rows, 1, block_width),
        banded_sums[1].reshape(col_total, part_rows, 1, block_width),
    )
    owned_rows = tuple(
        (
            part.astype(jnp.float32)
            for part in sent_together(
                (shaped_sums[0].astype(jnp.bfloat16), shaped_sums[1].astype(jnp.bfloat16)),
                "col",
                0,
                2,
                1,
            )
        )
    )
    flat_grad_in = owned_rows[0].reshape(part_rows * col_total, block_width)
    flat_grad_out = owned_rows[1].reshape(part_rows * col_total, block_width)
    new_flat_in, moment_in, second_in_f = adam_update(
        flat_in, flat_grad_in, flat_moment[0], flat_second[0]
    )
    new_flat_out, moment_out, second_out_f = adam_update(
        flat_out, flat_grad_out, flat_moment[1], flat_second[1]
    )
    live_mine = lax.dynamic_slice_in_dim(slot_live, row_index * slot_cap, slot_cap, 1)
    live_in_mine = live_mine[0][:, None, None]
    live_out_mine = live_mine[1][:, None, None]
    upd_in, tmom_in, tsec_in = adam_update(
        tile_in[0], tile_grad_in, tile_moment[0, 0], tile_second[0, 0]
    )
    upd_out, tmom_out, tsec_out = adam_update(
        tile_out[0], tile_grad_out, tile_moment[1, 0], tile_second[1, 0]
    )
    new_tile_in = jnp.where(live_in_mine, upd_in, tile_in[0])[None]
    new_tile_out = jnp.where(live_out_mine, upd_out, tile_out[0])[None]
    new_tmom = jnp.stack(
        [
            jnp.where(live_in_mine, tmom_in, tile_moment[0, 0]),
            jnp.where(live_out_mine, tmom_out, tile_moment[1, 0]),
        ]
    )[:, None]
    new_tsec = jnp.stack(
        [
            jnp.where(live_in_mine, tsec_in, tile_second[0, 0]),
            jnp.where(live_out_mine, tsec_out, tile_second[1, 0]),
        ]
    )[:, None]
    return (
        hidden_out,
        grad_tokens,
        new_flat_in,
        new_flat_out,
        jnp.stack([moment_in, moment_out]),
        jnp.stack([second_in_f, second_out_f]),
        new_tile_in,
        new_tile_out,
        new_tmom,
        new_tsec,
    )


def solution(mesh):
    return jax.shard_map(
        shards,
        mesh=mesh,
        in_specs=(
            P(("row", "col"), None),
            P(("row", "col"), None),
            P(),
            P(("row", "col"), None),
            P(("row", "col"), None),
            P(None, ("row", "col"), None),
            P(None, ("row", "col"), None),
            P("col", "row", None, None),
            P("col", "row", None, None),
            P(None, "col", "row", None, None),
            P(None, "col", "row", None, None),
            P(None, "col", None),
        ),
        out_specs=(
            P(("row", "col"), None),
            P(("row", "col"), None),
            P(("row", "col"), None),
            P(("row", "col"), None),
            P(None, ("row", "col"), None),
            P(None, ("row", "col"), None),
            P("col", "row", None, None),
            P("col", "row", None, None),
            P(None, "col", "row", None, None),
            P(None, "col", "row", None, None),
        ),
        check_vma=False,
    )
```

profile of v0, /device:TPU:65, one launch (start us, length us, event | category | flops | bytes accessed | tf_op | source)
XLA Modules:
  0.0 759.8 jit_solution(802024007805609347)
XLA Ops:
  7.2 1.2 copy.66
  8.4 1.2 copy.65
  9.9 23.0 %all_to_all.76 = bf16[4,32,2048]{2,0,1:T(4,128)(2,1)S(1)} all-to-all(bf16[4,32,2048]{2,0,1:T(4,128)(2,1)S(1)} %pad_maximum_fusion.5), channel_id=1, replica_groups=mesh['row'=8,'col'=32] {'col'}, dimensions={1} | all-to-all | bytes 1048576 | tf_op jit(solution)/shard_map/all_to_all | solution.py:51
  34.0 0.9 pad_maximum_fusion.4
  35.3 42.4 %all_to_all.77 = bf16[32,16,1024]{2,1,0:T(8,128)(2,1)S(1)} all-to-all(bf16[32,16,1024]{2,1,0:T(8,128)(2,1)S(1)} %broadcast_in_dim.132), channel_id=1, replica_groups=mesh['row'=8,'col'=32] {'col'}, dimensions={0} | all-to-all | bytes 2097152 | tf_op jit(solution)/shard_map/all_to_all | solution.py:23
  77.7 66.5 %all-gather.3.cloned.1.call-done = bf16[1024,2048]{1,0:T(8,128)(2,1)} async-done(((bf16[128,2048]{1,0:T(8,128)(2,1)}), bf16[1024,2048]{1,0:T(8,128)(2,1)}) %all-gather.3.cloned.1.call-update) | async-done | bytes 4194320 | tf_op jit(solution)/shard_map/all_gather | solution.py:60
  144.2 3.0 fusion.22
  147.2 1.4 fusion.27
  148.6 50.5 %all_to_all.78 = bf16[32,16,1024]{2,1,0:T(8,128)(2,1)S(1)} all-to-all(bf16[32,16,1024]{2,1,0:T(8,128)(2,1)S(1)} %bitcast.235), channel_id=1, replica_groups=mesh['row'=8,'col'=32] {'col'}, dimensions={0} | all-to-all | bytes 2097152 | tf_op jit(solution)/shard_map/all_to_all | solution.py:39
  199.5 1.1 broadcast_in_dim.133
  200.6 6.2 all-to-all-start.3
  206.9 91.7 %all-to-all-done.3 = bf16[32,16,1024]{2,1,0:T(8,128)(2,1)S(1)} async-done(((bf16[32,16,1024]{2,1,0:T(8,128)(2,1)}), bf16[32,16,1024]{2,1,0:T(8,128)(2,1)S(1)}, u32[]{:S(2)}, u32[]{:S(2)}) %all-to-all-start.3) | async-done | bytes 1048608 | tf_op jit(solution)/shard_map/all_to_all | solution.py:23
  298.6 1.2 broadcast_in_dim.136
  299.8 6.6 all-to-all-start.5
  308.3 5.5 fusion.102
  313.8 4.1 gather_fusion
  317.9 2.1 gather_fusion.1
  320.0 2.8 broadcast_select_fusion
  322.8 1.4 copy-done.9
  324.2 2.6 fusion.105
  326.8 5.2 all-to-all-done.5
  332.0 4.2 fusion.10
  336.2 2.3 convolution_convert_fusion.2
  338.5 6.2 all-to-all-start.6
  344.7 4.6 convolution_convert_fusion.3
  349.3 20.9 %all-to-all-done.6 = bf16[32,16,1024]{2,1,0:T(8,128)(2,1)S(1)} async-done(((bf16[32,16,1024]{2,1,0:T(8,128)(2,1)}), bf16[32,16,1024]{2,1,0:T(8,128)(2,1)S(1)}, u32[]{:S(2)}, u32[]{:S(2)}) %all-to-all-start.6) | async-done | bytes 1048608 | tf_op jit(solution)/shard_map/all_to_all | solution.py:39
  370.2 6.2 all-to-all-start.4
  376.7 0.9 fusion.97
  377.6 24.4 %all-to-all-done.4 = bf16[32,16,1024]{2,1,0:T(8,128)(2,1)S(1)} async-done(((bf16[32,16,1024]{2,1,0:T(8,128)(2,1)}), bf16[32,16,1024]{2,1,0:T(8,128)(2,1)S(1)}, u32[]{:S(2)}, u32[]{:S(2)}) %all-to-all-start.4) | async-done | bytes 1048608 | tf_op jit(solution)/shard_map/all_to_all | solution.py:39
  402.2 1.6 fusion.86
  403.9 31.6 %all_to_all.79 = bf16[32,16,1024]{2,1,0:T(8,128)(2,1)S(1)} all-to-all(bf16[32,16,1024]{2,1,0:T(8,128)(2,1)S(1)} %broadcast_in_dim.137), channel_id=1, replica_groups=mesh['row'=8,'col'=32] {'col'}, dimensions={0} | all-to-all | bytes 2097152 | tf_op jit(solution)/shard_map/all_to_all | solution.py:23
  435.5 1.5 convolution_convert_fusion
  437.6 2.4 fusion.15
  440.0 1.0 copy-done.36
  441.0 1.3 convolution_convert_fusion.1
  442.3 2.4 pad_maximum_fusion.1
  444.7 6.6 copy.77
  452.5 1.3 copy.73
  453.9 4.6 fusion.100
  458.4 2.3 gather_fusion.3
  460.8 4.2 fusion.32
  464.9 4.2 gather_fusion.2
  469.2 2.2 fusion
  471.4 1.4 fusion.1
  472.8 3.7 pad_maximum_fusion
  476.6 1.2 copy-done.37
  477.8 3.9 fusion.24
  481.6 6.3 all-to-all-start.8
  488.0 50.4 %all-to-all-done.8 = bf16[32,16,1024]{2,1,0:T(8,128)(2,1)S(1)} async-done(((bf16[32,16,1024]{2,1,0:T(8,128)(2,1)}), bf16[32,16,1024]{2,1,0:T(8,128)(2,1)S(1)}, u32[]{:S(2)}, u32[]{:S(2)}) %all-to-all-start.8) | async-done | bytes 1048608 | tf_op jit(solution)/shard_map/all_to_all | solution.py:39
  539.4 38.9 %reduce-scatter.7.cloned.1.call-done = bf16[128,2048]{1,0:T(8,128)(2,1)} async-done(((bf16[1024,2048]{1,0:T(8,128)(2,1)}), bf16[128,2048]{1,0:T(8,128)(2,1)}) %reduce-scatter.7.cloned.1.call-update) | async-done | bytes 524304
  578.3 1.9 fusion.103
  580.2 1.8 convert_element_type.165
  581.9 1.8 convert_element_type.166
  583.7 2.1 maximum_bitcast_fusion.2
  585.8 8.8 %all-to-all-start.9 = ((bf16[32,8,1,1024]{3,1,2,0:T(8,128)(2,1)}), bf16[32,8,1,1024]{3,1,2,0:T(8,128)(2,1)}, u32[]{:S(2)}, u32[]{:S(2)}) async-start(bf16[32,8,1,1024]{3,1,2,0:T(8,128)(2,1)} %maximum_bitcast_fusion.2), calls=%async_computation.9 | async-start | bytes 1048576 | tf_op jit(solution)/shard_map/all_to_all | solution.py:51
  594.6 144.3 %reduce-scatter.5.cloned.1.call-done = bf16[3,128,1024]{2,1,0:T(8,128)(2,1)} async-done(((bf16[24,128,1024]{2,1,0:T(8,128)(2,1)}), bf16[3,128,1024]{2,1,0:T(8,128)(2,1)}) %reduce-scatter.5.cloned.1.call-update) | async-done | bytes 786448 | tf_op jit(solution)/shard_map/reduce_scatter | solution.py:74
  738.9 1.8 fusion.53
  740.7 1.2 maximum_bitcast_fusion
  741.9 1.2 maximum_bitcast_fusion.1
  743.7 2.1 fusion.77
  745.9 1.3 copy.82
  747.2 3.4 fusion.61
  751.2 1.0 pad_maximum_fusion.3
  752.2 1.0 pad_maximum_fusion.2
  (119 shorter events, 8.8 us)
Async XLA Ops:
  7.2 137.0 %all-gather.3.cloned.1.call-start = ((), (), s32[]{:S(2)}) async-start(), calls=%async_computation.12 | async-start | bytes 4718592 | tf_op jit(solution)/shard_map/all_gather | solution.py:60
  32.8 1.1 copy-start.11
  32.8 1.1 copy-start.12
  33.0 1.9 copy-start.16
  33.0 2.0 copy-start.24
  33.9 274.4 %all-gather.5.cloned.1.call-start = ((), (), s32[]{:S(2)}) async-start(), calls=%async_computation.13 | async-start | bytes 7077888 | tf_op jit(solution)/shard_map/all_gather | solution.py:60
  35.1 112.1 %copy-start.25 = (f32[16]{0:T(128)}, f32[16]{0:T(128)S(1)}, u32[]{:S(2)}) copy-start(f32[16]{0:T(128)S(1)} %add_rsqrt_fusion.1) | copy-start | bytes 196
  77.7 69.5 %copy-start.14 = (bf16[32,16,1024]{2,1,0:T(8,128)(2,1)}, bf16[32,16,1024]{2,1,0:T(8,128)(2,1)S(1)}, u32[]{:S(2)}) copy-start(bf16[32,16,1024]{2,1,0:T(8,128)(2,1)S(1)} %all_to_all.77) | copy-start | bytes 3145732
  144.2 3.0 copy-start.31
  147.2 1.4 copy-start.33
  199.1 99.4 %copy-start.22 = (bf16[16,1024]{1,0:T(8,128)(2,1)S(1)}, bf16[16,1024]{1,0:T(8,128)(2,1)}, u32[]{:S(2)}) copy-start(bf16[16,1024]{1,0:T(8,128)(2,1)} %param.17) | copy-start | bytes 98308
  199.4 100.4 %copy-start.19 = (bf16[16,1024]{1,0:T(8,128)(2,1)}, bf16[16,1024]{1,0:T(8,128)(2,1)S(1)}, u32[]{:S(2)}) copy-start(bf16[16,1024]{1,0:T(8,128)(2,1)S(1)} %get-tuple-element.69) | copy-start | bytes 98308
  199.4 100.3 %copy-start.27 = (f32[16]{0:T(128)}, f32[16]{0:T(128)S(1)}, u32[]{:S(2)}) copy-start(f32[16]{0:T(128)S(1)} %add_rsqrt_fusion) | copy-start | bytes 196
  200.6 98.0 %all-to-all-start.3 = ((bf16[32,16,1024]{2,1,0:T(8,128)(2,1)}), bf16[32,16,1024]{2,1,0:T(8,128)(2,1)S(1)}, u32[]{:S(2)}, u32[]{:S(2)}) async-start(bf16[32,16,1024]{2,1,0:T(8,128)(2,1)} %broadcast_in_dim.133), calls=%async_computation.3 | async-start | bytes 2097152 | tf_op jit(solution)/shard_map/all_to_all | solution.py:23
  206.8 99.5 %copy-start.23 = (s32[2,1,16]{2,1,0:T(1,128)S(1)}, s32[2,1,16]{2,1,0:T(1,128)}, u32[]{:S(2)}) copy-start(s32[2,1,16]{2,1,0:T(1,128)} %param.27) | copy-start | bytes 388
  298.6 9.7 %copy-start.5 = (bf16[32,16,1024]{2,1,0:T(8,128)(2,1)}, bf16[32,16,1024]{2,1,0:T(8,128)(2,1)S(1)}, u32[]{:S(2)}) copy-start(bf16[32,16,1024]{2,1,0:T(8,128)(2,1)S(1)} %all-to-all-done.3) | copy-start | bytes 3145732
  299.8 32.2 %all-to-all-start.5 = ((bf16[32,16,1024]{2,1,0:T(8,128)(2,1)}), bf16[32,16,1024]{2,1,0:T(8,128)(2,1)}, u32[]{:S(2)}, u32[]{:S(2)}) async-start(bf16[32,16,1024]{2,1,0:T(8,128)(2,1)} %broadcast_in_dim.136), calls=%async_computation.5 | async-start | bytes 2097152 | tf_op jit(solution)/shard_map/all_to_all | solution.py:23
  320.0 4.2 copy-start.6
  322.8 1.4 copy-start.9
  322.8 9.1 %copy-start.8 = (bf16[16,64,1024]{2,1,0:T(8,128)(2,1)}, bf16[16,64,1024]{2,1,0:T(8,128)(2,1)S(1)}, u32[]{:S(2)}) copy-start(bf16[16,64,1024]{2,1,0:T(8,128)(2,1)S(1)} %get-tuple-element.106) | copy-start | bytes 6291460
  332.0 4.2 copy-start.10
  336.2 2.3 copy-start.35
  338.5 31.8 %all-to-all-start.6 = ((bf16[32,16,1024]{2,1,0:T(8,128)(2,1)}), bf16[32,16,1024]{2,1,0:T(8,128)(2,1)S(1)}, u32[]{:S(2)}, u32[]{:S(2)}) async-start(bf16[32,16,1024]{2,1,0:T(8,128)(2,1)} %bitcast.21), calls=%async_computation.6 | async-start | bytes 2097152 | tf_op jit(solution)/shard_map/all_to_all | solution.py:39
  370.2 31.8 %all-to-all-start.4 = ((bf16[32,16,1024]{2,1,0:T(8,128)(2,1)}), bf16[32,16,1024]{2,1,0:T(8,128)(2,1)S(1)}, u32[]{:S(2)}, u32[]{:S(2)}) async-start(bf16[32,16,1024]{2,1,0:T(8,128)(2,1)} %bitcast.231), calls=%async_computation.4 | async-start | bytes 2097152 | tf_op jit(solution)/shard_map/all_to_all | solution.py:39
  376.5 201.9 %reduce-scatter.7.cloned.1.call-start = ((), (), s32[]{:S(2)}) async-start(), calls=%async_computation.15 | async-start | bytes 4718592
  376.7 0.9 copy-start.18
  402.0 33.5 %copy-start.34 = (f32[512,1024]{1,0:T(8,128)S(1)}, f32[512,1024]{1,0:T(8,128)}, u32[]{:S(2)}) copy-start(f32[512,1024]{1,0:T(8,128)} %copy-done.33) | copy-start | bytes 6291460
  403.8 31.7 %copy-start.20 = (bf16[16,1024]{1,0:T(8,128)(2,1)}, bf16[16,1024]{1,0:T(8,128)(2,1)S(1)}, u32[]{:S(2)}) copy-start(bf16[16,1024]{1,0:T(8,128)(2,1)S(1)} %get-tuple-element.94) | copy-start | bytes 98308
  435.5 2.2 copy-start.32
  437.6 3.3 copy-start.15
  440.0 1.0 copy-start.36
  451.3 287.7 %reduce-scatter.5.cloned.1.call-start = ((), (), s32[]{:S(2)}) async-start(), calls=%async_computation.14 | async-start | bytes 7077888 | tf_op jit(solution)/shard_map/reduce_scatter | solution.py:74
  464.9 4.2 copy-start.29
  469.1 2.3 copy-start
  469.2 2.3 copy-start.28
  469.2 2.3 copy-start.30
  476.5 1.3 copy-start.37
  481.6 56.9 %copy-start.17 = (bf16[16,1024]{1,0:T(8,128)(2,1)S(1)}, bf16[16,1024]{1,0:T(8,128)(2,1)}, u32[]{:S(2)}) copy-start(bf16[16,1024]{1,0:T(8,128)(2,1)} %param.16) | copy-start | bytes 98308
  481.6 57.1 %copy-start.21 = (bf16[16,1024]{1,0:T(8,128)(2,1)S(1)}, bf16[16,1024]{1,0:T(8,128)(2,1)}, u32[]{:S(2)}) copy-start(bf16[16,1024]{1,0:T(8,128)(2,1)} %copy-done.20) | copy-start | bytes 98308
  481.6 57.1 %copy-start.26 = (f32[16]{0:T(128)S(1)}, f32[16]{0:T(128)}, u32[]{:S(2)}) copy-start(f32[16]{0:T(128)} %copy-done.25) | copy-start | bytes 196
  481.6 56.8 %all-to-all-start.8 = ((bf16[32,16,1024]{2,1,0:T(8,128)(2,1)}), bf16[32,16,1024]{2,1,0:T(8,128)(2,1)S(1)}, u32[]{:S(2)}, u32[]{:S(2)}) async-start(bf16[32,16,1024]{2,1,0:T(8,128)(2,1)} %bitcast.23), calls=%async_computation.8 | async-start | bytes 2097152 | tf_op jit(solution)/shard_map/all_to_all | solution.py:39
  539.4 199.5 %copy-start.1 = (f32[2,1,3,64,1024]{4,3,2,1,0:T(8,128)S(1)}, f32[2,1,3,64,1024]{4,3,2,1,0:T(8,128)}, u32[]{:S(2)}) copy-start(f32[2,1,3,64,1024]{4,3,2,1,0:T(8,128)} %param.26) | copy-start | bytes 4718596
  539.4 199.5 %copy-start.2 = (f32[2,1,3,64,1024]{4,3,2,1,0:T(8,128)S(1)}, f32[2,1,3,64,1024]{4,3,2,1,0:T(8,128)}, u32[]{:S(2)}) copy-start(f32[2,1,3,64,1024]{4,3,2,1,0:T(8,128)} %param.25) | copy-start | bytes 4718596
  585.8 160.1 %all-to-all-start.9 = ((bf16[32,8,1,1024]{3,1,2,0:T(8,128)(2,1)}), bf16[32,8,1,1024]{3,1,2,0:T(8,128)(2,1)}, u32[]{:S(2)}, u32[]{:S(2)}) async-start(bf16[32,8,1,1024]{3,1,2,0:T(8,128)(2,1)} %maximum_bitcast_fusion.2), calls=%async_computation.9 | async-start | bytes 1048576 | tf_op jit(solution)/shard_map/all_to_all | solution.py:51
  741.9 1.4 copy-start.7
  741.9 1.8 copy-start.13
  747.2 3.4 copy-start.3
  747.2 3.4 copy-start.4
Sparse Core Ops, SparseCore 0:
  34.0 110.0 all-gather.2
  147.3 136.0 all-gather.4
  451.4 126.8 reduce-scatter.6
  582.4 156.4 reduce-scatter.4
where the time goes:
time: 764 us; the launch traced here: 760 us
  waiting for transfers between devices  442 us (58%)
  blocking collectives  147 us (19%)
  local copies, waits for them, and re-layouts  43.4 us (6%)
  starting transfers between devices  40.4 us (5%)
  other arithmetic  36 us (5%)
  matrix products  35.9 us (5%)
  between operations  14.3 us (2%)
    reduce_scatter x1, waiting for transfers between devices, sent_together_3(): lax.psum_scatter(both, axis, scatter_dimension=dim, tiled=True)  144 us
    all_to_all x2, waiting for transfers between devices, copy_for_each(): lax.all_to_all(jnp.broadcast_to(value[None], (peers, *value.shape)), axis...  96.9 us
    all_to_all x3, waiting for transfers between devices, sent_and_summed(): lax.all_to_all(parts, axis, split_axis=0, concat_axis=0, tiled=True)  95.7 us
    all_to_all x2, blocking collectives, copy_for_each(): lax.all_to_all(jnp.broadcast_to(value[None], (peers, *value.shape)), axis...  73.9 us
    all_gather x2, waiting for transfers between devices, sent_together_2(): lax.all_gather(both, axis, axis=dim, tiled=True)  66.5 us
    all_to_all x1, blocking collectives, sent_and_summed(): lax.all_to_all(parts, axis, split_axis=0, concat_axis=0, tiled=True)  50.5 us
    unnamed x5, waiting for transfers between devices  38.9 us
    all_to_all x1, blocking collectives, sent_together(): lax.all_to_all(both, axis, split_axis=split_dim, concat_axis=concat_dim,...  23 us
  transfers between devices with their start and end apart: 10, of which 8 were waited for; matrix products, arithmetic and copies ran while one was open for 10% of the time, Pallas kernels for 0%

commit v1 on v0

v1 whole, which is shorter than its diff:
```python
import functools

import jax
import jax.numpy as jnp
from jax import lax
from jax.experimental import pallas as pl
from jax.experimental.pallas import tpu as pltpu
from jax.sharding import Mesh, PartitionSpec as P

norm_eps = 1e-06
beta_one = 0.9
beta_two = 0.95
learn_rate = 0.002
decay_rate = 0.1
adam_eps = 1e-08
gelu_coef = 0.7978845608

ALL = ("zh", "y", "zl", "x", "c")
ROW = ("zh", "y")
COL = ("zl", "x", "c")
MESH = pl.DeviceIdType.MESH
BF = jnp.bfloat16
F32 = jnp.float32

def gelu_value(hidden):
    tanh_term = jnp.tanh(gelu_coef * (hidden + 0.044715 * hidden * hidden * hidden))
    return 0.5 * hidden * (1.0 + tanh_term)


def gelu_slope(hidden):
    tanh_term = jnp.tanh(gelu_coef * (hidden + 0.044715 * hidden * hidden * hidden))
    return 0.5 * (1.0 + tanh_term) + 0.5 * hidden * (1.0 - tanh_term * tanh_term) * gelu_coef * (
        1.0 + 0.134145 * hidden * hidden
    )


def adam_update(weight, gradient, moment, second):
    new_moment = beta_one * moment + (1.0 - beta_one) * gradient
    new_second = beta_two * second + (1.0 - beta_two) * gradient * gradient
    weight_float = weight.astype(jnp.float32)
    stepped = weight_float - learn_rate * (
        new_moment / (jnp.sqrt(new_second) + adam_eps) + decay_rate * weight_float
    )
    return (stepped.astype(jnp.bfloat16), new_moment, new_second)


def slot_tables(owner_rows, slot_cap, row_total):
    tile_count = owner_rows.shape[-1]
    positions = jnp.arange(tile_count, dtype=jnp.int32)
    same_owner = owner_rows[..., :, None] == owner_rows[..., None, :]
    earlier = positions[None, :] < positions[:, None]
    tile_rank = jnp.sum(jnp.where(same_owner & earlier, 1, 0), axis=-1).astype(jnp.int32)
    slot_dest = owner_rows * slot_cap + tile_rank
    slot_ids = jnp.arange(row_total * slot_cap, dtype=jnp.int32)
    matches = slot_dest[..., None, :] == slot_ids[:, None]
    slot_tile = jnp.sum(jnp.where(matches, positions, 0), axis=-1)
    slot_live = jnp.any(matches, axis=-1)
    return (slot_dest, slot_tile, slot_live)


def dev_z(z):
    return {"zh": z // 4, "zl": z % 4}


def at(a):
    return lax.axis_index(a)


def place():
    return at("zh") * 4 + at("zl"), at("x"), at("c"), at("y")


def peers_near(with_y):
    z, x, c, y = place()
    peers = [dev_z((z + d) % 8) for d in range(1, 8)]
    peers += [{"x": (x + 1) % 4}, {"x": (x + 3) % 4}, {"c": 1 - c}]
    if with_y:
        peers += [{"y": (y + 1) % 4}, {"y": (y + 3) % 4}]
    return peers


def greet(peers):
    sem = pltpu.get_barrier_semaphore()
    for p in peers:
        pl.semaphore_signal(sem, inc=1, device_id=p, device_id_type=MESH)
    pl.semaphore_wait(sem, len(peers))


def flat_dev(t):
    return {"zh": t // 32, "zl": (t // 8) % 4, "x": (t // 2) % 4, "c": t % 2}


def my_flat():
    z, x, c, _ = place()
    return z * 8 + x * 2 + c


def greet_all():
    me = my_flat()
    y = at("y")
    sem = pltpu.get_barrier_semaphore()

    def one(o, _):
        pl.semaphore_signal(sem, inc=1, device_id=flat_dev((me + o) % 64), device_id_type=MESH)
        return 0

    lax.fori_loop(1, 64, one, 0)
    for d in (1, 3):
        pl.semaphore_signal(sem, inc=1, device_id={"y": (y + d) % 4}, device_id_type=MESH)
    pl.semaphore_wait(sem, 65)


def rcopy(src, dst, ssem, rsem, dev):
    cp = pltpu.make_async_remote_copy(
        src_ref=src, dst_ref=dst, send_sem=ssem, recv_sem=rsem, device_id=dev, device_id_type=MESH
    )
    cp.start()
    return cp


def exchange_start(sbuf, rbuf, ssem, rsem):
    me = my_flat()

    def one(o, _):
        t = (me + o) % 64
        rcopy(sbuf.at[t], rbuf.at[me], ssem, rsem, flat_dev(t))
        return 0

    lax.fori_loop(1, 64, one, 0)
    rbuf[me] = sbuf[me]


def exchange_wait(sbuf, rbuf, ssem, rsem):
    part = pltpu.make_async_copy(rbuf.at[pl.ds(0, 63)], rbuf.at[pl.ds(0, 63)], rsem)
    part.wait()


def exchange_sent(sbuf, ssem):
    part = pltpu.make_async_copy(sbuf.at[pl.ds(0, 63)], sbuf.at[pl.ds(0, 63)], ssem)
    part.wait()


def blk(c, x, n=128, off=0):
    return pl.ds(pl.multiple_of(c * 512 + x * 128 + off, 16), n)


class Gather:
    sems = 7 + 2 + 2 + 4

    def __init__(self, own, full, ss, rs):
        self.own, self.full, self.ss, self.rs = own, full, ss, rs

    def start_z(self):
        z, x, c, _ = place()
        mine = blk(c, x, 16, z * 16)
        self.sent = []
        self.zc = [
            rcopy(self.own, self.full.at[mine], self.ss.at[d - 1], self.rs.at[d - 1], dev_z((z + d) % 8))
            for d in range(1, 8)
        ]
        self.full[mine, :] = self.own[...]

    def move(self, rows, k, dev):
        ref = self.full.at[rows]
        cp = rcopy(ref, ref, self.ss.at[k], self.rs.at[k], dev)
        self.sent.append(cp)
        return cp

    def start_x(self):
        z, x, c, _ = place()
        for cp in self.zc:
            cp.wait_recv()
        self.right = self.move(blk(c, x), 7, {"x": (x + 1) % 4})
        self.left = self.move(blk(c, x), 8, {"x": (x + 3) % 4})
        self.cores = [self.move(blk(c, x), 11, {"c": 1 - c})]

    def forward_x(self):
        z, x, c, _ = place()
        self.right.wait_recv()
        self.fr = self.move(blk(c, (x + 3) % 4, 64), 9, {"x": (x + 1) % 4})
        self.left.wait_recv()
        self.fl = self.move(blk(c, (x + 1) % 4, 64, 64), 10, {"x": (x + 3) % 4})
        self.cores.append(self.move(blk(c, (x + 3) % 4), 12, {"c": 1 - c}))
        self.cores.append(self.move(blk(c, (x + 1) % 4), 13, {"c": 1 - c}))

    def finish(self):
        z, x, c, _ = place()
        self.fr.wait_recv()
        self.fl.wait_recv()
        self.cores.append(self.move(blk(c, (x + 2) % 4), 14, {"c": 1 - c}))
        for cp in self.cores:
            cp.wait_recv()
        for cp in self.zc + self.sent:
            cp.wait_send()


def add_rows(dst, dst_at, terms, rows, step=32):
    for r in range(0, rows, step):
        total = None
        for ref, base in terms:
            v = ref[pl.ds(base + r, step), :].astype(F32)
            total = v if total is None else total + v
        dst[pl.ds(dst_at + r, step), :] = total.astype(dst.dtype)


class Reduce:
    sems = 4 + 2 + 4 + 7

    @staticmethod
    def scratch():
        return [
            pltpu.VMEM((512, 1024), BF),
            pltpu.VMEM((128, 1024), BF),
            pltpu.VMEM((128, 1024), BF),
            pltpu.VMEM((256, 1024), BF),
            pltpu.VMEM((256, 1024), BF),
            pltpu.VMEM((128, 1024), BF),
            pltpu.VMEM((112, 1024), BF),
        ]

    def __init__(self, part, bufs, ss, rs):
        self.part, self.ss, self.rs = part, ss, rs
        self.crecv, self.obuf, self.orecv, self.nbuf, self.xrecv, self.zbuf, self.zrecv = bufs
        self.sent = []

    def send(self, src, dst, k, dev):
        cp = rcopy(src, dst, self.ss.at[k], self.rs.at[k], dev)
        self.sent.append(cp)
        return cp

    def start_c(self):
        z, x, c, _ = place()
        self.cores = []
        for k, d in enumerate((2, 1, 3, 0)):
            xx = (x + d) % 4
            self.cores.append(
                self.send(
                    self.part.at[blk(1 - c, xx)],
                    self.crecv.at[pl.ds(pl.multiple_of(xx * 128, 128), 128)],
                    k,
                    {"c": 1 - c},
                )
            )

    def start_opposite(self):
        z, x, c, _ = place()
        self.cores[0].wait_recv()
        o = (x + 2) % 4
        terms = [(self.part, c * 512 + o * 128), (self.crecv, o * 128)]
        add_rows(self.obuf, 0, terms, 128)
        half = pl.ds(0, 64)
        rest = pl.ds(64, 64)
        self.o_right = self.send(self.obuf.at[half], self.orecv.at[half], 4, {"x": (x + 1) % 4})
        self.o_left = self.send(self.obuf.at[rest], self.orecv.at[rest], 5, {"x": (x + 3) % 4})

    def start_near(self):
        z, x, c, _ = place()
        r, l = (x + 1) % 4, (x + 3) % 4
        self.near = []
        self.cores[1].wait_recv()
        add_rows(self.nbuf, 64, [(self.part, c * 512 + r * 128 + 64), (self.crecv, r * 128 + 64)], 64)
        s = pl.ds(64, 64)
        self.near.append(self.send(self.nbuf.at[s], self.xrecv.at[s], 6, {"x": r}))
        self.cores[2].wait_recv()
        add_rows(self.nbuf, 128, [(self.part, c * 512 + l * 128), (self.crecv, l * 128)], 64)
        s = pl.ds(128, 64)
        self.near.append(self.send(self.nbuf.at[s], self.xrecv.at[s], 7, {"x": l}))

    def finish_near(self):
        z, x, c, _ = place()
        r, l = (x + 1) % 4, (x + 3) % 4
        self.o_right.wait_recv()
        add_rows(
            self.nbuf, 0,
            [(self.part, c * 512 + r * 128), (self.crecv, r * 128), (self.orecv, 0)], 64,
        )
        s = pl.ds(0, 64)
        self.near.append(self.send(self.nbuf.at[s], self.xrecv.at[s], 8, {"x": r}))
        self.o_left.wait_recv()
        add_rows(
            self.nbuf, 192,
            [(self.part, c * 512 + l * 128 + 64), (self.crecv, l * 128 + 64), (self.orecv, 64)], 64,
        )
        s = pl.ds(192, 64)
        self.near.append(self.send(self.nbuf.at[s], self.xrecv.at[s], 9, {"x": l}))

    def start_z(self):
        z, x, c, _ = place()
        self.cores[3].wait_recv()
        for cp in self.near:
            cp.wait_recv()
        terms = [(self.part, c * 512 + x * 128), (self.crecv, x * 128), (self.xrecv, 0), (self.xrecv, 128)]
        add_rows(self.zbuf, 0, terms, 128)
        self.zc = []
        for d in range(1, 8):
            t = (z + d) % 8
            src = self.zbuf.at[pl.ds(pl.multiple_of(t * 16, 16), 16)]
            self.zc.append(self.send(src, self.zrecv.at[pl.ds((d - 1) * 16, 16)], 9 + d, dev_z(t)))

    def total(self):
        z, x, c, _ = place()
        out = self.zbuf[pl.ds(pl.multiple_of(z * 16, 16), 16), :].astype(F32)
        for d in range(1, 8):
            self.zc[d - 1].wait_recv()
            out = out + self.zrecv[pl.ds((d - 1) * 16, 16), :].astype(F32)
        return out

    def drain(self):
        for cp in self.sent:
            cp.wait_send()


def opening_kernel(normed, cot, sbuf, normed_all, cot_all, w_in, w_out, rbuf, gs, gr, ws, wr, ys, yr):
    z, x, c, y = place()
    greet_all()
    exchange_start(sbuf, rbuf, ws, wr)
    a = Gather(normed, normed_all, gs.at[0], gr.at[0])
    b = Gather(cot, cot_all, gs.at[1], gr.at[1])
    a.start_z()
    b.start_z()
    exchange_wait(sbuf, rbuf, ws, wr)
    for h in range(2):
        def tile(q, _):
            v = [rbuf[h * 32 + q * 4 + i].astype(F32) for i in range(4)]
            rows = pl.ds(pl.multiple_of(q * 16, 16), 16)
            w_in[h, y, rows, :] = jnp.concatenate([u[0:4] for u in v], axis=0).astype(BF)
            w_out[h, y, rows, :] = jnp.concatenate([u[4:8] for u in v], axis=0).astype(BF)
            return 0

        lax.fori_loop(0, 8, tile, 0)
    up, down = {"y": (y + 1) % 4}, {"y": (y + 3) % 4}
    ups, downs = {}, {}
    for h in range(2):
        for m, w in enumerate((w_in, w_out)):
            k = h * 2 + m
            ups[h, m] = rcopy(w.at[h, y], w.at[h, y], ys.at[k], yr.at[k], up)
    for h in (1, 0):
        for m, w in enumerate((w_in, w_out)):
            k = 4 + h * 2 + m
            downs[h, m] = rcopy(w.at[h, y], w.at[h, y], ys.at[k], yr.at[k], down)
    a.start_x()
    b.start_x()
    a.forward_x()
    b.forward_x()
    far = []
    for m, w in enumerate((w_in, w_out)):
        ups[0, m].wait_recv()
        s = w.at[0, (y + 3) % 4]
        far.append(rcopy(s, s, ys.at[8 + m], yr.at[8 + m], up))
        downs[1, m].wait_recv()
        s = w.at[1, (y + 1) % 4]
        far.append(rcopy(s, s, ys.at[10 + m], yr.at[10 + m], down))
    a.finish()
    b.finish()
    for m in range(2):
        ups[1, m].wait_recv()
        downs[0, m].wait_recv()
    for cp in far:
        cp.wait_recv()
    for cp in far + list(ups.values()) + list(downs.values()):
        cp.wait_send()
    exchange_sent(sbuf, ws)


def opening(normed, cot, sbuf):
    tok = jax.ShapeDtypeStruct((1024, 1024), BF)
    wt = jax.ShapeDtypeStruct((2, 4, 128, 512), BF)
    n = Gather.sems
    dma = pltpu.SemaphoreType.DMA
    return pl.pallas_call(
        opening_kernel,
        name="opening",
        out_shape=(tok, tok, wt, wt),
        in_specs=[pl.BlockSpec(memory_space=pltpu.VMEM)] * 3,
        out_specs=(pl.BlockSpec(memory_space=pltpu.VMEM),) * 4,
        scratch_shapes=[
            pltpu.VMEM((64, 8, 512), BF),
            dma((2, n)), dma((2, n)), dma, dma, dma((12,)), dma((12,)),
        ],
        compiler_params=pltpu.CompilerParams(collective_id=0, has_side_effects=True, vmem_limit_bytes=40 * 2**20),
        cost_estimate=pl.CostEstimate(flops=40_000_000_000, bytes_accessed=2**23, transcendentals=0),
    )(normed, cot, sbuf)


def turn_kernel(first, part, base, gain, aux, new, full, *scratch):
    n = len(Reduce.scratch())
    bufs, (own, gs, gr, rs, rr) = scratch[:n], scratch[n:]
    greet(peers_near(False))
    r = Reduce(part, bufs, rs, rr)
    r.start_c()
    r.start_opposite()
    r.start_near()
    r.finish_near()
    r.start_z()
    total = r.total()
    if first:
        new_val = (base[...].astype(F32) + total).astype(BF)
        f = new_val.astype(F32)
        inv = lax.rsqrt(jnp.mean(f * f, axis=1, keepdims=True) + norm_eps)
        own[...] = (f * inv * gain[...]).astype(BF)
        new[...] = new_val
        src = own
    else:
        f = aux[...].astype(F32)
        inv = lax.rsqrt(jnp.mean(f * f, axis=1, keepdims=True) + norm_eps)
        gated = total * gain[...]
        new[...] = (
            base[...].astype(F32)
            + inv * gated
            - f * inv * inv * inv * jnp.mean(f * gated, axis=1, keepdims=True)
        ).astype(BF)
        src = new
    g = Gather(src, full, gs, gr)
    g.start_z()
    r.drain()
    g.start_x()
    g.forward_x()
    g.finish()


def turn(first, part, base, gain, aux):
    dma = pltpu.SemaphoreType.DMA
    return pl.pallas_call(
        functools.partial(turn_kernel, first),
        name="turn_one" if first else "turn_two",
        out_shape=(jax.ShapeDtypeStruct((16, 1024), BF), jax.ShapeDtypeStruct((1024, 1024), BF)),
        in_specs=[pl.BlockSpec(memory_space=pltpu.VMEM)] * 4,
        out_specs=(pl.BlockSpec(memory_space=pltpu.VMEM),) * 2,
        scratch_shapes=Reduce.scratch()
        + [pltpu.VMEM((16, 1024), BF), dma((Gather.sems,)), dma((Gather.sems,)), dma((Reduce.sems,)), dma((Reduce.sems,))],
        compiler_params=pltpu.CompilerParams(collective_id=1 if first else 2, has_side_effects=True, vmem_limit_bytes=40 * 2**20),
        cost_estimate=pl.CostEstimate(flops=40_000_000_000, bytes_accessed=2**23, transcendentals=0),
    )(part, base, gain, aux)


def closing_kernel(part_a, part_b, g_in, g_out, sum_a, sum_b, rbuf, *scratch):
    n = len(Reduce.scratch())
    bufs_a, bufs_b = scratch[:n], scratch[n : 2 * n]
    oh, orv, nh, xr_in, sbuf, rs, rr, ys, yr, ws, wr = scratch[2 * n :]
    z, x, c, y = place()
    greet_all()
    up, down = {"y": (y + 1) % 4}, {"y": (y + 3) % 4}
    u, d, o = (y + 1) % 4, (y + 3) % 4, (y + 2) % 4
    gr = (g_in, g_out)
    sent, opp, plain, mixed = [], [], [], []
    for m in range(2):
        opp.append(rcopy(gr[m].at[0, o], orv.at[m, 0], ys.at[m], yr.at[m], up))
        opp.append(rcopy(gr[m].at[1, o], orv.at[m, 1], ys.at[2 + m], yr.at[2 + m], down))
    for m in range(2):
        plain.append(rcopy(gr[m].at[1, u], xr_in.at[m, 0, 1], ys.at[4 + m], yr.at[4 + m], up))
        plain.append(rcopy(gr[m].at[0, d], xr_in.at[m, 1, 0], ys.at[6 + m], yr.at[6 + m], down))
    a = Reduce(part_b, bufs_b, rs.at[0], rr.at[0])
    b = Reduce(part_a, bufs_a, rs.at[1], rr.at[1])
    for r in (a, b):
        r.start_c()
    for r in (a, b):
        r.start_opposite()
    for r in (a, b):
        r.start_near()
    for m in range(2):
        opp[2 * m].wait_recv()
        for s in range(0, 128, 32):
            nh[m, 0, s : s + 32, :] = (
                gr[m][0, u, s : s + 32, :].astype(F32) + orv[m, 0, s : s + 32, :].astype(F32)
            ).astype(BF)
        mixed.append(rcopy(nh.at[m, 0], xr_in.at[m, 0, 0], ys.at[8 + m], yr.at[8 + m], up))
        opp[2 * m + 1].wait_recv()
        for s in range(0, 128, 32):
            nh[m, 1, s : s + 32, :] = (
                gr[m][1, d, s : s + 32, :].astype(F32) + orv[m, 1, s : s + 32, :].astype(F32)
            ).astype(BF)
        mixed.append(rcopy(nh.at[m, 1], xr_in.at[m, 1, 1], ys.at[10 + m], yr.at[10 + m], down))
    for r in (a, b):
        r.finish_near()
    for r in (a, b):
        r.start_z()
    for cp in plain + mixed:
        cp.wait_recv()
    for h in range(2):
        def tile(q, _):
            rows = pl.ds(pl.multiple_of(q * 16, 16), 16)
            t = [
                gr[m][h, y, rows, :].astype(F32)
                + xr_in[m, 0, h, rows, :].astype(F32)
                + xr_in[m, 1, h, rows, :].astype(F32)
                for m in range(2)
            ]
            for i in range(4):
                sbuf[h * 32 + q * 4 + i] = jnp.concatenate(
                    [t[0][4 * i : 4 * i + 4], t[1][4 * i : 4 * i + 4]], axis=0
                ).astype(BF)
            return 0

        lax.fori_loop(0, 8, tile, 0)
    exchange_start(sbuf, rbuf, ws, wr)
    sum_b[...] = a.total()
    sum_a[...] = b.total()
    exchange_wait(sbuf, rbuf, ws, wr)
    exchange_sent(sbuf, ws)
    a.drain()
    b.drain()
    for cp in opp + plain + mixed:
        cp.wait_send()


def closing(part_a, part_b, g_in, g_out):
    dma = pltpu.SemaphoreType.DMA
    tok = jax.ShapeDtypeStruct((16, 1024), F32)
    return pl.pallas_call(
        closing_kernel,
        name="closing",
        out_shape=(tok, tok, jax.ShapeDtypeStruct((64, 8, 512), BF)),
        in_specs=[pl.BlockSpec(memory_space=pltpu.VMEM)] * 4,
        out_specs=(pl.BlockSpec(memory_space=pltpu.VMEM),) * 3,
        scratch_shapes=Reduce.scratch() * 2
        + [
            pltpu.VMEM((2, 2, 128, 512), BF),
            pltpu.VMEM((2, 2, 128, 512), BF),
            pltpu.VMEM((2, 2, 128, 512), BF),
            pltpu.VMEM((2, 2, 2, 128, 512), BF),
            pltpu.VMEM((64, 8, 512), BF),
            dma((2, Reduce.sems)), dma((2, Reduce.sems)), dma((12,)), dma((12,)), dma, dma,
        ],
        compiler_params=pltpu.CompilerParams(collective_id=3, has_side_effects=True, vmem_limit_bytes=48 * 2**20),
        cost_estimate=pl.CostEstimate(flops=40_000_000_000, bytes_accessed=2**23, transcendentals=0),
    )(part_a, part_b, g_in, g_out)


def pick_kernel(idx, slots, w_in, w_out):
    for k in range(16):
        w_in[k * 64 : (k + 1) * 64, :] = slots[idx[0, k], 0:64, :]
        w_out[k * 64 : (k + 1) * 64, :] = slots[idx[1, k], 64:128, :]


def pick(idx, slots):
    wt = jax.ShapeDtypeStruct((1024, 512), BF)
    return pl.pallas_call(
        pick_kernel,
        name="pick",
        out_shape=(wt, wt),
        in_specs=[pl.BlockSpec(memory_space=pltpu.SMEM), pl.BlockSpec(memory_space=pltpu.VMEM)],
        out_specs=(pl.BlockSpec(memory_space=pltpu.VMEM),) * 2,
        cost_estimate=pl.CostEstimate(flops=4_000_000_000, bytes_accessed=2**22, transcendentals=0),
    )(idx, slots)


def place_kernel(idx, live, g_in, g_out, slots):
    for k in range(24):
        for m, g in enumerate((g_in, g_out)):
            v = g[idx[m, k]]
            keep = jnp.full(v.shape, live[m, k], jnp.int32) > 0
            slots[k, m * 64 : (m + 1) * 64, :] = jnp.where(keep, v.astype(F32), 0.0).astype(BF)


def place_slots(idx, live, g_in, g_out):
    return pl.pallas_call(
        place_kernel,
        name="place",
        out_shape=jax.ShapeDtypeStruct((24, 128, 512), BF),
        in_specs=[pl.BlockSpec(memory_space=pltpu.SMEM)] * 2 + [pl.BlockSpec(memory_space=pltpu.VMEM)] * 2,
        out_specs=pl.BlockSpec(memory_space=pltpu.VMEM),
        cost_estimate=pl.CostEstimate(flops=4_000_000_000, bytes_accessed=2**22, transcendentals=0),
    )(idx, live, g_in.reshape(16, 64, 512), g_out.reshape(16, 64, 512))


def dot(a, b, dims, kind=F32):
    return lax.dot_general(a, b, (dims, ((), ())), preferred_element_type=F32).astype(kind)


def shards(
    tokens, grad_out, gains, flat_in, flat_out, flat_moment, flat_second,
    tile_in, tile_out, tile_moment, tile_second, owners,
):
    zh, y = at("zh"), at("y")
    row = zh * 4 + y
    swap = [(0, 1), (1, 0)]

    slot_dest, slot_tile, slot_live = slot_tables(owners[:, 0, :], 3, 8)
    both = jnp.concatenate([tile_in[0], tile_out[0]], axis=1)
    lo, hi = both[:, :, :512], both[:, :, 512:]
    keep, give = jnp.where(zh == 0, lo, hi), jnp.where(zh == 0, hi, lo)
    taken = lax.ppermute(give, "zh", swap)
    slots = lax.all_gather(jnp.concatenate([keep, taken], axis=0), "y", axis=0, tiled=True)
    dest_row, dest_slot = slot_dest // 3, slot_dest % 3
    dest_at = (dest_row % 4) * 6 + ((dest_row // 4) ^ zh) * 3 + dest_slot
    p = jnp.arange(24)
    p_slot = (((p // 3) % 2 ^ zh) * 4 + p // 6) * 3 + p % 3
    out_tile = jnp.take(slot_tile, p_slot, axis=1)
    out_live = jnp.take(slot_live.astype(jnp.int32), p_slot, axis=1)

    tok_float = tokens.astype(F32)
    inv_one = lax.rsqrt(jnp.mean(tok_float * tok_float, axis=1, keepdims=True) + norm_eps)
    normed = (tok_float * inv_one * gains[0]).astype(BF)
    flat = jnp.stack([flat_in.reshape(4, 32, 2, 512), flat_out.reshape(4, 32, 2, 512)])
    sbuf = flat.transpose(3, 2, 0, 1, 4).reshape(64, 8, 512)
    normed_one, cot_two, w_in_one, w_out_one = opening(normed, grad_out, sbuf)
    w_in_one, w_out_one = w_in_one.reshape(1024, 512), w_out_one.reshape(1024, 512)

    hidden_one = dot(normed_one, w_in_one, ((1,), (0,)))
    act_one = gelu_value(hidden_one).astype(BF)
    part = dot(act_one, w_out_one, ((1,), (1,)), BF)
    middle, normed_two = turn(True, part, tokens, gains[1:2], tokens)

    w_in_two, w_out_two = pick(dest_at, slots)
    hidden_two = dot(normed_two, w_in_two, ((1,), (0,)))
    act_two = gelu_value(hidden_two).astype(BF)
    d_act_two = dot(cot_two, w_out_two, ((1,), (0,)))
    d_hidden_two = (d_act_two * gelu_slope(hidden_two)).astype(BF)
    part = dot(d_hidden_two, w_in_two, ((1,), (1,)), BF)
    grad_in_two = dot(normed_two, d_hidden_two, ((0,), (0,)), BF)
    grad_out_two = dot(cot_two, act_two, ((0,), (0,)), BF)
    outgoing = place_slots(out_tile, out_live, grad_in_two, grad_out_two)
    summed = lax.psum_scatter(outgoing, "y", scatter_dimension=0, tiled=True)
    part_two = dot(act_two, w_out_two, ((1,), (1,)), BF)
    grad_mid, cot_one = turn(False, part, grad_out, gains[1:2], middle)

    d_act_one = dot(cot_one, w_out_one, ((1,), (0,)))
    d_hidden_one = (d_act_one * gelu_slope(hidden_one)).astype(BF)
    part = dot(d_hidden_one, w_in_one, ((1,), (1,)), BF)
    grad_in_one = dot(normed_one, d_hidden_one, ((0,), (0,)), BF).reshape(2, 4, 128, 512)
    grad_out_one = dot(cot_one, act_one, ((0,), (0,)), BF).reshape(2, 4, 128, 512)
    sum_two, d_normed, rbuf = closing(part_two, part, grad_in_one, grad_out_one)

    hidden_out = (middle.astype(F32) + sum_two).astype(BF)
    gated = d_normed * gains[0]
    grad_tokens = (
        grad_mid.astype(F32)
        + inv_one * gated
        - tok_float * inv_one * inv_one * inv_one * jnp.mean(tok_float * gated, axis=1, keepdims=True)
    ).astype(BF)

    flat_grad = rbuf.reshape(2, 32, 2, 4, 512).transpose(2, 3, 1, 0, 4).reshape(2, 128, 1024).astype(F32)
    new_flat_in, m_in, v_in = adam_update(flat_in, flat_grad[0], flat_moment[0], flat_second[0])
    new_flat_out, m_out, v_out = adam_update(flat_out, flat_grad[1], flat_moment[1], flat_second[1])

    mine, other = summed[:3], lax.ppermute(summed[3:], "zh", swap)
    lo, hi = jnp.where(zh == 0, mine, other), jnp.where(zh == 0, other, mine)
    tile_grad = jnp.concatenate([lo, hi], axis=2).astype(F32)
    live = lax.dynamic_slice_in_dim(slot_live, row * 3, 3, 1)
    new_tiles, tms, tss = [], [], []
    for m, w in enumerate((tile_in[0], tile_out[0])):
        mask = live[m][:, None, None]
        g = tile_grad[:, m * 64 : (m + 1) * 64, :]
        w2, m2, v2 = adam_update(w, g, tile_moment[m, 0], tile_second[m, 0])
        new_tiles.append(jnp.where(mask, w2, w)[None])
        tms.append(jnp.where(mask, m2, tile_moment[m, 0]))
        tss.append(jnp.where(mask, v2, tile_second[m, 0]))
    return (
        hidden_out, grad_tokens, new_flat_in, new_flat_out,
        jnp.stack([m_in, m_out]), jnp.stack([v_in, v_out]),
        new_tiles[0], new_tiles[1], jnp.stack(tms)[:, None], jnp.stack(tss)[:, None],
    )


def solution(mesh):
    mesh = Mesh(mesh.devices.reshape(2, 4, 4, 4, 2), ALL)
    whole = P(ALL, None)
    state = P(None, ALL, None)
    tile = P(COL, ROW, None, None)
    tile_state = P(None, COL, ROW, None, None)
    return jax.shard_map(
        shards,
        mesh=mesh,
        in_specs=(whole, whole, P(), whole, whole, state, state, tile, tile, tile_state, tile_state, P(None, COL, None)),
        out_specs=(whole, whole, whole, whole, state, state, tile, tile, tile_state, tile_state),
        check_vma=False,
    )
```

time: 764 us -> 318 us (0.42)
  waiting for transfers between devices: 442 us -> 12.7 us
  Pallas kernels: 0 us -> 217 us
  blocking collectives: 147 us -> 0 us
  starting transfers between devices: 40.4 us -> 9.21 us
  local copies, waits for them, and re-layouts: 43.4 us -> 15.5 us
  other arithmetic: 36 us -> 21.1 us
  matrix products: 35.9 us -> 26.2 us
    pallas_call x0 -> x6, Pallas kernels: none -> 217 us  [the longest x2 99.7 us: turn(): pl.pallas_call(functools.partial(turn_kernel, first), name='turn_one' if...]
    all_to_all x6 -> x0, waiting for transfers between devices: 193 us -> none  [the longest x2 96.9 us: copy_for_each(): lax.all_to_all(jnp.broadcast_to(value[None], (peers, *value.shape)), axis...]
    all_to_all x4 -> x0, blocking collectives: 147 us -> none  [the longest x2 73.9 us: copy_for_each(): lax.all_to_all(jnp.broadcast_to(value[None], (peers, *value.shape)), axis...]
    reduce_scatter x1, waiting for transfers between devices: 144 us -> 0.01 us  [shards(): summed = lax.psum_scatter(outgoing, 'y', scatter_dimension=0, tiled=True)]
    all_gather x2 -> x1, waiting for transfers between devices: 66.5 us -> 0.01 us  [shards(): lax.all_gather(jnp.concatenate([keep, taken], axis=0), 'y', axis=0, tiled...]
    all_to_all x6 -> x0, starting transfers between devices: 40.3 us -> none  [the longest x3 18.7 us: sent_and_summed(): lax.all_to_all(parts, axis, split_axis=0, concat_axis=0, tiled=True)]
    unnamed x5 -> x2, waiting for transfers between devices: 38.9 us -> 0.03 us
    ppermute x0 -> x2, waiting for transfers between devices: none -> 12.6 us  [the longest x1 12.6 us: shards(): mine, other = (summed[:3], lax.ppermute(summed[3:], 'zh', swap))]
  transfers between devices with their start and end apart: 10 -> 4, of which waited for: 8 -> 1; matrix products, arithmetic and copies ran while one was open for 10% -> 11% of each run, Pallas kernels for 0% -> 51%
where the time goes in v1:
time: 318 us; the launch traced here: 316 us
  Pallas kernels  217 us (68%)
  matrix products  26.2 us (8%)
  other arithmetic  21.1 us (7%)
  local copies, waits for them, and re-layouts  15.5 us (5%)
  between operations  14.6 us (5%)
  waiting for transfers between devices  12.7 us (4%)
  starting transfers between devices  9.21 us (3%)
    pallas_call x2, Pallas kernels, turn(): pl.pallas_call(functools.partial(turn_kernel, first), name='turn_one' if...  99.7 us
    pallas_call x1, Pallas kernels, closing(): pl.pallas_call(closing_kernel, name='closing', out_shape=(tok, tok, jax.S...  58.4 us
    pallas_call x1, Pallas kernels, opening(): pl.pallas_call(opening_kernel, name='opening', out_shape=(tok, tok, wt, w...  51.4 us
    dot_general x12, matrix products, dot(): lax.dot_general(a, b, (dims, ((), ())), preferred_element_type=F32)  26.2 us
    ppermute x1, waiting for transfers between devices, shards(): mine, other = (summed[:3], lax.ppermute(summed[3:], 'zh', swap))  12.6 us
  transfers between devices with their start and end apart: 4, of which 1 were waited for; matrix products, arithmetic and copies ran while one was open for 11% of the time, Pallas kernels for 51%

profile of v1, /device:TPU:65, one launch (start us, length us, event | category | flops | bytes accessed | tf_op | source)
XLA Modules:
  0.0 316.2 jit_solution(6287704186021799268)
XLA Ops:
  7.2 2.3 broadcast_select_fusion.3
  9.5 5.1 %collective-permute-start = (bf16[3,128,512]{2,1,0:T(8,128)(2,1)}, bf16[3,128,512]{2,1,0:T(8,128)(2,1)S(1)}, u32[]{:S(2)}, u32[]{:S(2)}) collective-permute-start(bf16[3,128,512]{2,1,0:T(8,128)(2,1)} %get-tuple-element.88), channel_id=1, source_target_pairs={{0,128},{128,0},{1,129},{129,1},{2,130},{130,2},{3,131},{131,3},{4... | collective-permute-start | bytes 1179656 | tf_op jit(solution)/shard_map/ppermute | solution.py:582
  14.7 0.9 select_reduce_fusion.1
  15.6 0.7 fusion.62
  16.3 0.1 fusion.58
  16.4 0.1 select_reduce_fusion
  16.5 0.9 fusion.56
  17.5 0.8 fusion.70
  18.4 0.6 gather_fusion.1
  19.1 0.6 gather_fusion
  19.8 1.2 stack_reshape.6
  20.9 0.2 copy.44
  21.2 0.2 stack_reshape.7
  21.3 0.2 copy.45
  21.6 0.3 maximum_bitcast_fusion.2
  21.9 0.1 reshape.91.sbuf
  22.2 51.4 %opening.1 = (bf16[1024,1024]{1,0:T(8,128)(2,1)S(1)}, bf16[1024,1024]{1,0:T(8,128)(2,1)S(1)}, bf16[2,4,128,512]{3,2,1,0:T(8,128)(2,1)S(1)}, bf16[2,4,128,512]{3,2,1,0:T(8,128)(2,1)S(1)}) custom-call(bf16[16,1024]{1,0:T(8,128)(2,1)S(1)} %fusion.51.normed, bf16[16,1024]{1,0:T(8,128)(2,1)S(1)} %copy-done.1, bf16[64,8,512]{2,1,0:T(8,128)(2,1)S(1)} %reshape.91.sbuf), custom_call_target="tpu_custom_call" | custom-call | flops 40000000000 | bytes 8388608 | tf_op jit(solution)/shard_map/opening/pallas_call | solution.py:370
  73.6 1.3 copy-done.2
  74.9 1.3 copy-done.6
  76.2 0.6 fusion.61.idx
  76.8 0.6 select_bitcast_fusion
  77.4 0.9 pad_maximum_fusion.2
  78.4 0.2 reduce-scatter.2.cloned.1.call-start
  78.6 0.6 slice_bitcast_fusion
  79.2 2.8 fusion.71
  82.0 1.4 convolution_convert_fusion.3.part
  83.5 50.1 %turn_one.1 = (bf16[16,1024]{1,0:T(8,128)(2,1)S(1)}, bf16[1024,1024]{1,0:T(8,128)(2,1)S(1)}) custom-call(bf16[1024,1024]{1,0:T(8,128)(2,1)S(1)} %convolution_convert_fusion.3.part, bf16[16,1024]{1,0:T(8,128)(2,1)S(1)} %copy-done, f32[1,1024]{1,0:T(1,128)S(1)} %get-tuple-element.89.gain, bf16[16,1024]{1,0:T(8,128)(2,1)S(1)} %copy-done), custom_call_target="tpu_custom_call" | custom-call | flops 40000000000 | bytes 8388608 | tf_op jit(solution)/shard_map/turn_one/pallas_call | solution.py:423
  133.6 1.4 copy-done.4
  134.9 3.4 %pick.1 = (bf16[1024,512]{1,0:T(8,128)(2,1)}, bf16[1024,512]{1,0:T(8,128)(2,1)}) custom-call(s32[2,16]{1,0:T(2,128)} %fusion.61.idx, bf16[24,128,512]{2,1,0:T(8,128)(2,1)} %all-gather.2.cloned.1.call-done.slots), custom_call_target="tpu_custom_call" | custom-call | flops 4000000000 | bytes 4194304 | tf_op jit(solution)/shard_map/pick/pallas_call | solution.py:537
  138.3 3.2 %fusion.72 = f32[1024,512]{1,0:T(8,128)S(1)} fusion(bf16[1024,1024]{1,0:T(8,128)(2,1)} %copy-done.4, bf16[1024,512]{1,0:T(8,128)(2,1)} %get-tuple-element.29), kind=kOutput, calls=%fused_computation.169 | convolution fusion | flops 1073741824 | bytes 5242880 | tf_op jit(solution)/shard_map/dot_general | solution.py:567
  141.6 2.4 convolution_convert_fusion.4
  144.0 2.2 fusion.8
  146.2 2.3 convolution_convert_fusion.5
  148.5 1.3 convolution_convert_fusion.1.part
  149.8 49.6 %turn_two.1 = (bf16[16,1024]{1,0:T(8,128)(2,1)S(1)}, bf16[1024,1024]{1,0:T(8,128)(2,1)S(1)}) custom-call(bf16[1024,1024]{1,0:T(8,128)(2,1)S(1)} %convolution_convert_fusion.1.part, bf16[16,1024]{1,0:T(8,128)(2,1)S(1)} %copy-done.1, f32[1,1024]{1,0:T(1,128)S(1)} %get-tuple-element.89.gain, bf16[16,1024]{1,0:T(8,128)(2,1)S(1)} %get-tuple-element.27.aux), custom_call_target="tpu_custom_call" | custom-call | flops 40000000000 | bytes 8388608 | tf_op jit(solution)/shard_map/turn_two/pallas_call | solution.py:423
  199.4 2.5 fusion.13
  201.9 4.1 %place.1 = bf16[24,128,512]{2,1,0:T(8,128)(2,1)} custom-call(s32[2,24]{1,0:T(2,128)} %get-tuple-element.94.idx, s32[2,24]{1,0:T(2,128)} %get-tuple-element.93.live, bf16[16,64,512]{2,1,0:T(8,128)(2,1)} %bitcast.152, bf16[16,64,512]{2,1,0:T(8,128)(2,1)} %bitcast.151), custom_call_target="tpu_custom_call" | custom-call | flops 4000000000 | bytes 4194304 | tf_op jit(solution)/shard_map/place/pallas_call | solution.py:556
  206.0 2.7 convolution_convert_fusion.part_b
  208.7 2.7 convolution_convert_fusion.7
  211.4 1.4 convolution_convert_fusion.2.part_a
  212.8 0.2 copy-done.9
  213.0 0.6 copy-done.29
  213.6 1.4 convolution_convert_fusion.6
  215.0 58.4 %closing.1 = (f32[16,1024]{1,0:T(8,128)S(1)}, f32[16,1024]{1,0:T(8,128)S(1)}, bf16[64,8,512]{2,1,0:T(8,128)(2,1)S(1)}) custom-call(bf16[1024,1024]{1,0:T(8,128)(2,1)S(1)} %convolution_convert_fusion.2.part_a, bf16[1024,1024]{1,0:T(8,128)(2,1)} %convolution_convert_fusion.part_b, bf16[2,4,128,512]{3,2,1,0:T(8,128)(2,1)S(1)} %bitcast.136, ...), custom_call_target="tpu_custom_call" | custom-call | flops 40000000000 | bytes 8388608 | tf_op jit(solution)/shard_map/closing/pallas_call | solution.py:509
  273.4 0.3 reshape.98
  273.9 0.4 copy.47
  274.3 0.4 copy.46
  274.7 1.2 slice.82
  275.9 1.2 slice.83
  277.2 0.1 fusion.57
  277.3 0.7 fusion.55
  278.0 2.7 multiply_add_fusion.3
  280.8 1.0 slice.103
  281.8 3.8 %collective-permute-start.1 = (bf16[3,128,512]{2,1,0:T(8,128)(2,1)S(1)}, bf16[3,128,512]{2,1,0:T(8,128)(2,1)S(1)}, u32[]{:S(2)}, u32[]{:S(2)}) collective-permute-start(bf16[3,128,512]{2,1,0:T(8,128)(2,1)S(1)} %slice.103), channel_id=1, source_target_pairs={{0,128},{128,0},{1,129},{129,1},{2,130},{130,2},{3,131},{131,3},{4... | collective-permute-start | bytes 1179656 | tf_op jit(solution)/shard_map/ppermute | solution.py:636
  285.6 3.1 pad_maximum_fusion
  288.7 0.1 copy.57
  288.8 0.1 copy.58
  288.9 0.7 copy-done.17
  289.7 1.6 fusion.35
  291.3 12.6 %collective-permute-done.1 = bf16[3,128,512]{2,1,0:T(8,128)(2,1)S(1)} collective-permute-done((bf16[3,128,512]{2,1,0:T(8,128)(2,1)S(1)}, bf16[3,128,512]{2,1,0:T(8,128)(2,1)S(1)}, u32[]{:S(2)}, u32[]{:S(2)}) %collective-permute-start.1) | collective-permute-done | bytes 393248 | tf_op jit(solution)/shard_map/ppermute | solution.py:636
  304.0 0.2 maximum_convert_fusion
  304.3 2.1 fusion.48
  306.4 1.0 fusion.27
  307.4 2.0 maximum_bitcast_fusion
  (87 shorter events, 1.0 us)
Async XLA Ops:
  7.2 14.0 %copy-start.16 = (bf16[128,1024]{1,0:T(8,128)(2,1)S(1)}, bf16[128,1024]{1,0:T(8,128)(2,1)}, u32[]{:S(2)}) copy-start(bf16[128,1024]{1,0:T(8,128)(2,1)} %param.18) | copy-start | bytes 786436
  7.2 127.8 %all-gather.2.cloned.1.call-start = ((), (), s32[]{:S(2)}) async-start(), calls=%async_computation.1 | async-start | bytes 3932160 | tf_op jit(solution)/shard_map/all_gather | solution.py:583
  9.5 67.9 %collective-permute-start = (bf16[3,128,512]{2,1,0:T(8,128)(2,1)}, bf16[3,128,512]{2,1,0:T(8,128)(2,1)S(1)}, u32[]{:S(2)}, u32[]{:S(2)}) collective-permute-start(bf16[3,128,512]{2,1,0:T(8,128)(2,1)} %get-tuple-element.88), channel_id=1, source_target_pairs={{0,128},{128,0},{1,129},{129,1},{2,130},{130,2},{3,131},{131,3},{4... | collective-permute-start | bytes 1179656 | tf_op jit(solution)/shard_map/ppermute | solution.py:582
  17.4 4.6 %copy-start.25 = (f32[16]{0:T(128)}, f32[16]{0:T(128)S(1)}, u32[]{:S(2)}) copy-start(f32[16]{0:T(128)S(1)} %add_rsqrt_fusion) | copy-start | bytes 196
  18.3 3.8 %copy-start.20 = (f32[1,1024]{1,0:T(1,128)}, f32[1,1024]{1,0:T(1,128)S(1)}, u32[]{:S(2)}) copy-start(f32[1,1024]{1,0:T(1,128)S(1)} %get-tuple-element.90) | copy-start | bytes 12292
  19.8 2.3 copy-start
  19.8 2.4 copy-start.1
  22.2 54.1 %copy-start.22 = (s32[2,1,16]{2,1,0:T(1,128)S(1)}, s32[2,1,16]{2,1,0:T(1,128)}, u32[]{:S(2)}) copy-start(s32[2,1,16]{2,1,0:T(1,128)} %param.25) | copy-start | bytes 388
  73.6 1.3 copy-start.2
  74.9 1.3 copy-start.6
  78.4 202.4 %reduce-scatter.2.cloned.1.call-start = ((), (), s32[]{:S(2)}) async-start(), calls=%async_computation.2 | async-start | bytes 3932160 | tf_op jit(solution)/shard_map/reduce_scatter | solution.py:613
  82.0 1.4 copy-start.27
  133.6 1.4 copy-start.4
  138.3 3.3 %copy-start.7 = (bf16[1024,1024]{1,0:T(8,128)(2,1)S(1)}, bf16[1024,1024]{1,0:T(8,128)(2,1)}, u32[]{:S(2)}) copy-start(bf16[1024,1024]{1,0:T(8,128)(2,1)} %copy-done.6) | copy-start | bytes 6291460
  141.5 2.4 copy-start.30
  141.6 2.4 copy-start.33
  144.0 2.2 copy-start.5
  146.2 2.3 copy-start.32
  149.8 49.6 %copy-start.28 = (f32[1024,512]{1,0:T(8,128)S(1)}, f32[1024,512]{1,0:T(8,128)}, u32[]{:S(2)}) copy-start(f32[1024,512]{1,0:T(8,128)} %copy-done.27) | copy-start | bytes 6291460
  199.4 2.5 copy-start.8
  201.9 4.1 %copy-start.35 = (bf16[1024,512]{1,0:T(8,128)(2,1)}, bf16[1024,512]{1,0:T(8,128)(2,1)S(1)}, u32[]{:S(2)}) copy-start(bf16[1024,512]{1,0:T(8,128)(2,1)S(1)} %fusion.13) | copy-start | bytes 3145732
  206.0 2.7 copy-start.3
  208.7 2.7 copy-start.31
  208.7 2.7 copy-start.34
  211.4 1.6 copy-start.9
  211.4 2.2 copy-start.29
  273.8 3.4 %copy-start.21 = (f32[1,1024]{1,0:T(1,128)S(1)}, f32[1,1024]{1,0:T(1,128)}, u32[]{:S(2)}) copy-start(f32[1,1024]{1,0:T(1,128)} %copy-done.20) | copy-start | bytes 12292
  273.8 3.5 %copy-start.26 = (f32[16]{0:T(128)S(1)}, f32[16]{0:T(128)}, u32[]{:S(2)}) copy-start(f32[16]{0:T(128)} %copy-done.25) | copy-start | bytes 196
  273.8 4.2 %copy-start.12 = (f32[2,128,1024]{2,1,0:T(8,128)S(1)}, f32[2,128,1024]{2,1,0:T(8,128)}, u32[]{:S(2)}) copy-start(f32[2,128,1024]{2,1,0:T(8,128)} %param.19) | copy-start | bytes 3145732
  273.8 4.2 %copy-start.13 = (f32[2,128,1024]{2,1,0:T(8,128)S(1)}, f32[2,128,1024]{2,1,0:T(8,128)}, u32[]{:S(2)}) copy-start(f32[2,128,1024]{2,1,0:T(8,128)} %param.20) | copy-start | bytes 3145732
  281.8 22.2 %collective-permute-start.1 = (bf16[3,128,512]{2,1,0:T(8,128)(2,1)S(1)}, bf16[3,128,512]{2,1,0:T(8,128)(2,1)S(1)}, u32[]{:S(2)}, u32[]{:S(2)}) collective-permute-start(bf16[3,128,512]{2,1,0:T(8,128)(2,1)S(1)} %slice.103), channel_id=1, source_target_pairs={{0,128},{128,0},{1,129},{129,1},{2,130},{130,2},{3,131},{131,3},{4... | collective-permute-start | bytes 1179656 | tf_op jit(solution)/shard_map/ppermute | solution.py:636
  288.7 0.9 copy-start.17
  288.7 1.0 copy-start.18
  289.7 14.2 %copy-start.19 = (bf16[6,128,512]{2,1,0:T(8,128)(2,1)S(1)}, bf16[6,128,512]{2,1,0:T(8,128)(2,1)}, u32[]{:S(2)}) copy-start(bf16[6,128,512]{2,1,0:T(8,128)(2,1)} %reduce-scatter.2.cloned.1.call-done) | copy-start | bytes 2359300
  291.3 12.9 %copy-start.10 = (f32[2,1,3,64,1024]{4,3,2,1,0:T(8,128)S(1)}, f32[2,1,3,64,1024]{4,3,2,1,0:T(8,128)}, u32[]{:S(2)}) copy-start(f32[2,1,3,64,1024]{4,3,2,1,0:T(8,128)} %param.23) | copy-start | bytes 4718596
  291.3 12.9 %copy-start.11 = (f32[2,1,3,64,1024]{4,3,2,1,0:T(8,128)S(1)}, f32[2,1,3,64,1024]{4,3,2,1,0:T(8,128)}, u32[]{:S(2)}) copy-start(f32[2,1,3,64,1024]{4,3,2,1,0:T(8,128)} %param.24) | copy-start | bytes 4718596
  291.3 12.9 %copy-start.14 = (bf16[1,3,64,1024]{3,2,1,0:T(8,128)(2,1)S(1)}, bf16[1,3,64,1024]{3,2,1,0:T(8,128)(2,1)}, u32[]{:S(2)}) copy-start(bf16[1,3,64,1024]{3,2,1,0:T(8,128)(2,1)} %param.22) | copy-start | bytes 1179652
  291.3 12.9 %copy-start.15 = (bf16[1,3,64,1024]{3,2,1,0:T(8,128)(2,1)S(1)}, bf16[1,3,64,1024]{3,2,1,0:T(8,128)(2,1)}, u32[]{:S(2)}) copy-start(bf16[1,3,64,1024]{3,2,1,0:T(8,128)(2,1)} %param.21) | copy-start | bytes 1179652
  291.3 13.0 %copy-start.23 = (pred[3]{0:T(512)(128)(4,1)S(1)}, pred[3]{0:T(512)(128)(4,1)}, u32[]{:S(2)}) copy-start(pred[3]{0:T(512)(128)(4,1)} %get-tuple-element.91) | copy-start | bytes 13
  291.3 12.9 %copy-start.24 = (pred[3]{0:T(512)(128)(4,1)S(1)}, pred[3]{0:T(512)(128)(4,1)}, u32[]{:S(2)}) copy-start(pred[3]{0:T(512)(128)(4,1)} %get-tuple-element.92) | copy-start | bytes 13
Sparse Core Ops, SparseCore 0:
  78.5 42.1 all-gather.1
  206.1 53.8 reduce-scatter.1

commit v2 on v1

v2 whole, which is shorter than its diff:
```python
import functools

import jax
import jax.numpy as jnp
from jax import lax
from jax.experimental import pallas as pl
from jax.experimental.pallas import tpu as pltpu
from jax.sharding import Mesh, PartitionSpec as P

norm_eps = 1e-06
beta_one = 0.9
beta_two = 0.95
learn_rate = 0.002
decay_rate = 0.1
adam_eps = 1e-08
gelu_coef = 0.7978845608

ALL = ("zh", "y", "zl", "x", "c")
ROW = ("zh", "y")
COL = ("zl", "x", "c")
MESH = pl.DeviceIdType.MESH
BF = jnp.bfloat16
F32 = jnp.float32

def gelu_value(hidden):
    tanh_term = jnp.tanh(gelu_coef * (hidden + 0.044715 * hidden * hidden * hidden))
    return 0.5 * hidden * (1.0 + tanh_term)


def gelu_slope(hidden):
    tanh_term = jnp.tanh(gelu_coef * (hidden + 0.044715 * hidden * hidden * hidden))
    return 0.5 * (1.0 + tanh_term) + 0.5 * hidden * (1.0 - tanh_term * tanh_term) * gelu_coef * (
        1.0 + 0.134145 * hidden * hidden
    )


def adam_update(weight, gradient, moment, second):
    new_moment = beta_one * moment + (1.0 - beta_one) * gradient
    new_second = beta_two * second + (1.0 - beta_two) * gradient * gradient
    weight_float = weight.astype(jnp.float32)
    stepped = weight_float - learn_rate * (
        new_moment / (jnp.sqrt(new_second) + adam_eps) + decay_rate * weight_float
    )
    return (stepped.astype(jnp.bfloat16), new_moment, new_second)


def dev_z(z):
    return {"zh": z // 4, "zl": z % 4}


def at(a):
    return lax.axis_index(a)


def place():
    return at("zh") * 4 + at("zl"), at("x"), at("c"), at("y")


def peers_near(with_y):
    z, x, c, y = place()
    peers = [dev_z((z + d) % 8) for d in range(1, 8)]
    peers += [{"x": (x + 1) % 4}, {"x": (x + 3) % 4}, {"c": 1 - c}]
    if with_y:
        peers += [{"y": (y + 1) % 4}, {"y": (y + 3) % 4}]
    return peers


def greet(peers):
    sem = pltpu.get_barrier_semaphore()
    for p in peers:
        pl.semaphore_signal(sem, inc=1, device_id=p, device_id_type=MESH)
    pl.semaphore_wait(sem, len(peers))


def flat_dev(t):
    return {"zh": t // 32, "zl": (t // 8) % 4, "x": (t // 2) % 4, "c": t % 2}


def my_flat():
    z, x, c, _ = place()
    return z * 8 + x * 2 + c


def greet_all():
    me = my_flat()
    y = at("y")
    sem = pltpu.get_barrier_semaphore()

    def one(o, _):
        pl.semaphore_signal(sem, inc=1, device_id=flat_dev((me + o) % 64), device_id_type=MESH)
        return 0

    lax.fori_loop(1, 64, one, 0)
    for d in (1, 3):
        pl.semaphore_signal(sem, inc=1, device_id={"y": (y + d) % 4}, device_id_type=MESH)
    pl.semaphore_wait(sem, 65)


def rcopy(src, dst, ssem, rsem, dev):
    cp = pltpu.make_async_remote_copy(
        src_ref=src, dst_ref=dst, send_sem=ssem, recv_sem=rsem, device_id=dev, device_id_type=MESH
    )
    cp.start()
    return cp


def exchange_start(sbuf, rbuf, ssem, rsem):
    me = my_flat()

    def one(o, _):
        t = (me + o) % 64
        rcopy(sbuf.at[t], rbuf.at[me], ssem, rsem, flat_dev(t))
        return 0

    lax.fori_loop(1, 64, one, 0)
    rbuf[me] = sbuf[me]


def exchange_wait(sbuf, rbuf, ssem, rsem):
    part = pltpu.make_async_copy(rbuf.at[pl.ds(0, 63)], rbuf.at[pl.ds(0, 63)], rsem)
    part.wait()


def exchange_sent(sbuf, ssem):
    part = pltpu.make_async_copy(sbuf.at[pl.ds(0, 63)], sbuf.at[pl.ds(0, 63)], ssem)
    part.wait()


def blk(c, x, n=128, off=0):
    return pl.ds(pl.multiple_of(c * 512 + x * 128 + off, 16), n)


class Gather:
    sems = 7 + 2 + 2 + 4

    def __init__(self, own, full, ss, rs):
        self.own, self.full, self.ss, self.rs = own, full, ss, rs

    def start_z(self):
        z, x, c, _ = place()
        mine = blk(c, x, 16, z * 16)
        self.sent = []
        self.zc = [
            rcopy(self.own, self.full.at[mine], self.ss.at[d - 1], self.rs.at[d - 1], dev_z((z + d) % 8))
            for d in range(1, 8)
        ]
        self.full[mine, :] = self.own[...]

    def move(self, rows, k, dev):
        ref = self.full.at[rows]
        cp = rcopy(ref, ref, self.ss.at[k], self.rs.at[k], dev)
        self.sent.append(cp)
        return cp

    def start_x(self):
        z, x, c, _ = place()
        for cp in self.zc:
            cp.wait_recv()
        self.right = self.move(blk(c, x), 7, {"x": (x + 1) % 4})
        self.left = self.move(blk(c, x), 8, {"x": (x + 3) % 4})
        self.cores = [self.move(blk(c, x), 11, {"c": 1 - c})]

    def forward_x(self):
        z, x, c, _ = place()
        self.right.wait_recv()
        self.fr = self.move(blk(c, (x + 3) % 4, 64), 9, {"x": (x + 1) % 4})
        self.left.wait_recv()
        self.fl = self.move(blk(c, (x + 1) % 4, 64, 64), 10, {"x": (x + 3) % 4})
        self.cores.append(self.move(blk(c, (x + 3) % 4), 12, {"c": 1 - c}))
        self.cores.append(self.move(blk(c, (x + 1) % 4), 13, {"c": 1 - c}))

    def finish(self):
        z, x, c, _ = place()
        self.fr.wait_recv()
        self.fl.wait_recv()
        self.cores.append(self.move(blk(c, (x + 2) % 4), 14, {"c": 1 - c}))
        for cp in self.cores:
            cp.wait_recv()
        for cp in self.zc + self.sent:
            cp.wait_send()


def add_rows(dst, dst_at, terms, rows, step=32):
    for r in range(0, rows, step):
        total = None
        for ref, base in terms:
            v = ref[pl.ds(base + r, step), :].astype(F32)
            total = v if total is None else total + v
        dst[pl.ds(dst_at + r, step), :] = total.astype(dst.dtype)


class Reduce:
    sems = 4 + 2 + 4 + 7

    @staticmethod
    def scratch():
        return [
            pltpu.VMEM((512, 1024), BF),
            pltpu.VMEM((128, 1024), BF),
            pltpu.VMEM((128, 1024), BF),
            pltpu.VMEM((256, 1024), BF),
            pltpu.VMEM((256, 1024), BF),
            pltpu.VMEM((128, 1024), BF),
            pltpu.VMEM((112, 1024), BF),
        ]

    def __init__(self, part, bufs, ss, rs):
        self.part, self.ss, self.rs = part, ss, rs
        self.crecv, self.obuf, self.orecv, self.nbuf, self.xrecv, self.zbuf, self.zrecv = bufs
        self.sent = []

    def send(self, src, dst, k, dev):
        cp = rcopy(src, dst, self.ss.at[k], self.rs.at[k], dev)
        self.sent.append(cp)
        return cp

    def start_c(self):
        z, x, c, _ = place()
        self.cores = []
        for k, d in enumerate((2, 1, 3, 0)):
            xx = (x + d) % 4
            self.cores.append(
                self.send(
                    self.part.at[blk(1 - c, xx)],
                    self.crecv.at[pl.ds(pl.multiple_of(xx * 128, 128), 128)],
                    k,
                    {"c": 1 - c},
                )
            )

    def start_opposite(self):
        z, x, c, _ = place()
        self.cores[0].wait_recv()
        o = (x + 2) % 4
        terms = [(self.part, c * 512 + o * 128), (self.crecv, o * 128)]
        add_rows(self.obuf, 0, terms, 128)
        half = pl.ds(0, 64)
        rest = pl.ds(64, 64)
        self.o_right = self.send(self.obuf.at[half], self.orecv.at[half], 4, {"x": (x + 1) % 4})
        self.o_left = self.send(self.obuf.at[rest], self.orecv.at[rest], 5, {"x": (x + 3) % 4})

    def start_near(self):
        z, x, c, _ = place()
        r, l = (x + 1) % 4, (x + 3) % 4
        self.near = []
        self.cores[1].wait_recv()
        add_rows(self.nbuf, 64, [(self.part, c * 512 + r * 128 + 64), (self.crecv, r * 128 + 64)], 64)
        s = pl.ds(64, 64)
        self.near.append(self.send(self.nbuf.at[s], self.xrecv.at[s], 6, {"x": r}))
        self.cores[2].wait_recv()
        add_rows(self.nbuf, 128, [(self.part, c * 512 + l * 128), (self.crecv, l * 128)], 64)
        s = pl.ds(128, 64)
        self.near.append(self.send(self.nbuf.at[s], self.xrecv.at[s], 7, {"x": l}))

    def finish_near(self):
        z, x, c, _ = place()
        r, l = (x + 1) % 4, (x + 3) % 4
        self.o_right.wait_recv()
        add_rows(
            self.nbuf, 0,
            [(self.part, c * 512 + r * 128), (self.crecv, r * 128), (self.orecv, 0)], 64,
        )
        s = pl.ds(0, 64)
        self.near.append(self.send(self.nbuf.at[s], self.xrecv.at[s], 8, {"x": r}))
        self.o_left.wait_recv()
        add_rows(
            self.nbuf, 192,
            [(self.part, c * 512 + l * 128 + 64), (self.crecv, l * 128 + 64), (self.orecv, 64)], 64,
        )
        s = pl.ds(192, 64)
        self.near.append(self.send(self.nbuf.at[s], self.xrecv.at[s], 9, {"x": l}))

    def start_z(self):
        z, x, c, _ = place()
        self.cores[3].wait_recv()
        for cp in self.near:
            cp.wait_recv()
        terms = [(self.part, c * 512 + x * 128), (self.crecv, x * 128), (self.xrecv, 0), (self.xrecv, 128)]
        add_rows(self.zbuf, 0, terms, 128)
        self.zc = []
        for d in range(1, 8):
            t = (z + d) % 8
            src = self.zbuf.at[pl.ds(pl.multiple_of(t * 16, 16), 16)]
            self.zc.append(self.send(src, self.zrecv.at[pl.ds((d - 1) * 16, 16)], 9 + d, dev_z(t)))

    def total(self):
        z, x, c, _ = place()
        out = self.zbuf[pl.ds(pl.multiple_of(z * 16, 16), 16), :].astype(F32)
        for d in range(1, 8):
            self.zc[d - 1].wait_recv()
            out = out + self.zrecv[pl.ds((d - 1) * 16, 16), :].astype(F32)
        return out

    def drain(self):
        for cp in self.sent:
            cp.wait_send()


class YGather:
    def __init__(self, own, full, ss, rs):
        self.own, self.full, self.ss, self.rs = own, full, ss, rs

    def copy(self, src, m, h, yy, k, dev):
        return rcopy(src, self.full[m].at[h, yy], self.ss.at[k], self.rs.at[k], dev)

    def start(self):
        y = at("y")
        self.up, self.down = {"y": (y + 1) % 4}, {"y": (y + 3) % 4}
        self.ups, self.downs = {}, {}
        for h in range(2):
            for m in range(2):
                self.ups[h, m] = self.copy(self.own(m, h), m, h, y, h * 2 + m, self.up)
        for h in (1, 0):
            for m in range(2):
                self.downs[h, m] = self.copy(self.own(m, h), m, h, y, 4 + h * 2 + m, self.down)

    def forward(self):
        y = at("y")
        self.far = []
        for m in range(2):
            self.ups[0, m].wait_recv()
            yy = (y + 3) % 4
            self.far.append(self.copy(self.full[m].at[0, yy], m, 0, yy, 8 + m, self.up))
            self.downs[1, m].wait_recv()
            yy = (y + 1) % 4
            self.far.append(self.copy(self.full[m].at[1, yy], m, 1, yy, 10 + m, self.down))

    def finish(self):
        for m in range(2):
            self.ups[1, m].wait_recv()
            self.downs[0, m].wait_recv()
        for cp in self.far:
            cp.wait_recv()

    def drain(self):
        for cp in self.far + list(self.ups.values()) + list(self.downs.values()):
            cp.wait_send()


class YReduce:
    @staticmethod
    def scratch(rows):
        return [
            pltpu.VMEM((2, 2, rows, 512), BF),
            pltpu.VMEM((2, 2, rows, 512), BF),
            pltpu.VMEM((2, 2, 2, rows, 512), BF),
        ]

    def __init__(self, part, rows, bufs, ss, rs):
        self.part, self.rows, self.ss, self.rs = part, rows, ss, rs
        self.orv, self.nh, self.xin = bufs

    def copy(self, src, dst, k, dev):
        return rcopy(src, dst, self.ss.at[k], self.rs.at[k], dev)

    def start(self):
        y = at("y")
        self.up, self.down = {"y": (y + 1) % 4}, {"y": (y + 3) % 4}
        u, d, o = (y + 1) % 4, (y + 3) % 4, (y + 2) % 4
        self.opp, self.plain, self.mixed = [], [], []
        for m in range(2):
            self.opp.append(self.copy(self.part[m].at[0, o], self.orv.at[m, 0], m, self.up))
            self.opp.append(self.copy(self.part[m].at[1, o], self.orv.at[m, 1], 2 + m, self.down))
        for m in range(2):
            self.plain.append(self.copy(self.part[m].at[1, u], self.xin.at[m, 0, 1], 4 + m, self.up))
            self.plain.append(self.copy(self.part[m].at[0, d], self.xin.at[m, 1, 0], 6 + m, self.down))

    def middle(self):
        y = at("y")
        u, d = (y + 1) % 4, (y + 3) % 4
        for m in range(2):
            for h, yy, dev in ((0, u, self.up), (1, d, self.down)):
                self.opp[2 * m + h].wait_recv()
                for s in range(0, self.rows, 32):
                    self.nh[m, h, s : s + 32, :] = (
                        self.part[m][h, yy, s : s + 32, :].astype(F32) + self.orv[m, h, s : s + 32, :].astype(F32)
                    ).astype(BF)
                self.mixed.append(self.copy(self.nh.at[m, h], self.xin.at[m, h, h], 8 + 2 * h + m, dev))

    def finish(self):
        for cp in self.plain + self.mixed:
            cp.wait_recv()

    def total(self, m, h, rows):
        return (
            self.part[m][h, at("y"), rows, :].astype(F32)
            + self.xin[m, 0, h, rows, :].astype(F32)
            + self.xin[m, 1, h, rows, :].astype(F32)
        )

    def drain(self):
        for cp in self.opp + self.plain + self.mixed:
            cp.wait_send()


def inv_rms(f):
    return lax.rsqrt(jnp.mean(f * f, axis=1, keepdims=True) + norm_eps)


def slot_of(owners, m, k):
    own, rank = owners[m, k], jnp.int32(0)
    for j in range(16):
        rank = rank + jnp.where((owners[m, j] == own) & (j < k), 1, 0)
    return own * 3 + rank


def ones_if(hit):
    return jnp.full((64, 512), jnp.where(hit, 1.0, 0.0), F32).astype(BF)


def half(h):
    return pl.ds(pl.multiple_of(h * 512, 128), 512)


def opening_kernel(
    tokens, cot, gains, sbuf, t_in, t_out, normed_all, cot_all, w_in, w_out, pair, rbuf, normed, gs, gr, ws, wr, ys, yr, ps, pr
):
    z, x, c, y = place()
    zh = at("zh")
    f = tokens[...].astype(F32)
    normed[...] = (f * inv_rms(f) * gains[0:1, :]).astype(BF)
    greet_all()
    exchange_start(sbuf, rbuf, ws, wr)
    a = Gather(normed, normed_all, gs.at[0], gr.at[0])
    b = Gather(cot, cot_all, gs.at[1], gr.at[1])
    a.start_z()
    b.start_z()
    pairs = [
        rcopy(t.at[:, :, half(1 - zh)], pair.at[m, zh], ps.at[m], pr.at[m], {"zh": 1 - zh})
        for m, t in enumerate((t_in, t_out))
    ]
    for m, t in enumerate((t_in, t_out)):
        pair[m, zh] = t[:, :, half(zh)]
    exchange_wait(sbuf, rbuf, ws, wr)
    for h in range(2):
        def tile(q, _):
            v = [rbuf[h * 32 + q * 4 + i].astype(F32) for i in range(4)]
            rows = pl.ds(pl.multiple_of(q * 16, 16), 16)
            w_in[h, y, rows, :] = jnp.concatenate([u[0:4] for u in v], axis=0).astype(BF)
            w_out[h, y, rows, :] = jnp.concatenate([u[4:8] for u in v], axis=0).astype(BF)
            return 0

        lax.fori_loop(0, 8, tile, 0)
    full = (w_in, w_out)
    yg = YGather(lambda m, h: full[m].at[h, y], full, ys, yr)
    yg.start()
    a.start_x()
    b.start_x()
    a.forward_x()
    yg.forward()
    b.forward_x()
    a.finish()
    b.finish()
    yg.finish()
    for cp in pairs:
        cp.wait_recv()
        cp.wait_send()
    yg.drain()
    exchange_sent(sbuf, ws)


VM = pl.BlockSpec(memory_space=pltpu.VMEM)
SM = pl.BlockSpec(memory_space=pltpu.SMEM)
DMA = pltpu.SemaphoreType.DMA


def comm_call(kernel, name, ident, out_shape, scratch, in_specs, args):
    return pl.pallas_call(
        kernel,
        name=name,
        out_shape=out_shape,
        in_specs=in_specs,
        out_specs=(VM,) * len(out_shape),
        scratch_shapes=scratch,
        compiler_params=pltpu.CompilerParams(collective_id=ident, has_side_effects=True, vmem_limit_bytes=56 * 2**20),
        cost_estimate=pl.CostEstimate(flops=40_000_000_000, bytes_accessed=2**23, transcendentals=0),
    )(*args)


def shape(*dims, kind=BF):
    return jax.ShapeDtypeStruct(dims, kind)


def opening(*args):
    n = Gather.sems
    out = (shape(1024, 1024), shape(1024, 1024), shape(2, 4, 128, 512), shape(2, 4, 128, 512), shape(2, 2, 3, 64, 512))
    scratch = [
        pltpu.VMEM((64, 8, 512), BF), pltpu.VMEM((16, 1024), BF),
        DMA((2, n)), DMA((2, n)), DMA, DMA, DMA((12,)), DMA((12,)), DMA((2,)), DMA((2,)),
    ]
    return comm_call(opening_kernel, "opening", 0, out, scratch, [VM] * 6, args)


def turn_one_kernel(owners, part, tokens, gains, pair, new, full, w_in, w_out, s_in, s_out, *scratch):
    n = len(Reduce.scratch())
    bufs, (own, gs, gr, rs, rr, ys, yr) = scratch[:n], scratch[n:]
    y = at("y")
    slots = (s_in, s_out)
    greet(peers_near(True))
    r = Reduce(part, bufs, rs, rr)
    r.start_c()
    yg = YGather(lambda m, h: pair.at[m, h], slots, ys, yr)
    yg.start()
    r.start_opposite()
    r.start_near()
    for m in range(2):
        for h in range(2):
            slots[m][h, y] = pair[m, h]
    r.finish_near()
    yg.forward()
    r.start_z()
    total = r.total()
    mid = (tokens[...].astype(F32) + total).astype(BF)
    f = mid.astype(F32)
    own[...] = (f * inv_rms(f) * gains[1:2, :]).astype(BF)
    new[...] = mid
    g = Gather(own, full, gs, gr)
    g.start_z()
    r.drain()
    g.start_x()
    yg.finish()
    for m, w in enumerate((w_in, w_out)):
        def tile(k, _, m=m, w=w):
            want = slot_of(owners, m, k)
            total = jnp.zeros((64, 512), BF)
            for q in range(24):
                r, s = q // 3, q % 3
                total = total + slots[m][r // 4, r % 4, s * 64 : (s + 1) * 64, :] * ones_if(want == q)
            w[pl.ds(pl.multiple_of(k * 64, 64), 64), :] = total
            return 0

        lax.fori_loop(0, 16, tile, 0)
    g.forward_x()
    g.finish()
    yg.drain()


def turn_one(*args):
    out = (shape(16, 1024), shape(1024, 1024), shape(1024, 512), shape(1024, 512))
    scratch = [pltpu.VMEM((2, 4, 192, 512), BF)] * 2 + Reduce.scratch() + [
        pltpu.VMEM((16, 1024), BF), DMA((Gather.sems,)), DMA((Gather.sems,)), DMA((Reduce.sems,)), DMA((Reduce.sems,)),
        DMA((12,)), DMA((12,)),
    ]
    return comm_call(turn_one_kernel, "turn_one", 1, out, scratch, [SM] + [VM] * 4, args)


def before_input(f, inv, gated, base):
    return base + inv * gated - f * inv * inv * inv * jnp.mean(f * gated, axis=1, keepdims=True)


def turn_two_kernel(owners, part, cot, mid, gains, g_in, g_out, new, full, tile_sum, p_in, p_out, *scratch):
    n = len(Reduce.scratch())
    bufs, ybufs, (gs, gr, rs, rr, ys, yr) = scratch[:n], scratch[n : n + 3], scratch[n + 3 :]
    z, x, c, y = place()
    greet(peers_near(True))
    r = Reduce(part, bufs, rs, rr)
    r.start_c()
    r.start_opposite()
    r.start_near()
    parts = (p_in, p_out)
    for m, g in enumerate((g_in, g_out)):
        dest = [slot_of(owners, m, k) for k in range(16)]

        def slot(q, _, g=g, p=parts[m], dest=dest):
            row, s = q // 3, q % 3
            total = jnp.zeros((64, 512), BF)
            for k in range(16):
                total = total + g[k] * ones_if(dest[k] == q)
            p[row // 4, row % 4, pl.ds(pl.multiple_of(s * 64, 64), 64), :] = total
            return 0

        lax.fori_loop(0, 24, slot, 0)
    yr_ = YReduce(parts, 192, ybufs, ys, yr)
    yr_.start()
    r.finish_near()
    r.start_z()
    total = r.total()
    f = mid[...].astype(F32)
    new[...] = before_input(f, inv_rms(f), total * gains[1:2, :], cot[...].astype(F32)).astype(BF)
    g = Gather(new, full, gs, gr)
    g.start_z()
    yr_.middle()
    r.drain()
    g.start_x()
    g.forward_x()
    yr_.finish()
    for m in range(2):
        for h in range(2):
            for s in range(0, 192, 32):
                rows = pl.ds(s, 32)
                tile_sum[m, h, rows, :] = yr_.total(m, h, rows).astype(BF)
    g.finish()
    yr_.drain()


def turn_two(*args):
    out = (shape(16, 1024), shape(1024, 1024), shape(2, 2, 192, 512))
    scratch = [pltpu.VMEM((2, 4, 192, 512), BF)] * 2 + Reduce.scratch() + YReduce.scratch(192) + [
        DMA((Gather.sems,)), DMA((Gather.sems,)), DMA((Reduce.sems,)), DMA((Reduce.sems,)), DMA((12,)), DMA((12,)),
    ]
    return comm_call(turn_two_kernel, "turn_two", 2, out, scratch, [SM] + [VM] * 6, args)


def closing_kernel(
    part_two, part_one, g_in, g_out, tokens, mid, grad_mid, gains, tile_sum,
    hidden_out, grad_tokens, rbuf, tile_grad, sbuf, tile_got, *scratch,
):
    n = len(Reduce.scratch())
    bufs_a, bufs_b, ybufs = scratch[:n], scratch[n : 2 * n], scratch[2 * n : 2 * n + 3]
    rs, rr, ys, yr, ws, wr, ps, pr = scratch[2 * n + 3 :]
    zh = at("zh")
    greet_all()
    red = YReduce((g_in, g_out), 128, ybufs, ys, yr)
    red.start()
    a = Reduce(part_one, bufs_a, rs.at[0], rr.at[0])
    b = Reduce(part_two, bufs_b, rs.at[1], rr.at[1])
    for r in (a, b):
        r.start_c()
    pairs = [
        rcopy(tile_sum.at[m, 1 - zh], tile_got.at[m], ps.at[m], pr.at[m], {"zh": 1 - zh}) for m in range(2)
    ]
    for r in (a, b):
        r.start_opposite()
    for r in (a, b):
        r.start_near()
    red.middle()
    for r in (a, b):
        r.finish_near()
    for r in (a, b):
        r.start_z()
    red.finish()
    for h in range(2):
        def tile(q, _):
            rows = pl.ds(pl.multiple_of(q * 16, 16), 16)
            t = [red.total(m, h, rows) for m in range(2)]
            for i in range(4):
                sbuf[h * 32 + q * 4 + i] = jnp.concatenate(
                    [t[0][4 * i : 4 * i + 4], t[1][4 * i : 4 * i + 4]], axis=0
                ).astype(BF)
            return 0

        lax.fori_loop(0, 8, tile, 0)
    exchange_start(sbuf, rbuf, ws, wr)
    for m, cp in enumerate(pairs):
        cp.wait_recv()
        tile_grad[m, :, half(zh)] = tile_sum[m, zh]
        tile_grad[m, :, half(1 - zh)] = tile_got[m]
    f = tokens[...].astype(F32)
    grad_tokens[...] = before_input(f, inv_rms(f), a.total() * gains[0:1, :], grad_mid[...].astype(F32)).astype(BF)
    hidden_out[...] = (mid[...].astype(F32) + b.total()).astype(BF)
    exchange_wait(sbuf, rbuf, ws, wr)
    exchange_sent(sbuf, ws)
    a.drain()
    b.drain()
    red.drain()
    for cp in pairs:
        cp.wait_send()


def closing(*args):
    out = (shape(16, 1024), shape(16, 1024), shape(64, 8, 512), shape(2, 192, 1024))
    scratch = [pltpu.VMEM((64, 8, 512), BF), pltpu.VMEM((2, 192, 512), BF)]
    scratch += Reduce.scratch() * 2 + YReduce.scratch(128) + [
        DMA((2, Reduce.sems)), DMA((2, Reduce.sems)), DMA((12,)), DMA((12,)), DMA, DMA, DMA((2,)), DMA((2,)),
    ]
    return comm_call(closing_kernel, "closing", 3, out, scratch, [VM] * 9, args)


def adam_kernel(
    owners, rbuf, tile_grad, f_in, f_out, fm, fv, t_in, t_out, tm, tv,
    nf_in, nf_out, nfm, nfv, nt_in, nt_out, ntm, ntv, wide,
):
    d = pl.program_id(0)

    @pl.when(d == 0)
    def _():
        for q in range(4):
            wide[q] = rbuf[:, :, q * 128 : (q + 1) * 128].astype(F32).reshape(512, 128)

    row = at("zh") * 4 + at("y")
    for m, (w, nw) in enumerate(((f_in, nf_in), (f_out, nf_out))):
        for h in range(2):
            for q in range(4):
                cols = slice(h * 512 + q * 128, h * 512 + q * 128 + 128)
                grad = wide[q, pl.ds(h * 256 + m * 4 + d, 32, stride=8), :]
                w1, m1, v1 = adam_update(w[:, cols], grad, fm[m, :, cols], fv[m, :, cols])
                nw[:, cols] = w1
                nfm[m, :, cols] = m1
                nfv[m, :, cols] = v1
    for m, (w, nw) in enumerate(((t_in, nt_in), (t_out, nt_out))):
        count = jnp.int32(0)
        for k in range(16):
            count = count + jnp.where(owners[m, k] == row, 1, 0)
        for i in range(3):
            rows = slice(16 * i, 16 * i + 16)
            at_row = lax.broadcasted_iota(jnp.int32, (16, 1024), 0) + (d * 48 + 16 * i)
            keep = at_row < count * 64
            w0, m0, v0 = w[rows, :], tm[m, rows, :], tv[m, rows, :]
            w1, m1, v1 = adam_update(w0, tile_grad[m, rows, :].astype(F32), m0, v0)
            nw[rows, :] = jnp.where(keep, w1.astype(F32), w0.astype(F32)).astype(BF)
            ntm[m, rows, :] = jnp.where(keep, m1, m0)
            ntv[m, rows, :] = jnp.where(keep, v1, v0)


def adam(*args):
    flat = pl.BlockSpec((32, 1024), lambda d: (d, 0))
    tile = pl.BlockSpec((48, 1024), lambda d: (d, 0))
    flats = pl.BlockSpec((2, 32, 1024), lambda d: (0, d, 0))
    tiles = pl.BlockSpec((2, 48, 1024), lambda d: (0, d, 0))
    state = [flat, flat, flats, flats, tile, tile, tiles, tiles]
    return pl.pallas_call(
        adam_kernel,
        name="adam",
        grid=(4,),
        out_shape=(
            shape(128, 1024), shape(128, 1024), shape(2, 128, 1024, kind=F32), shape(2, 128, 1024, kind=F32),
            shape(192, 1024), shape(192, 1024), shape(2, 192, 1024, kind=F32), shape(2, 192, 1024, kind=F32),
        ),
        in_specs=[SM, VM, tiles] + state,
        out_specs=tuple(state),
        scratch_shapes=[pltpu.VMEM((4, 512, 128), F32)],
        cost_estimate=pl.CostEstimate(flops=4_000_000_000, bytes_accessed=13 * 2**20, transcendentals=0),
    )(*args)


def dot(a, b, dims, kind=F32):
    return lax.dot_general(a, b, (dims, ((), ())), preferred_element_type=F32).astype(kind)


def shards(
    tokens, grad_out, gains, flat_in, flat_out, flat_moment, flat_second,
    tile_in, tile_out, tile_moment, tile_second, owners,
):
    own = owners[:, 0, :]
    flat = jnp.stack([flat_in.reshape(4, 32, 2, 512), flat_out.reshape(4, 32, 2, 512)])
    sbuf = flat.transpose(3, 2, 0, 1, 4).reshape(64, 8, 512)
    normed_one, cot_two, w_in_one, w_out_one, pair = opening(tokens, grad_out, gains, sbuf, tile_in[0], tile_out[0])
    w_in_one, w_out_one = w_in_one.reshape(1024, 512), w_out_one.reshape(1024, 512)

    hidden_one = dot(normed_one, w_in_one, ((1,), (0,)))
    act_one = gelu_value(hidden_one).astype(BF)
    part = dot(act_one, w_out_one, ((1,), (1,)), BF)
    middle, normed_two, w_in_two, w_out_two = turn_one(own, part, tokens, gains, pair.reshape(2, 2, 192, 512))

    hidden_two = dot(normed_two, w_in_two, ((1,), (0,)))
    act_two = gelu_value(hidden_two).astype(BF)
    d_act_two = dot(cot_two, w_out_two, ((1,), (0,)))
    d_hidden_two = (d_act_two * gelu_slope(hidden_two)).astype(BF)
    part = dot(d_hidden_two, w_in_two, ((1,), (1,)), BF)
    grad_in_two = dot(normed_two, d_hidden_two, ((0,), (0,)), BF).reshape(16, 64, 512)
    grad_out_two = dot(cot_two, act_two, ((0,), (0,)), BF).reshape(16, 64, 512)
    grad_mid, cot_one, tile_sum = turn_two(own, part, grad_out, middle, gains, grad_in_two, grad_out_two)
    part_two = dot(act_two, w_out_two, ((1,), (1,)), BF)

    d_act_one = dot(cot_one, w_out_one, ((1,), (0,)))
    d_hidden_one = (d_act_one * gelu_slope(hidden_one)).astype(BF)
    part = dot(d_hidden_one, w_in_one, ((1,), (1,)), BF)
    grad_in_one = dot(normed_one, d_hidden_one, ((0,), (0,)), BF).reshape(2, 4, 128, 512)
    grad_out_one = dot(cot_one, act_one, ((0,), (0,)), BF).reshape(2, 4, 128, 512)
    hidden_out, grad_tokens, rbuf, tile_grad = closing(
        part_two, part, grad_in_one, grad_out_one, tokens, middle, grad_mid, gains, tile_sum
    )
    tile, tiles = (192, 1024), (2, 192, 1024)
    outs = adam(
        own, rbuf, tile_grad, flat_in, flat_out, flat_moment, flat_second,
        tile_in.reshape(tile), tile_out.reshape(tile), tile_moment.reshape(tiles), tile_second.reshape(tiles),
    )
    return (
        hidden_out, grad_tokens, *outs[:4], outs[4].reshape(tile_in.shape), outs[5].reshape(tile_in.shape),
        outs[6].reshape(tile_moment.shape), outs[7].reshape(tile_moment.shape),
    )


def solution(mesh):
    mesh = Mesh(mesh.devices.reshape(2, 4, 4, 4, 2), ALL)
    whole = P(ALL, None)
    state = P(None, ALL, None)
    tile = P(COL, ROW, None, None)
    tile_state = P(None, COL, ROW, None, None)
    return jax.shard_map(
        shards,
        mesh=mesh,
        in_specs=(whole, whole, P(), whole, whole, state, state, tile, tile, tile_state, tile_state, P(None, COL, None)),
        out_specs=(whole, whole, whole, whole, state, state, tile, tile, tile_state, tile_state),
        check_vma=False,
    )
```

time: 318 us -> 263 us (0.83)
  other arithmetic: 21.1 us -> 0.34 us
  between operations: 14.6 us -> 0.83 us
  waiting for transfers between devices: 12.7 us -> 0 us
  local copies, waits for them, and re-layouts: 15.5 us -> 4.9 us
  starting transfers between devices: 9.21 us -> 0 us
  matrix products: 26.2 us -> 32.7 us
  Pallas kernels: 217 us -> 222 us
    ppermute x2 -> x0, waiting for transfers between devices: 12.6 us -> none  [the longest x1 12.6 us: shards(): mine, other = (summed[:3], lax.ppermute(summed[3:], 'zh', swap))]
    ppermute x2 -> x0, starting transfers between devices: 8.95 us -> none  [the longest x1 5.11 us: shards(): taken = lax.ppermute(give, 'zh', swap)]
    dot_general x12, matrix products: 26.2 us -> 32.7 us  [dot(): lax.dot_general(a, b, (dims, ((), ())), preferred_element_type=F32)]
    slice x7 -> x0, local copies, waits for them, and re-layouts: 5.18 us -> none  [the longest x3 1.73 us: shards(): flat_grad[1]]
    unnamed x74 -> x22, local copies, waits for them, and re-layouts: 5.94 us -> 1.27 us
    pallas_call x6 -> x5, Pallas kernels: 217 us -> 222 us  [the longest x4 214 us: comm_call(): pl.pallas_call(kernel, name=name, out_shape=out_shape, in_specs=in_specs,...]
    another operation x2 -> x0, other arithmetic: 4.05 us -> none  [the longest x1 3.08 us: shards(): jnp.stack([m_in, m_out])]
    add x2 -> x0, other arithmetic: 3.31 us -> none  [the longest x1 2.72 us: adam_update(): new_moment = beta_one * moment + (1.0 - beta_one) * gradient]
  transfers between devices with their start and end apart: 4 -> 0, of which waited for: 1 -> 0; matrix products, arithmetic and copies ran while one was open for 11% -> 0% of each run, Pallas kernels for 51% -> 0%
where the time goes in v2:
time: 263 us; the launch traced here: 260 us
  Pallas kernels  222 us (84%)
  matrix products  32.7 us (12%)
  local copies, waits for them, and re-layouts  4.9 us (2%)
    pallas_call x4, Pallas kernels, comm_call(): pl.pallas_call(kernel, name=name, out_shape=out_shape, in_specs=in_specs,...  214 us
    dot_general x12, matrix products, dot(): lax.dot_general(a, b, (dims, ((), ())), preferred_element_type=F32)  32.7 us
    pallas_call x1, Pallas kernels, adam(): pl.pallas_call(adam_kernel, name='adam', grid=(4,), out_shape=(shape(128,...  7.38 us

profile of v2, /device:TPU:65, one launch (start us, length us, event | category | flops | bytes accessed | tf_op | source)
XLA Modules:
  0.0 260.3 jit_solution(5148192537501120533)
XLA Ops:
  0.6 1.2 stack_reshape.6
  1.8 0.2 copy.22
  2.0 1.2 stack_reshape.7
  3.2 0.2 copy.23
  3.4 0.3 maximum_bitcast_fusion
  3.7 0.9 reshape.68.sbuf
  4.6 56.4 %opening.1 = (bf16[1024,1024]{1,0:T(8,128)(2,1)}, bf16[1024,1024]{1,0:T(8,128)(2,1)}, bf16[2,4,128,512]{3,2,1,0:T(8,128)(2,1)}, bf16[2,4,128,512]{3,2,1,0:T(8,128)(2,1)}, bf16[2,2,3,64,512]{4,3,2,1,0:T(8,128)(2,1)}) custom-call(bf16[16,1024]{1,0:T(8,128)(2,1)} %tokens.5, bf16[16,1024]{1,0:T(8,128)(2,1)} %cot.3, f32[2,1024]{1,0:T(2,128)} %gains.7, ...), custom_call_target="tpu_custom_call" | custom-call | flops 40000000000 | bytes 8388608 | tf_op jit(solution)/shard_map/opening/pallas_call | solution.py:468
  61.0 0.0 copy-start.3
  61.0 3.2 %fusion.14 = f32[1024,512]{1,0:T(8,128)S(1)} fusion(bf16[1024,1024]{1,0:T(8,128)(2,1)} %get-tuple-element.34, bf16[1024,512]{1,0:T(8,128)(2,1)} %bitcast.55), kind=kOutput, calls=%fused_computation.29 | convolution fusion | flops 1073741824 | bytes 5242880 | tf_op jit(solution)/shard_map/dot_general | solution.py:727
  64.2 0.0 copy-done.3
  64.2 2.7 %convolution_convert_fusion.3.part = bf16[1024,1024]{1,0:T(8,128)(2,1)} fusion(bf16[1024,512]{1,0:T(8,128)(2,1)S(1)} %bitcast.57, f32[1024,512]{1,0:T(8,128)S(1)} %fusion.14), kind=kOutput, calls=%fused_computation.23 | convolution fusion | flops 1079508992 | bytes 5242880 | tf_op jit(solution)/shard_map/dot_general | solution.py:727
  67.0 49.4 %turn_one.1 = (bf16[16,1024]{1,0:T(8,128)(2,1)}, bf16[1024,1024]{1,0:T(8,128)(2,1)}, bf16[1024,512]{1,0:T(8,128)(2,1)}, bf16[1024,512]{1,0:T(8,128)(2,1)}) custom-call(s32[2,16]{1,0:T(2,128)} %bitcast.50, bf16[1024,1024]{1,0:T(8,128)(2,1)} %convolution_convert_fusion.3.part, bf16[16,1024]{1,0:T(8,128)(2,1)} %tokens.5, f32[2,1024]{1,0:T(2,128)} %gains.7, ...), custom_call_target="tpu_custom_call" | custom-call | flops 40000000000 | bytes 8388608 | tf_op jit(solution)/shard_map/turn_one/pallas_call | solution.py:468
  116.4 0.0 copy-start.7
  116.4 0.0 copy-start.8
  116.5 3.2 %fusion.15 = f32[1024,512]{1,0:T(8,128)S(1)} fusion(bf16[1024,1024]{1,0:T(8,128)(2,1)} %get-tuple-element.38, bf16[1024,512]{1,0:T(8,128)(2,1)} %get-tuple-element.39), kind=kOutput, calls=%fused_computation.30 | convolution fusion | flops 1073741824 | bytes 5242880 | tf_op jit(solution)/shard_map/dot_general | solution.py:727
  119.7 0.0 copy-done.7
  119.7 0.0 copy-done.8
  119.7 2.2 fusion.8
  122.0 2.4 convolution_convert_fusion.6
  124.4 0.0 copy-start.5
  124.4 2.7 %convolution_convert_fusion.2.part_two = bf16[1024,1024]{1,0:T(8,128)(2,1)} fusion(bf16[1024,512]{1,0:T(8,128)(2,1)S(1)} %copy-done.7, f32[1024,512]{1,0:T(8,128)S(1)} %fusion.15), kind=kOutput, calls=%fused_computation.22 | convolution fusion | flops 1079508992 | bytes 5242880 | tf_op jit(solution)/shard_map/dot_general | solution.py:727
  127.1 0.0 copy-done.5
  127.1 0.0 copy-start.6
  127.1 2.2 convolution_convert_fusion.7
  129.4 0.0 copy-done.6
  129.4 2.6 %convolution_convert_fusion.1.part = bf16[1024,1024]{1,0:T(8,128)(2,1)} fusion(bf16[1024,512]{1,0:T(8,128)(2,1)S(1)} %fusion.8, bf16[1024,512]{1,0:T(8,128)(2,1)S(1)} %copy-done.6), kind=kOutput, calls=%fused_computation.21 | convolution fusion | flops 1074790400 | bytes 4194304 | tf_op jit(solution)/shard_map/dot_general | solution.py:727
  132.0 53.6 %turn_two.1 = (bf16[16,1024]{1,0:T(8,128)(2,1)}, bf16[1024,1024]{1,0:T(8,128)(2,1)}, bf16[2,2,192,512]{3,2,1,0:T(8,128)(2,1)}) custom-call(s32[2,16]{1,0:T(2,128)} %bitcast.51, bf16[1024,1024]{1,0:T(8,128)(2,1)} %convolution_convert_fusion.1.part, bf16[16,1024]{1,0:T(8,128)(2,1)} %cot.3, bf16[16,1024]{1,0:T(8,128)(2,1)} %get-tuple-element.42.mid, ...), custom_call_target="tpu_custom_call" | custom-call | flops 40000000000 | bytes 8388608 | tf_op jit(solution)/shard_map/turn_two/pallas_call | solution.py:468
  185.6 0.0 copy-start.9
  185.6 4.0 %fusion.13 = bf16[1024,512]{1,0:T(8,128)(2,1)S(1)} fusion(f32[1024,512]{1,0:T(8,128)S(1)} %fusion.14, bf16[1024,1024]{1,0:T(8,128)(2,1)} %get-tuple-element.43, bf16[1024,512]{1,0:T(8,128)(2,1)S(1)} %bitcast.58), kind=kOutput, calls=%fused_computation.17 | convolution fusion | flops 1083703296 | bytes 6291456 | tf_op jit(solution)/shard_map/dot_general | solution.py:727
  189.5 0.0 copy-done.9
  189.5 0.0 copy-start.4
  189.6 2.4 convolution_convert_fusion.4
  192.0 0.0 copy-done.4
  192.0 0.0 copy-start.2
  192.0 2.3 convolution_convert_fusion.5
  194.2 0.0 copy-done.2
  194.2 2.6 %convolution_convert_fusion.part_one = bf16[1024,1024]{1,0:T(8,128)(2,1)} fusion(bf16[1024,512]{1,0:T(8,128)(2,1)S(1)} %fusion.13, bf16[1024,512]{1,0:T(8,128)(2,1)S(1)} %bitcast.56), kind=kOutput, calls=%fused_computation.20 | convolution fusion | flops 1074790400 | bytes 4194304 | tf_op jit(solution)/shard_map/dot_general | solution.py:727
  196.9 54.8 %closing.1 = (bf16[16,1024]{1,0:T(8,128)(2,1)}, bf16[16,1024]{1,0:T(8,128)(2,1)}, bf16[64,8,512]{2,1,0:T(8,128)(2,1)}, bf16[2,192,1024]{2,1,0:T(8,128)(2,1)}) custom-call(bf16[1024,1024]{1,0:T(8,128)(2,1)} %convolution_convert_fusion.2.part_two, bf16[1024,1024]{1,0:T(8,128)(2,1)} %convolution_convert_fusion.part_one, bf16[2,4,128,512]{3,2,1,0:T(8,128)(2,1)} %bitcast.60, ...), custom_call_target="tpu_custom_call" | custom-call | flops 40000000000 | bytes 8388608 | tf_op jit(solution)/shard_map/closing/pallas_call | solution.py:468
  251.6 0.0 copy-start.1
  251.6 0.0 copy-start
  251.7 7.4 %adam.1 = (bf16[128,1024]{1,0:T(8,128)(2,1)}, bf16[128,1024]{1,0:T(8,128)(2,1)}, f32[2,128,1024]{2,1,0:T(8,128)}, f32[2,128,1024]{2,1,0:T(8,128)}, bf16[192,1024...) custom-call(s32[2,16]{1,0:T(2,128)} %bitcast.52, ...), custom_call_target="tpu_custom_call" | custom-call | flops 4000000000 | bytes 13631488 | tf_op jit(solution)/shard_map/adam/pallas_call | solution.py:711
  259.0 0.0 copy-done.1
  259.0 0.6 copy.28
  259.7 0.0 copy-done
  259.7 0.6 copy.29
Async XLA Ops:
  61.0 3.2 %copy-start.3 = (bf16[2,4,128,512]{3,2,1,0:T(8,128)(2,1)S(1)}, bf16[2,4,128,512]{3,2,1,0:T(8,128)(2,1)}, u32[]{:S(2)}) copy-start(bf16[2,4,128,512]{3,2,1,0:T(8,128)(2,1)} %get-tuple-element.36) | copy-start | bytes 3145732
  116.4 3.3 %copy-start.7 = (bf16[1024,512]{1,0:T(8,128)(2,1)S(1)}, bf16[1024,512]{1,0:T(8,128)(2,1)}, u32[]{:S(2)}) copy-start(bf16[1024,512]{1,0:T(8,128)(2,1)} %get-tuple-element.40) | copy-start | bytes 3145732
  116.4 3.3 %copy-start.8 = (bf16[1024,1024]{1,0:T(8,128)(2,1)S(1)}, bf16[1024,1024]{1,0:T(8,128)(2,1)}, u32[]{:S(2)}) copy-start(bf16[1024,1024]{1,0:T(8,128)(2,1)} %get-tuple-element.41) | copy-start | bytes 6291460
  124.4 2.7 %copy-start.5 = (bf16[1024,1024]{1,0:T(8,128)(2,1)S(1)}, bf16[1024,1024]{1,0:T(8,128)(2,1)}, u32[]{:S(2)}) copy-start(bf16[1024,1024]{1,0:T(8,128)(2,1)} %get-tuple-element.38) | copy-start | bytes 6291460
  127.1 2.3 copy-start.6
  185.6 4.0 %copy-start.9 = (bf16[1024,1024]{1,0:T(8,128)(2,1)S(1)}, bf16[1024,1024]{1,0:T(8,128)(2,1)}, u32[]{:S(2)}) copy-start(bf16[1024,1024]{1,0:T(8,128)(2,1)} %get-tuple-element.43) | copy-start | bytes 6291460
  189.5 2.4 copy-start.4
  192.0 2.3 copy-start.2
  251.6 7.4 %copy-start.1 = (bf16[16,1024]{1,0:T(8,128)(2,1)S(1)}, bf16[16,1024]{1,0:T(8,128)(2,1)}, u32[]{:S(2)}) copy-start(bf16[16,1024]{1,0:T(8,128)(2,1)} %get-tuple-element.78) | copy-start | bytes 98308
  251.6 8.0 %copy-start = (bf16[16,1024]{1,0:T(8,128)(2,1)S(1)}, bf16[16,1024]{1,0:T(8,128)(2,1)}, u32[]{:S(2)}) copy-start(bf16[16,1024]{1,0:T(8,128)(2,1)} %get-tuple-element.79) | copy-start | bytes 98308

commit v3 on v2

--- a/solution.py
+++ b/solution.py
@@ -56,22 +56,6 @@
     return at("zh") * 4 + at("zl"), at("x"), at("c"), at("y")
 
 
-def peers_near(with_y):
-    z, x, c, y = place()
-    peers = [dev_z((z + d) % 8) for d in range(1, 8)]
-    peers += [{"x": (x + 1) % 4}, {"x": (x + 3) % 4}, {"c": 1 - c}]
-    if with_y:
-        peers += [{"y": (y + 1) % 4}, {"y": (y + 3) % 4}]
-    return peers
-
-
-def greet(peers):
-    sem = pltpu.get_barrier_semaphore()
-    for p in peers:
-        pl.semaphore_signal(sem, inc=1, device_id=p, device_id_type=MESH)
-    pl.semaphore_wait(sem, len(peers))
-
-
 def flat_dev(t):
     return {"zh": t // 32, "zl": (t // 8) % 4, "x": (t // 2) % 4, "c": t % 2}
 
@@ -160,22 +144,29 @@
         self.left = self.move(blk(c, x), 8, {"x": (x + 3) % 4})
         self.cores = [self.move(blk(c, x), 11, {"c": 1 - c})]
 
-    def forward_x(self):
+    def right_in(self):
         z, x, c, _ = place()
         self.right.wait_recv()
         self.fr = self.move(blk(c, (x + 3) % 4, 64), 9, {"x": (x + 1) % 4})
+        self.cores.append(self.move(blk(c, (x + 3) % 4), 12, {"c": 1 - c}))
+
+    def left_in(self):
+        z, x, c, _ = place()
         self.left.wait_recv()
         self.fl = self.move(blk(c, (x + 1) % 4, 64, 64), 10, {"x": (x + 3) % 4})
-        self.cores.append(self.move(blk(c, (x + 3) % 4), 12, {"c": 1 - c}))
         self.cores.append(self.move(blk(c, (x + 1) % 4), 13, {"c": 1 - c}))
 
-    def finish(self):
+    def far_in(self):
         z, x, c, _ = place()
         self.fr.wait_recv()
         self.fl.wait_recv()
         self.cores.append(self.move(blk(c, (x + 2) % 4), 14, {"c": 1 - c}))
+
+    def cores_in(self):
         for cp in self.cores:
             cp.wait_recv()
+
+    def drain(self):
         for cp in self.zc + self.sent:
             cp.wait_send()
 
@@ -349,33 +340,31 @@
     def __init__(self, part, rows, bufs, ss, rs):
         self.part, self.rows, self.ss, self.rs = part, rows, ss, rs
         self.orv, self.nh, self.xin = bufs
+        y = at("y")
+        self.up, self.down = {"y": (y + 1) % 4}, {"y": (y + 3) % 4}
+        self.opp, self.plain, self.mixed = {}, [], []
 
     def copy(self, src, dst, k, dev):
         return rcopy(src, dst, self.ss.at[k], self.rs.at[k], dev)
 
-    def start(self):
+    def start(self, m):
         y = at("y")
-        self.up, self.down = {"y": (y + 1) % 4}, {"y": (y + 3) % 4}
         u, d, o = (y + 1) % 4, (y + 3) % 4, (y + 2) % 4
-        self.opp, self.plain, self.mixed = [], [], []
-        for m in range(2):
-            self.opp.append(self.copy(self.part[m].at[0, o], self.orv.at[m, 0], m, self.up))
-            self.opp.append(self.copy(self.part[m].at[1, o], self.orv.at[m, 1], 2 + m, self.down))
-        for m in range(2):
-            self.plain.append(self.copy(self.part[m].at[1, u], self.xin.at[m, 0, 1], 4 + m, self.up))
-            self.plain.append(self.copy(self.part[m].at[0, d], self.xin.at[m, 1, 0], 6 + m, self.down))
-
-    def middle(self):
+        self.opp[m, 0] = self.copy(self.part[m].at[0, o], self.orv.at[m, 0], m, self.up)
+        self.opp[m, 1] = self.copy(self.part[m].at[1, o], self.orv.at[m, 1], 2 + m, self.down)
+        self.plain.append(self.copy(self.part[m].at[1, u], self.xin.at[m, 0, 1], 4 + m, self.up))
+        self.plain.append(self.copy(self.part[m].at[0, d], self.xin.at[m, 1, 0], 6 + m, self.down))
+
+    def middle(self, m):
         y = at("y")
         u, d = (y + 1) % 4, (y + 3) % 4
-        for m in range(2):
-            for h, yy, dev in ((0, u, self.up), (1, d, self.down)):
-                self.opp[2 * m + h].wait_recv()
-                for s in range(0, self.rows, 32):
-                    self.nh[m, h, s : s + 32, :] = (
-                        self.part[m][h, yy, s : s + 32, :].astype(F32) + self.orv[m, h, s : s + 32, :].astype(F32)
-                    ).astype(BF)
-                self.mixed.append(self.copy(self.nh.at[m, h], self.xin.at[m, h, h], 8 + 2 * h + m, dev))
+        for h, yy, dev in ((0, u, self.up), (1, d, self.down)):
+            self.opp[m, h].wait_recv()
+            for s in range(0, self.rows, 32):
+                self.nh[m, h, s : s + 32, :] = (
+                    self.part[m][h, yy, s : s + 32, :].astype(F32) + self.orv[m, h, s : s + 32, :].astype(F32)
+                ).astype(BF)
+            self.mixed.append(self.copy(self.nh.at[m, h], self.xin.at[m, h, h], 8 + 2 * h + m, dev))
 
     def finish(self):
         for cp in self.plain + self.mixed:
@@ -389,7 +378,7 @@
         )
 
     def drain(self):
-        for cp in self.opp + self.plain + self.mixed:
+        for cp in list(self.opp.values()) + self.plain + self.mixed:
             cp.wait_send()
 
 
@@ -410,53 +399,6 @@
 
 def half(h):
     return pl.ds(pl.multiple_of(h * 512, 128), 512)
-
-
-def opening_kernel(
-    tokens, cot, gains, sbuf, t_in, t_out, normed_all, cot_all, w_in, w_out, pair, rbuf, normed, gs, gr, ws, wr, ys, yr, ps, pr
-):
-    z, x, c, y = place()
-    zh = at("zh")
-    f = tokens[...].astype(F32)
-    normed[...] = (f * inv_rms(f) * gains[0:1, :]).astype(BF)
-    greet_all()
-    exchange_start(sbuf, rbuf, ws, wr)
-    a = Gather(normed, normed_all, gs.at[0], gr.at[0])
-    b = Gather(cot, cot_all, gs.at[1], gr.at[1])
-    a.start_z()
-    b.start_z()
-    pairs = [
-        rcopy(t.at[:, :, half(1 - zh)], pair.at[m, zh], ps.at[m], pr.at[m], {"zh": 1 - zh})
-        for m, t in enumerate((t_in, t_out))
-    ]
-    for m, t in enumerate((t_in, t_out)):
-        pair[m, zh] = t[:, :, half(zh)]
-    exchange_wait(sbuf, rbuf, ws, wr)
-    for h in range(2):
-        def tile(q, _):
-            v = [rbuf[h * 32 + q * 4 + i].astype(F32) for i in range(4)]
-            rows = pl.ds(pl.multiple_of(q * 16, 16), 16)
-            w_in[h, y, rows, :] = jnp.concatenate([u[0:4] for u in v], axis=0).astype(BF)
-            w_out[h, y, rows, :] = jnp.concatenate([u[4:8] for u in v], axis=0).astype(BF)
-            return 0
-
-        lax.fori_loop(0, 8, tile, 0)
-    full = (w_in, w_out)
-    yg = YGather(lambda m, h: full[m].at[h, y], full, ys, yr)
-    yg.start()
-    a.start_x()
-    b.start_x()
-    a.forward_x()
-    yg.forward()
-    b.forward_x()
-    a.finish()
-    b.finish()
-    yg.finish()
-    for cp in pairs:
-        cp.wait_recv()
-        cp.wait_send()
-    yg.drain()
-    exchange_sent(sbuf, ws)
 
 
 VM = pl.BlockSpec(memory_space=pltpu.VMEM)
@@ -472,7 +414,7 @@
         in_specs=in_specs,
         out_specs=(VM,) * len(out_shape),
         scratch_shapes=scratch,
-        compiler_params=pltpu.CompilerParams(collective_id=ident, has_side_effects=True, vmem_limit_bytes=56 * 2**20),
+        compiler_params=pltpu.CompilerParams(collective_id=ident, has_side_effects=True, vmem_limit_bytes=67_043_328),
         cost_estimate=pl.CostEstimate(flops=40_000_000_000, bytes_accessed=2**23, transcendentals=0),
     )(*args)
 
@@ -481,189 +423,307 @@
     return jax.ShapeDtypeStruct(dims, kind)
 
 
-def opening(*args):
-    n = Gather.sems
-    out = (shape(1024, 1024), shape(1024, 1024), shape(2, 4, 128, 512), shape(2, 4, 128, 512), shape(2, 2, 3, 64, 512))
-    scratch = [
-        pltpu.VMEM((64, 8, 512), BF), pltpu.VMEM((16, 1024), BF),
-        DMA((2, n)), DMA((2, n)), DMA, DMA, DMA((12,)), DMA((12,)), DMA((2,)), DMA((2,)),
+def before_input(f, inv, gated, base):
+    return base + inv * gated - f * inv * inv * inv * jnp.mean(f * gated, axis=1, keepdims=True)
+
+
+def full(w):
+    return w[...].reshape(1024, 512)
+
+
+def mul(a, b, dims):
+    return lax.dot_general(a, b, (dims, ((), ())), preferred_element_type=F32)
+
+
+def up(rows, src, w_in, hid, act):
+    h = mul(src[rows, :], full(w_in), ((1,), (0,)))
+    hid[rows, :] = h
+    act[rows, :] = gelu_value(h).astype(BF)
+
+
+def down(rows, cot, w_out, hid, dh):
+    d = mul(cot[rows, :], full(w_out), ((1,), (0,)))
+    dh[rows, :] = (d * gelu_slope(hid[rows, :])).astype(BF)
+
+
+def back(rows, src, w, part):
+    part[rows, :] = mul(src[rows, :], full(w), ((1,), (1,))).astype(BF)
+
+
+def outer(left, right, store):
+    for i in range(4):
+        store(i, mul(left[:, i * 256 : (i + 1) * 256], right[...], ((0,), (0,))).astype(BF))
+
+
+def as_flat(ref):
+    def store(i, v):
+        ref[i // 2, (i % 2) * 2] = v[:128]
+        ref[i // 2, (i % 2) * 2 + 1] = v[128:]
+
+    return store
+
+
+def as_tiles(ref):
+    def store(i, v):
+        ref[i * 4 : (i + 1) * 4] = v.reshape(4, 64, 512)
+
+    return store
+
+
+def pick_tiles(owners, m, slots, w):
+    def tile(k, _):
+        want = slot_of(owners, m, k)
+        total = jnp.zeros((64, 512), BF)
+        for q in range(24):
+            r, s = q // 3, q % 3
+            total = total + slots[r // 4, r % 4, s * 64 : (s + 1) * 64, :] * ones_if(want == q)
+        w[k] = total
+        return 0
+
+    lax.fori_loop(0, 16, tile, 0)
+
+
+def place_tiles(owners, m, g, p):
+    dest = [slot_of(owners, m, k) for k in range(16)]
+
+    def slot(q, _):
+        row, s = q // 3, q % 3
+        total = jnp.zeros((64, 512), BF)
+        for k in range(16):
+            total = total + g[k] * ones_if(dest[k] == q)
+        p[row // 4, row % 4, pl.ds(pl.multiple_of(s * 64, 64), 64), :] = total
+        return 0
+
+    lax.fori_loop(0, 24, slot, 0)
+
+
+def scratch_of():
+    vm = pltpu.VMEM
+    tok, wt, act, f32 = vm((1024, 1024), BF), vm((2, 4, 128, 512), BF), vm((1024, 512), BF), vm((1024, 512), F32)
+    tiles, slots, flat = vm((16, 64, 512), BF), vm((2, 4, 192, 512), BF), vm((64, 8, 512), BF)
+    own, n, k = vm((16, 1024), BF), Gather.sems, Reduce.sems
+    named = dict(
+        normed_one=tok, normed_two=tok, cot_two=tok, cot_one=tok, part_a=tok, part_b=tok,
+        w_in_one=wt, w_out_one=wt, w_in_two=tiles, w_out_two=tiles, hid_one=f32, hid_two=f32, act_one=act, act_two=act, dh=act,
+        pair=vm((2, 2, 192, 512), BF), rbuf_w=flat, s_in=slots, s_out=slots, gt_in=tiles, gt_out=tiles, p_in=slots, p_out=slots,
+        gf_in=wt, gf_out=wt, sbuf_g=flat, tile_sum=vm((2, 2, 192, 512), BF), tile_got=vm((2, 192, 512), BF),
+        own_one=own, own_two=own, mid=own, grad_mid=own,
+        gs=DMA((4, n)), gr=DMA((4, n)), rs=DMA((4, k)), rr=DMA((4, k)), ys=DMA((4, 12)), yr=DMA((4, 12)),
+        ws=DMA((2,)), wr=DMA((2,)), ps=DMA((4,)), pr=DMA((4,)),
+    )
+    reduces = [Reduce.scratch() for _ in range(3)]
+    return named, reduces, YReduce.scratch(192), YReduce.scratch(128)
+
+
+class Bag:
+    pass
+
+
+def step_kernel(owners, tokens, cot, gains, sbuf, t_in, t_out, hidden_out, grad_tokens, rbuf, tile_grad, *scratch):
+    named, reduces, tile_y, flat_y = scratch_of()
+    v, refs = Bag(), list(scratch)
+    for name in named:
+        setattr(v, name, refs.pop(0))
+    bufs = []
+    for r in reduces:
+        bufs.append(refs[: len(r)])
+        refs = refs[len(r) :]
+    tile_bufs, flat_bufs = refs[:3], refs[3:]
+    z, x, c, y = place()
+    zh = at("zh")
+    near = [blk(c, (x + d) % 4) for d in (0, 3, 1, 2)]
+    far = [blk(1 - c, 0, 256), blk(1 - c, 2, 256)]
+
+    f = tokens[...].astype(F32)
+    v.own_one[...] = (f * inv_rms(f) * gains[0:1, :]).astype(BF)
+    greet_all()
+    exchange_start(sbuf, v.rbuf_w, v.ws.at[0], v.wr.at[0])
+    a = Gather(v.own_one, v.normed_one, v.gs.at[0], v.gr.at[0])
+    b = Gather(cot, v.cot_two, v.gs.at[1], v.gr.at[1])
+    a.start_z()
+    b.start_z()
+    pairs = [
+        rcopy(t.at[:, half(1 - zh)], v.pair.at[m, zh], v.ps.at[m], v.pr.at[m], {"zh": 1 - zh})
+        for m, t in enumerate((t_in, t_out))
     ]
-    return comm_call(opening_kernel, "opening", 0, out, scratch, [VM] * 6, args)
-
-
-def turn_one_kernel(owners, part, tokens, gains, pair, new, full, w_in, w_out, s_in, s_out, *scratch):
-    n = len(Reduce.scratch())
-    bufs, (own, gs, gr, rs, rr, ys, yr) = scratch[:n], scratch[n:]
-    y = at("y")
-    slots = (s_in, s_out)
-    greet(peers_near(True))
-    r = Reduce(part, bufs, rs, rr)
+    for m, t in enumerate((t_in, t_out)):
+        v.pair[m, zh] = t[:, half(zh)]
+    exchange_wait(sbuf, v.rbuf_w, v.ws.at[0], v.wr.at[0])
+    for h in range(2):
+        def tile(q, _):
+            got = [v.rbuf_w[h * 32 + q * 4 + i].astype(F32) for i in range(4)]
+            rows = pl.ds(pl.multiple_of(q * 16, 16), 16)
+            v.w_in_one[h, y, rows, :] = jnp.concatenate([u[0:4] for u in got], axis=0).astype(BF)
+            v.w_out_one[h, y, rows, :] = jnp.concatenate([u[4:8] for u in got], axis=0).astype(BF)
+            return 0
+
+        lax.fori_loop(0, 8, tile, 0)
+    ones = (v.w_in_one, v.w_out_one)
+    yg = YGather(lambda m, h: ones[m].at[h, y], ones, v.ys.at[0], v.yr.at[0])
+    yg.start()
+    a.start_x()
+    a.right_in()
+    a.left_in()
+    yg.forward()
+    a.far_in()
+    b.start_x()
+    a.cores_in()
+    yg.finish()
+
+    for rows in far:
+        up(rows, v.normed_one, v.w_in_one, v.hid_one, v.act_one)
+        back(rows, v.act_one, v.w_out_one, v.part_a)
+    r = Reduce(v.part_a, bufs[0], v.rs.at[0], v.rr.at[0])
     r.start_c()
-    yg = YGather(lambda m, h: pair.at[m, h], slots, ys, yr)
-    yg.start()
+    slots = (v.s_in, v.s_out)
+    for cp in pairs:
+        cp.wait_recv()
+    yt = YGather(lambda m, h: v.pair.at[m, h], slots, v.ys.at[1], v.yr.at[1])
+    yt.start()
+    for i in range(2):
+        rows = blk(c, 2 * i, 256)
+        up(rows, v.normed_one, v.w_in_one, v.hid_one, v.act_one)
+        back(rows, v.act_one, v.w_out_one, v.part_a)
     r.start_opposite()
     r.start_near()
+    b.right_in()
+    b.left_in()
     for m in range(2):
         for h in range(2):
-            slots[m][h, y] = pair[m, h]
+            slots[m][h, y] = v.pair[m, h]
     r.finish_near()
-    yg.forward()
     r.start_z()
-    total = r.total()
-    mid = (tokens[...].astype(F32) + total).astype(BF)
-    f = mid.astype(F32)
-    own[...] = (f * inv_rms(f) * gains[1:2, :]).astype(BF)
-    new[...] = mid
-    g = Gather(own, full, gs, gr)
-    g.start_z()
+    b.far_in()
+    yt.forward()
+    v.mid[...] = (tokens[...].astype(F32) + r.total()).astype(BF)
+    f = v.mid[...].astype(F32)
+    v.own_two[...] = (f * inv_rms(f) * gains[1:2, :]).astype(BF)
+    a2 = Gather(v.own_two, v.normed_two, v.gs.at[2], v.gr.at[2])
+    a2.start_z()
     r.drain()
-    g.start_x()
-    yg.finish()
-    for m, w in enumerate((w_in, w_out)):
-        def tile(k, _, m=m, w=w):
-            want = slot_of(owners, m, k)
-            total = jnp.zeros((64, 512), BF)
-            for q in range(24):
-                r, s = q // 3, q % 3
-                total = total + slots[m][r // 4, r % 4, s * 64 : (s + 1) * 64, :] * ones_if(want == q)
-            w[pl.ds(pl.multiple_of(k * 64, 64), 64), :] = total
-            return 0
-
-        lax.fori_loop(0, 16, tile, 0)
-    g.forward_x()
-    g.finish()
-    yg.drain()
-
-
-def turn_one(*args):
-    out = (shape(16, 1024), shape(1024, 1024), shape(1024, 512), shape(1024, 512))
-    scratch = [pltpu.VMEM((2, 4, 192, 512), BF)] * 2 + Reduce.scratch() + [
-        pltpu.VMEM((16, 1024), BF), DMA((Gather.sems,)), DMA((Gather.sems,)), DMA((Reduce.sems,)), DMA((Reduce.sems,)),
-        DMA((12,)), DMA((12,)),
-    ]
-    return comm_call(turn_one_kernel, "turn_one", 1, out, scratch, [SM] + [VM] * 4, args)
-
-
-def before_input(f, inv, gated, base):
-    return base + inv * gated - f * inv * inv * inv * jnp.mean(f * gated, axis=1, keepdims=True)
-
-
-def turn_two_kernel(owners, part, cot, mid, gains, g_in, g_out, new, full, tile_sum, p_in, p_out, *scratch):
-    n = len(Reduce.scratch())
-    bufs, ybufs, (gs, gr, rs, rr, ys, yr) = scratch[:n], scratch[n : n + 3], scratch[n + 3 :]
-    z, x, c, y = place()
-    greet(peers_near(True))
-    r = Reduce(part, bufs, rs, rr)
+    yt.finish()
+    for m, w in enumerate((v.w_in_two, v.w_out_two)):
+        pick_tiles(owners, m, slots[m], w)
+    a2.start_x()
+    b.cores_in()
+
+    def layer_two(rows):
+        up(rows, v.normed_two, v.w_in_two, v.hid_two, v.act_two)
+        down(rows, v.cot_two, v.w_out_two, v.hid_two, v.dh)
+        back(rows, v.dh, v.w_in_two, v.part_a)
+
+    layer_two(near[0])
+    a2.right_in()
+    layer_two(near[1])
+    a2.left_in()
+    layer_two(near[2])
+    a2.far_in()
+    layer_two(near[3])
+    a2.cores_in()
+    for rows in far:
+        layer_two(rows)
+    r = Reduce(v.part_a, bufs[1], v.rs.at[1], v.rr.at[1])
     r.start_c()
     r.start_opposite()
     r.start_near()
-    parts = (p_in, p_out)
-    for m, g in enumerate((g_in, g_out)):
-        dest = [slot_of(owners, m, k) for k in range(16)]
-
-        def slot(q, _, g=g, p=parts[m], dest=dest):
-            row, s = q // 3, q % 3
-            total = jnp.zeros((64, 512), BF)
-            for k in range(16):
-                total = total + g[k] * ones_if(dest[k] == q)
-            p[row // 4, row % 4, pl.ds(pl.multiple_of(s * 64, 64), 64), :] = total
-            return 0
-
-        lax.fori_loop(0, 24, slot, 0)
-    yr_ = YReduce(parts, 192, ybufs, ys, yr)
-    yr_.start()
+    outer(v.normed_two, v.dh, as_tiles(v.gt_in))
+    r.finish_near()
+    outer(v.cot_two, v.act_two, as_tiles(v.gt_out))
+    r.start_z()
+    ty = YReduce((v.p_in, v.p_out), 192, tile_bufs, v.ys.at[2], v.yr.at[2])
+    for m, (g, p) in enumerate(((v.gt_in, v.p_in), (v.gt_out, v.p_out))):
+        place_tiles(owners, m, g, p)
+        ty.start(m)
+    f = v.mid[...].astype(F32)
+    v.grad_mid[...] = before_input(f, inv_rms(f), r.total() * gains[1:2, :], cot[...].astype(F32)).astype(BF)
+    b2 = Gather(v.grad_mid, v.cot_one, v.gs.at[3], v.gr.at[3])
+    b2.start_z()
+    r.drain()
+    for i in range(4):
+        back(pl.ds(i * 256, 256), v.act_two, v.w_out_two, v.part_b)
+    s = Reduce(v.part_b, bufs[2], v.rs.at[2], v.rr.at[2])
+    s.start_c()
+    b2.start_x()
+    s.start_opposite()
+    s.start_near()
+
+    def layer_one(rows):
+        down(rows, v.cot_one, v.w_out_one, v.hid_one, v.dh)
+        back(rows, v.dh, v.w_in_one, v.part_a)
+
+    layer_one(near[0])
+    b2.right_in()
+    layer_one(near[1])
+    b2.left_in()
+    layer_one(near[2])
+    for m in range(2):
+        ty.middle(m)
+    b2.far_in()
+    layer_one(near[3])
+    b2.cores_in()
+    fy = YReduce((v.gf_in, v.gf_out), 128, flat_bufs, v.ys.at[3], v.yr.at[3])
+    outer(v.cot_one, v.act_one, as_flat(v.gf_out))
+    fy.start(1)
+    for rows in far:
+        down(rows, v.cot_one, v.w_out_one, v.hid_one, v.dh)
+    outer(v.normed_one, v.dh, as_flat(v.gf_in))
+    fy.start(0)
+    for rows in far:
+        back(rows, v.dh, v.w_in_one, v.part_a)
+    r = Reduce(v.part_a, bufs[0], v.rs.at[3], v.rr.at[3])
+    r.start_c()
+    s.finish_near()
+    r.start_opposite()
+    r.start_near()
+    ty.finish()
+    for m in range(2):
+        for h in range(2):
+            for k in range(0, 192, 32):
+                rows = pl.ds(k, 32)
+                v.tile_sum[m, h, rows, :] = ty.total(m, h, rows).astype(BF)
+    swaps = [
+        rcopy(v.tile_sum.at[m, 1 - zh], v.tile_got.at[m], v.ps.at[2 + m], v.pr.at[2 + m], {"zh": 1 - zh})
+        for m in range(2)
+    ]
+    fy.middle(1)
+    fy.middle(0)
+    s.start_z()
     r.finish_near()
     r.start_z()
-    total = r.total()
-    f = mid[...].astype(F32)
-    new[...] = before_input(f, inv_rms(f), total * gains[1:2, :], cot[...].astype(F32)).astype(BF)
-    g = Gather(new, full, gs, gr)
-    g.start_z()
-    yr_.middle()
-    r.drain()
-    g.start_x()
-    g.forward_x()
-    yr_.finish()
-    for m in range(2):
-        for h in range(2):
-            for s in range(0, 192, 32):
-                rows = pl.ds(s, 32)
-                tile_sum[m, h, rows, :] = yr_.total(m, h, rows).astype(BF)
-    g.finish()
-    yr_.drain()
-
-
-def turn_two(*args):
-    out = (shape(16, 1024), shape(1024, 1024), shape(2, 2, 192, 512))
-    scratch = [pltpu.VMEM((2, 4, 192, 512), BF)] * 2 + Reduce.scratch() + YReduce.scratch(192) + [
-        DMA((Gather.sems,)), DMA((Gather.sems,)), DMA((Reduce.sems,)), DMA((Reduce.sems,)), DMA((12,)), DMA((12,)),
-    ]
-    return comm_call(turn_two_kernel, "turn_two", 2, out, scratch, [SM] + [VM] * 6, args)
-
-
-def closing_kernel(
-    part_two, part_one, g_in, g_out, tokens, mid, grad_mid, gains, tile_sum,
-    hidden_out, grad_tokens, rbuf, tile_grad, sbuf, tile_got, *scratch,
-):
-    n = len(Reduce.scratch())
-    bufs_a, bufs_b, ybufs = scratch[:n], scratch[n : 2 * n], scratch[2 * n : 2 * n + 3]
-    rs, rr, ys, yr, ws, wr, ps, pr = scratch[2 * n + 3 :]
-    zh = at("zh")
-    greet_all()
-    red = YReduce((g_in, g_out), 128, ybufs, ys, yr)
-    red.start()
-    a = Reduce(part_one, bufs_a, rs.at[0], rr.at[0])
-    b = Reduce(part_two, bufs_b, rs.at[1], rr.at[1])
-    for r in (a, b):
-        r.start_c()
-    pairs = [
-        rcopy(tile_sum.at[m, 1 - zh], tile_got.at[m], ps.at[m], pr.at[m], {"zh": 1 - zh}) for m in range(2)
-    ]
-    for r in (a, b):
-        r.start_opposite()
-    for r in (a, b):
-        r.start_near()
-    red.middle()
-    for r in (a, b):
-        r.finish_near()
-    for r in (a, b):
-        r.start_z()
-    red.finish()
+    fy.finish()
     for h in range(2):
         def tile(q, _):
             rows = pl.ds(pl.multiple_of(q * 16, 16), 16)
-            t = [red.total(m, h, rows) for m in range(2)]
+            t = [fy.total(m, h, rows) for m in range(2)]
             for i in range(4):
-                sbuf[h * 32 + q * 4 + i] = jnp.concatenate(
+                v.sbuf_g[h * 32 + q * 4 + i] = jnp.concatenate(
                     [t[0][4 * i : 4 * i + 4], t[1][4 * i : 4 * i + 4]], axis=0
                 ).astype(BF)
             return 0
 
         lax.fori_loop(0, 8, tile, 0)
-    exchange_start(sbuf, rbuf, ws, wr)
-    for m, cp in enumerate(pairs):
+    exchange_start(v.sbuf_g, rbuf, v.ws.at[1], v.wr.at[1])
+    for m, cp in enumerate(swaps):
         cp.wait_recv()
-        tile_grad[m, :, half(zh)] = tile_sum[m, zh]
-        tile_grad[m, :, half(1 - zh)] = tile_got[m]
+        tile_grad[m, :, half(zh)] = v.tile_sum[m, zh]
+        tile_grad[m, :, half(1 - zh)] = v.tile_got[m]
+    hidden_out[...] = (v.mid[...].astype(F32) + s.total()).astype(BF)
     f = tokens[...].astype(F32)
-    grad_tokens[...] = before_input(f, inv_rms(f), a.total() * gains[0:1, :], grad_mid[...].astype(F32)).astype(BF)
-    hidden_out[...] = (mid[...].astype(F32) + b.total()).astype(BF)
-    exchange_wait(sbuf, rbuf, ws, wr)
-    exchange_sent(sbuf, ws)
-    a.drain()
-    b.drain()
-    red.drain()
-    for cp in pairs:
+    grad_tokens[...] = before_input(f, inv_rms(f), r.total() * gains[0:1, :], v.grad_mid[...].astype(F32)).astype(BF)
+    exchange_wait(v.sbuf_g, rbuf, v.ws.at[1], v.wr.at[1])
+    exchange_sent(v.sbuf_g, v.ws.at[1])
+    exchange_sent(sbuf, v.ws.at[0])
+    for cp in pairs + swaps:
         cp.wait_send()
-
-
-def closing(*args):
+    for q in (a, b, a2, b2, yg, yt, ty, fy, r, s):
+        q.drain()
+
+
+def step(*args):
+    named, reduces, tile_y, flat_y = scratch_of()
     out = (shape(16, 1024), shape(16, 1024), shape(64, 8, 512), shape(2, 192, 1024))
-    scratch = [pltpu.VMEM((64, 8, 512), BF), pltpu.VMEM((2, 192, 512), BF)]
-    scratch += Reduce.scratch() * 2 + YReduce.scratch(128) + [
-        DMA((2, Reduce.sems)), DMA((2, Reduce.sems)), DMA((12,)), DMA((12,)), DMA, DMA, DMA((2,)), DMA((2,)),
-    ]
-    return comm_call(closing_kernel, "closing", 3, out, scratch, [VM] * 9, args)
+    scratch = list(named.values()) + sum(reduces, []) + tile_y + flat_y
+    return comm_call(step_kernel, "step", 0, out, scratch, [SM] + [VM] * 6, args)
 
 
 def adam_kernel(
@@ -723,10 +783,6 @@
     )(*args)
 
 
-def dot(a, b, dims, kind=F32):
-    return lax.dot_general(a, b, (dims, ((), ())), preferred_element_type=F32).astype(kind)
-
-
 def shards(
     tokens, grad_out, gains, flat_in, flat_out, flat_moment, flat_second,
     tile_in, tile_out, tile_moment, tile_second, owners,
@@ -734,33 +790,10 @@
     own = owners[:, 0, :]
     flat = jnp.stack([flat_in.reshape(4, 32, 2, 512), flat_out.reshape(4, 32, 2, 512)])
     sbuf = flat.transpose(3, 2, 0, 1, 4).reshape(64, 8, 512)
-    normed_one, cot_two, w_in_one, w_out_one, pair = opening(tokens, grad_out, gains, sbuf, tile_in[0], tile_out[0])
-    w_in_one, w_out_one = w_in_one.reshape(1024, 512), w_out_one.reshape(1024, 512)
-
-    hidden_one = dot(normed_one, w_in_one, ((1,), (0,)))
-    act_one = gelu_value(hidden_one).astype(BF)
-    part = dot(act_one, w_out_one, ((1,), (1,)), BF)
-    middle, normed_two, w_in_two, w_out_two = turn_one(own, part, tokens, gains, pair.reshape(2, 2, 192, 512))
-
-    hidden_two = dot(normed_two, w_in_two, ((1,), (0,)))
-    act_two = gelu_value(hidden_two).astype(BF)
-    d_act_two = dot(cot_two, w_out_two, ((1,), (0,)))
-    d_hidden_two = (d_act_two * gelu_slope(hidden_two)).astype(BF)
-    part = dot(d_hidden_two, w_in_two, ((1,), (1,)), BF)
-    grad_in_two = dot(normed_two, d_hidden_two, ((0,), (0,)), BF).reshape(16, 64, 512)
-    grad_out_two = dot(cot_two, act_two, ((0,), (0,)), BF).reshape(16, 64, 512)
-    grad_mid, cot_one, tile_sum = turn_two(own, part, grad_out, middle, gains, grad_in_two, grad_out_two)
-    part_two = dot(act_two, w_out_two, ((1,), (1,)), BF)
-
-    d_act_one = dot(cot_one, w_out_one, ((1,), (0,)))
-    d_hidden_one = (d_act_one * gelu_slope(hidden_one)).astype(BF)
-    part = dot(d_hidden_one, w_in_one, ((1,), (1,)), BF)
-    grad_in_one = dot(normed_one, d_hidden_one, ((0,), (0,)), BF).reshape(2, 4, 128, 512)
-    grad_out_one = dot(cot_one, act_one, ((0,), (0,)), BF).reshape(2, 4, 128, 512)
-    hidden_out, grad_tokens, rbuf, tile_grad = closing(
-        part_two, part, grad_in_one, grad_out_one, tokens, middle, grad_mid, gains, tile_sum
+    tile, tiles = (192, 1024), (2, 192, 1024)
+    hidden_out, grad_tokens, rbuf, tile_grad = step(
+        own, tokens, grad_out, gains, sbuf, tile_in.reshape(tile), tile_out.reshape(tile)
     )
-    tile, tiles = (192, 1024), (2, 192, 1024)
     outs = adam(
         own, rbuf, tile_grad, flat_in, flat_out, flat_moment, flat_second,
         tile_in.reshape(tile), tile_out.reshape(tile), tile_moment.reshape(tiles), tile_second.reshape(tiles),

time: 263 us -> 218 us (0.83)
  matrix products: 32.7 us -> 0 us
  Pallas kernels: 222 us -> 211 us
    dot_general x12 -> x0, matrix products: 32.7 us -> none  [dot(): lax.dot_general(a, b, (dims, ((), ())), preferred_element_type=F32)]
    pallas_call x4 -> x1, Pallas kernels: 214 us -> 204 us  [comm_call(): pl.pallas_call(kernel, name=name, out_shape=out_shape, in_specs=in_specs,...]
where the time goes in v3:
time: 218 us; the launch traced here: 217 us
  Pallas kernels  211 us (97%)
  local copies, waits for them, and re-layouts  4.87 us (2%)
    pallas_call x1, Pallas kernels, comm_call(): pl.pallas_call(kernel, name=name, out_shape=out_shape, in_specs=in_specs,...  204 us
    pallas_call x1, Pallas kernels, adam(): pl.pallas_call(adam_kernel, name='adam', grid=(4,), out_shape=(shape(128,...  7.38 us

profile of v3, /device:TPU:65, one launch (start us, length us, event | category | flops | bytes accessed | tf_op | source)
XLA Modules:
  0.0 217.4 jit_solution(1517444702322306189)
XLA Ops:
  0.6 1.2 stack_reshape.6
  1.8 0.2 copy.22
  2.0 1.2 stack_reshape.7
  3.2 0.2 copy.23
  3.4 0.3 maximum_bitcast_fusion
  3.7 0.9 reshape.49.sbuf
  4.6 204.1 %step.1 = (bf16[16,1024]{1,0:T(8,128)(2,1)}, bf16[16,1024]{1,0:T(8,128)(2,1)}, bf16[64,8,512]{2,1,0:T(8,128)(2,1)}, bf16[2,192,1024]{2,1,0:T(8,128)(2,1)}) custom-call(s32[2,16]{1,0:T(2,128)} %bitcast.21, bf16[16,1024]{1,0:T(8,128)(2,1)} %tokens.1, bf16[16,1024]{1,0:T(8,128)(2,1)} %cot.1, f32[2,1024]{1,0:T(2,128)} %gains.1, ...), custom_call_target="tpu_custom_call" | custom-call | flops 40000000000 | bytes 8388608 | tf_op jit(solution)/shard_map/step/pallas_call | solution.py:410
  208.8 0.0 copy-start.1
  208.8 0.0 copy-start
  208.8 7.4 %adam.1 = (bf16[128,1024]{1,0:T(8,128)(2,1)}, bf16[128,1024]{1,0:T(8,128)(2,1)}, f32[2,128,1024]{2,1,0:T(8,128)}, f32[2,128,1024]{2,1,0:T(8,128)}, bf16[192,1024...) custom-call(s32[2,16]{1,0:T(2,128)} %bitcast.22, ...), custom_call_target="tpu_custom_call" | custom-call | flops 4000000000 | bytes 13631488 | tf_op jit(solution)/shard_map/adam/pallas_call | solution.py:771
  216.2 0.0 copy-done.1
  216.2 0.6 copy.28
  216.8 0.0 copy-done
  216.8 0.6 copy.29
Async XLA Ops:
  208.8 7.4 %copy-start.1 = (bf16[16,1024]{1,0:T(8,128)(2,1)S(1)}, bf16[16,1024]{1,0:T(8,128)(2,1)}, u32[]{:S(2)}) copy-start(bf16[16,1024]{1,0:T(8,128)(2,1)} %get-tuple-element.54) | copy-start | bytes 98308
  208.8 8.0 %copy-start = (bf16[16,1024]{1,0:T(8,128)(2,1)S(1)}, bf16[16,1024]{1,0:T(8,128)(2,1)}, u32[]{:S(2)}) copy-start(bf16[16,1024]{1,0:T(8,128)(2,1)} %get-tuple-element.55) | copy-start | bytes 98308

commit v4 on v3

--- a/solution.py
+++ b/solution.py
@@ -65,7 +65,7 @@
     return z * 8 + x * 2 + c
 
 
-def greet_all():
+def greet_all(meanwhile):
     me = my_flat()
     y = at("y")
     sem = pltpu.get_barrier_semaphore()
@@ -77,6 +77,7 @@
     lax.fori_loop(1, 64, one, 0)
     for d in (1, 3):
         pl.semaphore_signal(sem, inc=1, device_id={"y": (y + d) % 4}, device_id_type=MESH)
+    meanwhile()
     pl.semaphore_wait(sem, 65)
 
 
@@ -114,60 +115,72 @@
     return pl.ds(pl.multiple_of(c * 512 + x * 128 + off, 16), n)
 
 
+PIECES = (0, 1, 7, 2, 6, 3, 5, 4)
+
+
 class Gather:
-    sems = 7 + 2 + 2 + 4
+    sems = 7 + 16 + 8 + 4
 
     def __init__(self, own, full, ss, rs):
         self.own, self.full, self.ss, self.rs = own, full, ss, rs
-
-    def start_z(self):
-        z, x, c, _ = place()
-        mine = blk(c, x, 16, z * 16)
-        self.sent = []
-        self.zc = [
-            rcopy(self.own, self.full.at[mine], self.ss.at[d - 1], self.rs.at[d - 1], dev_z((z + d) % 8))
-            for d in range(1, 8)
-        ]
-        self.full[mine, :] = self.own[...]
-
-    def move(self, rows, k, dev):
-        ref = self.full.at[rows]
-        cp = rcopy(ref, ref, self.ss.at[k], self.rs.at[k], dev)
+        z, x, c, _ = place()
+        self.right_dev, self.left_dev, self.core_dev = {"x": (x + 1) % 4}, {"x": (x + 3) % 4}, {"c": 1 - c}
+        self.sent, self.right, self.left, self.far, self.cores = [], [], [], [], []
+
+    def piece(self, xx, d):
+        z, x, c, _ = place()
+        return blk(c, xx, 16, (z + 8 - d) % 8 * 16)
+
+    def send(self, src, rows, k, dev):
+        cp = rcopy(src, self.full.at[rows], self.ss.at[k], self.rs.at[k], dev)
         self.sent.append(cp)
         return cp
 
+    def pass_on(self, rows, k, dev):
+        return self.send(self.full.at[rows], rows, k, dev)
+
+    def start_z(self):
+        z, x, c, _ = place()
+        mine = self.piece(x, 0)
+        self.zc = {d: self.send(self.own, mine, d - 1, dev_z((z + d) % 8)) for d in PIECES[1:]}
+        self.right.append(self.send(self.own, mine, 7, self.right_dev))
+        self.left.append(self.send(self.own, mine, 15, self.left_dev))
+        self.full[mine, :] = self.own[...]
+
     def start_x(self):
         z, x, c, _ = place()
-        for cp in self.zc:
+        for k in range(1, 8):
+            d = PIECES[k]
+            self.zc[d].wait_recv()
+            self.right.append(self.pass_on(self.piece(x, d), 7 + k, self.right_dev))
+            self.left.append(self.pass_on(self.piece(x, d), 15 + k, self.left_dev))
+        self.cores.append(self.pass_on(blk(c, x), 31, self.core_dev))
+
+    def sides_in(self):
+        z, x, c, _ = place()
+        for k in range(8):
+            d = PIECES[k]
+            self.right[k].wait_recv()
+            if k % 2 == 0:
+                self.far.append(self.pass_on(self.piece((x + 3) % 4, d), 23 + k, self.right_dev))
+            self.left[k].wait_recv()
+            if k % 2 == 1:
+                self.far.append(self.pass_on(self.piece((x + 1) % 4, d), 23 + k, self.left_dev))
+        self.cores.append(self.pass_on(blk(c, (x + 3) % 4), 32, self.core_dev))
+        self.cores.append(self.pass_on(blk(c, (x + 1) % 4), 33, self.core_dev))
+
+    def far_in(self):
+        z, x, c, _ = place()
+        for cp in self.far:
             cp.wait_recv()
-        self.right = self.move(blk(c, x), 7, {"x": (x + 1) % 4})
-        self.left = self.move(blk(c, x), 8, {"x": (x + 3) % 4})
-        self.cores = [self.move(blk(c, x), 11, {"c": 1 - c})]
-
-    def right_in(self):
-        z, x, c, _ = place()
-        self.right.wait_recv()
-        self.fr = self.move(blk(c, (x + 3) % 4, 64), 9, {"x": (x + 1) % 4})
-        self.cores.append(self.move(blk(c, (x + 3) % 4), 12, {"c": 1 - c}))
-
-    def left_in(self):
-        z, x, c, _ = place()
-        self.left.wait_recv()
-        self.fl = self.move(blk(c, (x + 1) % 4, 64, 64), 10, {"x": (x + 3) % 4})
-        self.cores.append(self.move(blk(c, (x + 1) % 4), 13, {"c": 1 - c}))
-
-    def far_in(self):
-        z, x, c, _ = place()
-        self.fr.wait_recv()
-        self.fl.wait_recv()
-        self.cores.append(self.move(blk(c, (x + 2) % 4), 14, {"c": 1 - c}))
+        self.cores.append(self.pass_on(blk(c, (x + 2) % 4), 34, self.core_dev))
 
     def cores_in(self):
         for cp in self.cores:
             cp.wait_recv()
 
     def drain(self):
-        for cp in self.zc + self.sent:
+        for cp in self.sent:
             cp.wait_send()
 
 
@@ -505,7 +518,7 @@
     named = dict(
         normed_one=tok, normed_two=tok, cot_two=tok, cot_one=tok, part_a=tok, part_b=tok,
         w_in_one=wt, w_out_one=wt, w_in_two=tiles, w_out_two=tiles, hid_one=f32, hid_two=f32, act_one=act, act_two=act, dh=act,
-        pair=vm((2, 2, 192, 512), BF), rbuf_w=flat, s_in=slots, s_out=slots, gt_in=tiles, gt_out=tiles, p_in=slots, p_out=slots,
+        pair=vm((2, 2, 192, 512), BF), rbuf_w=flat, sbuf_w=flat, wide=vm((4, 512, 128), F32), s_in=slots, s_out=slots, gt_in=tiles, gt_out=tiles, p_in=slots, p_out=slots,
         gf_in=wt, gf_out=wt, sbuf_g=flat, tile_sum=vm((2, 2, 192, 512), BF), tile_got=vm((2, 192, 512), BF),
         own_one=own, own_two=own, mid=own, grad_mid=own,
         gs=DMA((4, n)), gr=DMA((4, n)), rs=DMA((4, k)), rr=DMA((4, k)), ys=DMA((4, 12)), yr=DMA((4, 12)),
@@ -519,7 +532,7 @@
     pass
 
 
-def step_kernel(owners, tokens, cot, gains, sbuf, t_in, t_out, hidden_out, grad_tokens, rbuf, tile_grad, *scratch):
+def step_kernel(owners, tokens, cot, gains, f_in, f_out, t_in, t_out, hidden_out, grad_tokens, rbuf, tile_grad, *scratch):
     named, reduces, tile_y, flat_y = scratch_of()
     v, refs = Bag(), list(scratch)
     for name in named:
@@ -534,18 +547,24 @@
     near = [blk(c, (x + d) % 4) for d in (0, 3, 1, 2)]
     far = [blk(1 - c, 0, 256), blk(1 - c, 2, 256)]
 
-    f = tokens[...].astype(F32)
-    v.own_one[...] = (f * inv_rms(f) * gains[0:1, :]).astype(BF)
-    greet_all()
+    def prepare():
+        f = tokens[...].astype(F32)
+        v.own_one[...] = (f * inv_rms(f) * gains[0:1, :]).astype(BF)
+        for m, flat in enumerate((f_in, f_out)):
+            for h in range(2):
+                for d in range(4):
+                    for q in range(4):
+                        cols = slice(h * 512 + q * 128, h * 512 + q * 128 + 128)
+                        v.wide[q, pl.ds(h * 256 + m * 4 + d, 32, stride=8), :] = flat[d * 32 : (d + 1) * 32, cols].astype(F32)
+        for q in range(4):
+            sbuf[:, :, q * 128 : (q + 1) * 128] = v.wide[q].reshape(64, 8, 128).astype(BF)
+
+    sbuf = v.sbuf_w
+    greet_all(prepare)
     exchange_start(sbuf, v.rbuf_w, v.ws.at[0], v.wr.at[0])
     a = Gather(v.own_one, v.normed_one, v.gs.at[0], v.gr.at[0])
     b = Gather(cot, v.cot_two, v.gs.at[1], v.gr.at[1])
     a.start_z()
-    b.start_z()
-    pairs = [
-        rcopy(t.at[:, half(1 - zh)], v.pair.at[m, zh], v.ps.at[m], v.pr.at[m], {"zh": 1 - zh})
-        for m, t in enumerate((t_in, t_out))
-    ]
     for m, t in enumerate((t_in, t_out)):
         v.pair[m, zh] = t[:, half(zh)]
     exchange_wait(sbuf, v.rbuf_w, v.ws.at[0], v.wr.at[0])
@@ -562,11 +581,14 @@
     yg = YGather(lambda m, h: ones[m].at[h, y], ones, v.ys.at[0], v.yr.at[0])
     yg.start()
     a.start_x()
-    a.right_in()
-    a.left_in()
+    pairs = [
+        rcopy(t.at[:, half(1 - zh)], v.pair.at[m, zh], v.ps.at[m], v.pr.at[m], {"zh": 1 - zh})
+        for m, t in enumerate((t_in, t_out))
+    ]
+    b.start_z()
     yg.forward()
+    a.sides_in()
     a.far_in()
-    b.start_x()
     a.cores_in()
     yg.finish()
 
@@ -575,36 +597,37 @@
         back(rows, v.act_one, v.w_out_one, v.part_a)
     r = Reduce(v.part_a, bufs[0], v.rs.at[0], v.rr.at[0])
     r.start_c()
-    slots = (v.s_in, v.s_out)
-    for cp in pairs:
-        cp.wait_recv()
-    yt = YGather(lambda m, h: v.pair.at[m, h], slots, v.ys.at[1], v.yr.at[1])
-    yt.start()
     for i in range(2):
         rows = blk(c, 2 * i, 256)
         up(rows, v.normed_one, v.w_in_one, v.hid_one, v.act_one)
         back(rows, v.act_one, v.w_out_one, v.part_a)
     r.start_opposite()
     r.start_near()
-    b.right_in()
-    b.left_in()
+    slots = (v.s_in, v.s_out)
+    for cp in pairs:
+        cp.wait_recv()
+    yt = YGather(lambda m, h: v.pair.at[m, h], slots, v.ys.at[1], v.yr.at[1])
+    yt.start()
     for m in range(2):
         for h in range(2):
             slots[m][h, y] = v.pair[m, h]
     r.finish_near()
+    b.start_x()
     r.start_z()
-    b.far_in()
     yt.forward()
+    b.sides_in()
     v.mid[...] = (tokens[...].astype(F32) + r.total()).astype(BF)
     f = v.mid[...].astype(F32)
     v.own_two[...] = (f * inv_rms(f) * gains[1:2, :]).astype(BF)
     a2 = Gather(v.own_two, v.normed_two, v.gs.at[2], v.gr.at[2])
     a2.start_z()
     r.drain()
+    b.far_in()
+    a2.start_x()
     yt.finish()
-    for m, w in enumerate((v.w_in_two, v.w_out_two)):
-        pick_tiles(owners, m, slots[m], w)
-    a2.start_x()
+    pick_tiles(owners, 0, slots[0], v.w_in_two)
+    a2.sides_in()
+    pick_tiles(owners, 1, slots[1], v.w_out_two)
     b.cores_in()
 
     def layer_two(rows):
@@ -612,11 +635,8 @@
         down(rows, v.cot_two, v.w_out_two, v.hid_two, v.dh)
         back(rows, v.dh, v.w_in_two, v.part_a)
 
-    layer_two(near[0])
-    a2.right_in()
-    layer_two(near[1])
-    a2.left_in()
-    layer_two(near[2])
+    for rows in near[:3]:
+        layer_two(rows)
     a2.far_in()
     layer_two(near[3])
     a2.cores_in()
@@ -626,55 +646,41 @@
     r.start_c()
     r.start_opposite()
     r.start_near()
+    ty = YReduce((v.p_in, v.p_out), 192, tile_bufs, v.ys.at[2], v.yr.at[2])
     outer(v.normed_two, v.dh, as_tiles(v.gt_in))
+    place_tiles(owners, 0, v.gt_in, v.p_in)
+    ty.start(0)
     r.finish_near()
     outer(v.cot_two, v.act_two, as_tiles(v.gt_out))
+    place_tiles(owners, 1, v.gt_out, v.p_out)
+    ty.start(1)
     r.start_z()
-    ty = YReduce((v.p_in, v.p_out), 192, tile_bufs, v.ys.at[2], v.yr.at[2])
-    for m, (g, p) in enumerate(((v.gt_in, v.p_in), (v.gt_out, v.p_out))):
-        place_tiles(owners, m, g, p)
-        ty.start(m)
+    for i in range(4):
+        back(pl.ds(i * 256, 256), v.act_two, v.w_out_two, v.part_b)
+    s = Reduce(v.part_b, bufs[2], v.rs.at[2], v.rr.at[2])
+    s.start_c()
+    s.start_opposite()
+    s.start_near()
     f = v.mid[...].astype(F32)
     v.grad_mid[...] = before_input(f, inv_rms(f), r.total() * gains[1:2, :], cot[...].astype(F32)).astype(BF)
     b2 = Gather(v.grad_mid, v.cot_one, v.gs.at[3], v.gr.at[3])
     b2.start_z()
     r.drain()
-    for i in range(4):
-        back(pl.ds(i * 256, 256), v.act_two, v.w_out_two, v.part_b)
-    s = Reduce(v.part_b, bufs[2], v.rs.at[2], v.rr.at[2])
-    s.start_c()
+    ty.middle(0)
+    s.finish_near()
     b2.start_x()
-    s.start_opposite()
-    s.start_near()
+    ty.middle(1)
+    s.start_z()
+    b2.sides_in()
 
     def layer_one(rows):
         down(rows, v.cot_one, v.w_out_one, v.hid_one, v.dh)
         back(rows, v.dh, v.w_in_one, v.part_a)
 
-    layer_one(near[0])
-    b2.right_in()
-    layer_one(near[1])
-    b2.left_in()
-    layer_one(near[2])
-    for m in range(2):
-        ty.middle(m)
+    for rows in near[:3]:
+        layer_one(rows)
     b2.far_in()
     layer_one(near[3])
-    b2.cores_in()
-    fy = YReduce((v.gf_in, v.gf_out), 128, flat_bufs, v.ys.at[3], v.yr.at[3])
-    outer(v.cot_one, v.act_one, as_flat(v.gf_out))
-    fy.start(1)
-    for rows in far:
-        down(rows, v.cot_one, v.w_out_one, v.hid_one, v.dh)
-    outer(v.normed_one, v.dh, as_flat(v.gf_in))
-    fy.start(0)
-    for rows in far:
-        back(rows, v.dh, v.w_in_one, v.part_a)
-    r = Reduce(v.part_a, bufs[0], v.rs.at[3], v.rr.at[3])
-    r.start_c()
-    s.finish_near()
-    r.start_opposite()
-    r.start_near()
     ty.finish()
     for m in range(2):
         for h in range(2):
@@ -685,10 +691,23 @@
         rcopy(v.tile_sum.at[m, 1 - zh], v.tile_got.at[m], v.ps.at[2 + m], v.pr.at[2 + m], {"zh": 1 - zh})
         for m in range(2)
     ]
+    b2.cores_in()
+    fy = YReduce((v.gf_in, v.gf_out), 128, flat_bufs, v.ys.at[3], v.yr.at[3])
+    outer(v.cot_one, v.act_one, as_flat(v.gf_out))
+    fy.start(1)
+    for rows in far:
+        down(rows, v.cot_one, v.w_out_one, v.hid_one, v.dh)
+    for rows in far:
+        back(rows, v.dh, v.w_in_one, v.part_a)
+    r = Reduce(v.part_a, bufs[0], v.rs.at[3], v.rr.at[3])
+    r.start_c()
+    outer(v.normed_one, v.dh, as_flat(v.gf_in))
+    fy.start(0)
+    r.start_opposite()
+    r.start_near()
     fy.middle(1)
+    r.finish_near()
     fy.middle(0)
-    s.start_z()
-    r.finish_near()
     r.start_z()
     fy.finish()
     for h in range(2):
@@ -723,7 +742,7 @@
     named, reduces, tile_y, flat_y = scratch_of()
     out = (shape(16, 1024), shape(16, 1024), shape(64, 8, 512), shape(2, 192, 1024))
     scratch = list(named.values()) + sum(reduces, []) + tile_y + flat_y
-    return comm_call(step_kernel, "step", 0, out, scratch, [SM] + [VM] * 6, args)
+    return comm_call(step_kernel, "step", 0, out, scratch, [SM] + [VM] * 7, args)
 
 
 def adam_kernel(
@@ -788,11 +807,9 @@
     tile_in, tile_out, tile_moment, tile_second, owners,
 ):
     own = owners[:, 0, :]
-    flat = jnp.stack([flat_in.reshape(4, 32, 2, 512), flat_out.reshape(4, 32, 2, 512)])
-    sbuf = flat.transpose(3, 2, 0, 1, 4).reshape(64, 8, 512)
     tile, tiles = (192, 1024), (2, 192, 1024)
     hidden_out, grad_tokens, rbuf, tile_grad = step(
-        own, tokens, grad_out, gains, sbuf, tile_in.reshape(tile), tile_out.reshape(tile)
+        own, tokens, grad_out, gains, flat_in, flat_out, tile_in.reshape(tile), tile_out.reshape(tile)
     )
     outs = adam(
         own, rbuf, tile_grad, flat_in, flat_out, flat_moment, flat_second,

time: 218 us -> 182 us (0.83)
  Pallas kernels: 211 us -> 180 us
  local copies, waits for them, and re-layouts: 4.87 us -> 1.24 us
    pallas_call x1, Pallas kernels: 204 us -> 172 us  [comm_call(): pl.pallas_call(kernel, name=name, out_shape=out_shape, in_specs=in_specs,...]
    another operation x4 -> x0, local copies, waits for them, and re-layouts: 2.71 us -> none  [shards(): jnp.stack([flat_in.reshape(4, 32, 2, 512), flat_out.reshape(4, 32, 2, 512)])]
where the time goes in v4:
time: 182 us; the launch traced here: 181 us
  Pallas kernels  180 us (99%)
    pallas_call x1, Pallas kernels, comm_call(): pl.pallas_call(kernel, name=name, out_shape=out_shape, in_specs=in_specs,...  172 us
    pallas_call x1, Pallas kernels, adam(): pl.pallas_call(adam_kernel, name='adam', grid=(4,), out_shape=(shape(128,...  7.38 us

profile of v4, /device:TPU:65, one launch (start us, length us, event | category | flops | bytes accessed | tf_op | source)
XLA Modules:
  0.0 181.5 jit_solution(11246274454901719244)
XLA Ops:
  0.6 172.2 %step.1 = (bf16[16,1024]{1,0:T(8,128)(2,1)}, bf16[16,1024]{1,0:T(8,128)(2,1)}, bf16[64,8,512]{2,1,0:T(8,128)(2,1)}, bf16[2,192,1024]{2,1,0:T(8,128)(2,1)}) custom-call(s32[2,16]{1,0:T(2,128)} %bitcast.19, bf16[16,1024]{1,0:T(8,128)(2,1)} %tokens.1, bf16[16,1024]{1,0:T(8,128)(2,1)} %cot.1, f32[2,1024]{1,0:T(2,128)} %gains.1, bf16[128,1024]{1,0:T(8,128)(2,1)} %f_in.3, ...), custom_call_target="tpu_custom_call" | custom-call | flops 40000000000 | bytes 8388608 | tf_op jit(solution)/shard_map/step/pallas_call | solution.py:423
  172.8 0.0 copy-start.1
  172.8 0.0 copy-start
  172.8 7.4 %adam.1 = (bf16[128,1024]{1,0:T(8,128)(2,1)}, bf16[128,1024]{1,0:T(8,128)(2,1)}, f32[2,128,1024]{2,1,0:T(8,128)}, f32[2,128,1024]{2,1,0:T(8,128)}, bf16[192,1024...) custom-call(s32[2,16]{1,0:T(2,128)} %bitcast.20, ...), custom_call_target="tpu_custom_call" | custom-call | flops 4000000000 | bytes 13631488 | tf_op jit(solution)/shard_map/adam/pallas_call | solution.py:790
  180.2 0.0 copy-done.1
  180.2 0.6 copy.26
  180.9 0.0 copy-done
  180.9 0.6 copy.27
Async XLA Ops:
  172.8 7.4 %copy-start.1 = (bf16[16,1024]{1,0:T(8,128)(2,1)S(1)}, bf16[16,1024]{1,0:T(8,128)(2,1)}, u32[]{:S(2)}) copy-start(bf16[16,1024]{1,0:T(8,128)(2,1)} %get-tuple-element.54) | copy-start | bytes 98308
  172.8 8.0 %copy-start = (bf16[16,1024]{1,0:T(8,128)(2,1)S(1)}, bf16[16,1024]{1,0:T(8,128)(2,1)}, u32[]{:S(2)}) copy-start(bf16[16,1024]{1,0:T(8,128)(2,1)} %get-tuple-element.55) | copy-start | bytes 98308

commit v5 on v4

--- a/solution.py
+++ b/solution.py
@@ -125,16 +125,14 @@
         self.own, self.full, self.ss, self.rs = own, full, ss, rs
         z, x, c, _ = place()
         self.right_dev, self.left_dev, self.core_dev = {"x": (x + 1) % 4}, {"x": (x + 3) % 4}, {"c": 1 - c}
-        self.sent, self.right, self.left, self.far, self.cores = [], [], [], [], []
+        self.right, self.left, self.far, self.cores = [], [], [], []
 
     def piece(self, xx, d):
         z, x, c, _ = place()
         return blk(c, xx, 16, (z + 8 - d) % 8 * 16)
 
     def send(self, src, rows, k, dev):
-        cp = rcopy(src, self.full.at[rows], self.ss.at[k], self.rs.at[k], dev)
-        self.sent.append(cp)
-        return cp
+        return rcopy(src, self.full.at[rows], self.ss, self.rs.at[k], dev)
 
     def pass_on(self, rows, k, dev):
         return self.send(self.full.at[rows], rows, k, dev)
@@ -180,8 +178,12 @@
             cp.wait_recv()
 
     def drain(self):
-        for cp in self.sent:
-            cp.wait_send()
+        sent_rows(self.full, self.ss)
+
+
+def sent_rows(ref, sem):
+    rows = ref.at[pl.ds(0, 1008)]
+    pltpu.make_async_copy(rows, rows, sem).wait()
 
 
 def add_rows(dst, dst_at, terms, rows, step=32):
@@ -211,12 +213,9 @@
     def __init__(self, part, bufs, ss, rs):
         self.part, self.ss, self.rs = part, ss, rs
         self.crecv, self.obuf, self.orecv, self.nbuf, self.xrecv, self.zbuf, self.zrecv = bufs
-        self.sent = []
 
     def send(self, src, dst, k, dev):
-        cp = rcopy(src, dst, self.ss.at[k], self.rs.at[k], dev)
-        self.sent.append(cp)
-        return cp
+        return rcopy(src, dst, self.ss, self.rs.at[k], dev)
 
     def start_c(self):
         z, x, c, _ = place()
@@ -296,8 +295,7 @@
         return out
 
     def drain(self):
-        for cp in self.sent:
-            cp.wait_send()
+        sent_rows(self.part, self.ss)
 
 
 class YGather:
@@ -329,10 +327,12 @@
             yy = (y + 1) % 4
             self.far.append(self.copy(self.full[m].at[1, yy], m, 1, yy, 10 + m, self.down))
 
-    def finish(self):
+    def sides(self):
         for m in range(2):
             self.ups[1, m].wait_recv()
             self.downs[0, m].wait_recv()
+
+    def finish(self):
         for cp in self.far:
             cp.wait_recv()
 
@@ -483,17 +483,18 @@
     return store
 
 
-def pick_tiles(owners, m, slots, w):
-    def tile(k, _):
-        want = slot_of(owners, m, k)
-        total = jnp.zeros((64, 512), BF)
-        for q in range(24):
-            r, s = q // 3, q % 3
-            total = total + slots[r // 4, r % 4, s * 64 : (s + 1) * 64, :] * ones_if(want == q)
-        w[k] = total
-        return 0
-
-    lax.fori_loop(0, 16, tile, 0)
+def pick_tiles(owners, slots, weights, yy, first=False):
+    for m in range(2):
+        def tile(k, _, m=m):
+            want = slot_of(owners, m, k)
+            total = jnp.zeros((64, 512), BF) if first else weights[m][k]
+            for h in range(2):
+                for s in range(3):
+                    total = total + slots[m][h, yy, s * 64 : (s + 1) * 64, :] * ones_if(want == (h * 4 + yy) * 3 + s)
+            weights[m][k] = total
+            return 0
+
+        lax.fori_loop(0, 16, tile, 0)
 
 
 def place_tiles(owners, m, g, p):
@@ -521,7 +522,7 @@
         pair=vm((2, 2, 192, 512), BF), rbuf_w=flat, sbuf_w=flat, wide=vm((4, 512, 128), F32), s_in=slots, s_out=slots, gt_in=tiles, gt_out=tiles, p_in=slots, p_out=slots,
         gf_in=wt, gf_out=wt, sbuf_g=flat, tile_sum=vm((2, 2, 192, 512), BF), tile_got=vm((2, 192, 512), BF),
         own_one=own, own_two=own, mid=own, grad_mid=own,
-        gs=DMA((4, n)), gr=DMA((4, n)), rs=DMA((4, k)), rr=DMA((4, k)), ys=DMA((4, 12)), yr=DMA((4, 12)),
+        gs=DMA((4,)), gr=DMA((4, n)), rs=DMA((4,)), rr=DMA((4, k)), ys=DMA((4, 12)), yr=DMA((4, 12)),
         ws=DMA((2,)), wr=DMA((2,)), ps=DMA((4,)), pr=DMA((4,)),
     )
     reduces = [Reduce.scratch() for _ in range(3)]
@@ -590,6 +591,7 @@
     a.sides_in()
     a.far_in()
     a.cores_in()
+    yg.sides()
     yg.finish()
 
     for rows in far:
@@ -616,6 +618,8 @@
     r.start_z()
     yt.forward()
     b.sides_in()
+    twos = (v.w_in_two, v.w_out_two)
+    pick_tiles(owners, slots, twos, y, True)
     v.mid[...] = (tokens[...].astype(F32) + r.total()).astype(BF)
     f = v.mid[...].astype(F32)
     v.own_two[...] = (f * inv_rms(f) * gains[1:2, :]).astype(BF)
@@ -624,10 +628,12 @@
     r.drain()
     b.far_in()
     a2.start_x()
+    yt.sides()
+    pick_tiles(owners, slots, twos, (y + 1) % 4)
+    pick_tiles(owners, slots, twos, (y + 3) % 4)
+    a2.sides_in()
     yt.finish()
-    pick_tiles(owners, 0, slots[0], v.w_in_two)
-    a2.sides_in()
-    pick_tiles(owners, 1, slots[1], v.w_out_two)
+    pick_tiles(owners, slots, twos, (y + 2) % 4)
     b.cores_in()
 
     def layer_two(rows):

time: 182 us -> 180 us (0.989)
  Pallas kernels: 180 us -> 177 us
    pallas_call x1, Pallas kernels: 172 us -> 169 us  [comm_call(): pl.pallas_call(kernel, name=name, out_shape=out_shape, in_specs=in_specs,...]
where the time goes in v5:
time: 180 us; the launch traced here: 179 us
  Pallas kernels  177 us (98%)
    pallas_call x1, Pallas kernels, comm_call(): pl.pallas_call(kernel, name=name, out_shape=out_shape, in_specs=in_specs,...  169 us
    pallas_call x1, Pallas kernels, adam(): pl.pallas_call(adam_kernel, name='adam', grid=(4,), out_shape=(shape(128,...  7.38 us

profile of v5, /device:TPU:65, one launch (start us, length us, event | category | flops | bytes accessed | tf_op | source)
XLA Modules:
  0.0 178.7 jit_solution(7749793876741808870)
XLA Ops:
  0.6 169.4 %step.1 = (bf16[16,1024]{1,0:T(8,128)(2,1)}, bf16[16,1024]{1,0:T(8,128)(2,1)}, bf16[64,8,512]{2,1,0:T(8,128)(2,1)}, bf16[2,192,1024]{2,1,0:T(8,128)(2,1)}) custom-call(s32[2,16]{1,0:T(2,128)} %bitcast.19, bf16[16,1024]{1,0:T(8,128)(2,1)} %tokens.1, bf16[16,1024]{1,0:T(8,128)(2,1)} %cot.1, f32[2,1024]{1,0:T(2,128)} %gains.1, bf16[128,1024]{1,0:T(8,128)(2,1)} %f_in.3, ...), custom_call_target="tpu_custom_call" | custom-call | flops 40000000000 | bytes 8388608 | tf_op jit(solution)/shard_map/step/pallas_call | solution.py:423
  170.1 0.0 copy-start.1
  170.1 0.0 copy-start
  170.1 7.4 %adam.1 = (bf16[128,1024]{1,0:T(8,128)(2,1)}, bf16[128,1024]{1,0:T(8,128)(2,1)}, f32[2,128,1024]{2,1,0:T(8,128)}, f32[2,128,1024]{2,1,0:T(8,128)}, bf16[192,1024...) custom-call(s32[2,16]{1,0:T(2,128)} %bitcast.20, ...), custom_call_target="tpu_custom_call" | custom-call | flops 4000000000 | bytes 13631488 | tf_op jit(solution)/shard_map/adam/pallas_call | solution.py:796
  177.5 0.0 copy-done.1
  177.5 0.6 copy.26
  178.1 0.0 copy-done
  178.1 0.6 copy.27
Async XLA Ops:
  170.1 7.4 %copy-start.1 = (bf16[16,1024]{1,0:T(8,128)(2,1)S(1)}, bf16[16,1024]{1,0:T(8,128)(2,1)}, u32[]{:S(2)}) copy-start(bf16[16,1024]{1,0:T(8,128)(2,1)} %get-tuple-element.54) | copy-start | bytes 98308
  170.1 8.0 %copy-start = (bf16[16,1024]{1,0:T(8,128)(2,1)S(1)}, bf16[16,1024]{1,0:T(8,128)(2,1)}, u32[]{:S(2)}) copy-start(bf16[16,1024]{1,0:T(8,128)(2,1)} %get-tuple-element.55) | copy-start | bytes 98308
